TPU v7x, 32 devices: a whole 2x2x4 slice. The times are simulated.
32 devices in a mesh: section: 2 (over x), batch: 16 (over z, y, core).
Axes of the slice: x: 2, y: 2, z: 4, core: 2. Of those that a mesh axis runs over, the one named last changes fastest.
Arguments:
- hidden_in: bfloat16 [8192, 1024], P('batch', 'section'), may hold values from -6 to 6
- cotangent: bfloat16 [8192, 1024], P('batch', 'section'), may hold values from -6 to 6
- lengths: int32 [32], P('batch'), may hold values from 30 to 256, as said below
- norm_gain: bfloat16 [2, 1024], P('section', 'batch'), may hold values from 0.099609375 to 1.8984375
- norm_offset: bfloat16 [2, 1024], P('section', 'batch'), may hold values from -1.5 to 1.5
- joint_weight: bfloat16 [2, 1024, 3072], P('section', 'batch'), may hold values from -0.1875 to 0.1875
- output_weight: bfloat16 [2, 1024, 1024], P('section', 'batch'), may hold values from -1.5 to 1.5
- expand_weight: bfloat16 [2, 1024, 4096], P('section', 'batch'), may hold values from -0.1875 to 0.1875
- inner_bias: bfloat16 [2, 4096], P('section', 'batch'), may hold values from -1.5 to 1.5
- contract_weight: bfloat16 [2, 4096, 1024], P('section', 'batch'), may hold values from -0.09375 to 0.09375
- outer_bias: bfloat16 [2, 1024], P('section', 'batch'), may hold values from -1.5 to 1.5
Outputs:
- hidden_out: bfloat16 [8192, 1024], P('batch', 'section')
- input_grad: bfloat16 [8192, 1024], P('batch', 'section')
- gain_grad: float32 [2, 1024], P('section')
- offset_grad: float32 [2, 1024], P('section')
- joint_grad: float32 [2, 1024, 3072], P('section')
- output_grad: float32 [2, 1024, 1024], P('section')
- expand_grad: float32 [2, 1024, 4096], P('section')
- inner_grad: float32 [2, 4096], P('section')
- contract_grad: float32 [2, 4096, 1024], P('section')
- outer_grad: float32 [2, 1024], P('section')
Inputs may be any that keep to these rules, and one draw needn't show every extreme that they name: `lengths`: among the 2 proteins of every index of batch, one, which one drawn from the seed, is exactly 256 long.
All inputs are finite; a program needn't handle non-finite values.
Results may differ from a plain program's by a relative error of at most 0.017.
Values may be sent and summed in bfloat16 or wider, within the bound.
A program may use at most 256 MiB of HBM per device.

v0:
```python
from functools import partial

import jax
import jax.numpy as jnp
from jax import lax
from jax.sharding import PartitionSpec as P

HEADS = 16
HEAD_DIM = 64
ROT = 32
SLOT = 256
MICRO = 2


norm_epsilon = 1e-05
rotary_base = 10000.0
masked_score = -1e30


def shifted(value, axis, steps):
    count = lax.axis_size(axis)
    initial, last = (max(0, -steps), min(count, count - steps))
    return lax.ppermute(value, axis, [(source, source + steps) for source in range(initial, last)])


def partner(value, axis, bit):
    mask = 2**bit
    pairs = [(source, source ^ mask) for source in range(lax.axis_size(axis))]
    return lax.ppermute(value, axis, pairs)


def rotary_tables():
    positions = jnp.arange(SLOT).astype(jnp.float32)
    exponent = jnp.arange(ROT // 2).astype(jnp.float32) * (2.0 / ROT)
    angles = positions[:, None] * (rotary_base ** (-exponent))[None, :]
    return (jnp.cos(angles)[:, None, :], jnp.sin(angles)[:, None, :])


def rotate(tensor, cosine, sine):
    turned = tensor[..., :ROT].reshape(tensor.shape[:-1] + (ROT // 2, 2))
    even_part = turned[..., 0]
    odd_part = turned[..., 1]
    paired = jnp.stack(
        [even_part * cosine - odd_part * sine, odd_part * cosine + even_part * sine], axis=-1
    )
    return jnp.concatenate([paired.reshape(tensor.shape[:-1] + (ROT,)), tensor[..., ROT:]], axis=-1)


def gelu_tanh(values):
    return jax.nn.gelu(values, approximate=True)


def allowed_keys(lengths_now):
    positions = jnp.arange(SLOT)
    causal = positions[None, :] <= positions[:, None]
    inside = positions[None, None, :] < lengths_now[:, None, None]
    return (causal[None] & inside)[:, None]


def attention_weights(queries, keys, allowed):
    scores = jnp.einsum(
        "sqhd,skhd->shqk", queries, keys, preferred_element_type=jnp.float32
    ) * HEAD_DIM ** (-0.5)
    scores = jnp.where(allowed, scores, masked_score)
    return jax.nn.softmax(scores, axis=-1)


def layer_forward(stream, weights, tables, allowed):
    gain, offset, joint, output, expand, inner, contract, outer = weights
    cosine, sine = tables
    average = jnp.mean(stream, axis=-1, keepdims=True)
    centered = stream - average
    variance = jnp.mean(centered * centered, axis=-1, keepdims=True)
    inverse = lax.rsqrt(variance + norm_epsilon)
    standard = centered * inverse
    normed = (standard * gain.astype(jnp.float32) + offset.astype(jnp.float32)).astype(jnp.bfloat16)
    projected = jnp.dot(normed, joint, preferred_element_type=jnp.float32)
    heads = projected.reshape(-1, SLOT, 3, HEADS, HEAD_DIM)
    queries = rotate(heads[:, :, 0], cosine, sine).astype(jnp.bfloat16)
    keys = rotate(heads[:, :, 1], cosine, sine).astype(jnp.bfloat16)
    values = heads[:, :, 2].astype(jnp.bfloat16)
    attention = attention_weights(queries, keys, allowed).astype(jnp.bfloat16)
    mixture = jnp.einsum("shqk,skhd->sqhd", attention, values, preferred_element_type=jnp.float32)
    mixture = mixture.reshape(stream.shape).astype(jnp.bfloat16)
    hidden_pre = jnp.dot(normed, expand, preferred_element_type=jnp.float32) + inner.astype(
        jnp.float32
    )
    activated = gelu_tanh(hidden_pre).astype(jnp.bfloat16)
    result = stream + jnp.dot(mixture, output, preferred_element_type=jnp.float32)
    result = (
        result
        + jnp.dot(activated, contract, preferred_element_type=jnp.float32)
        + outer.astype(jnp.float32)
    )
    return (
        result,
        (standard, inverse, normed, queries, keys, values, mixture, hidden_pre, activated),
    )


def layer_backward(upstream, stored, weights, tables, allowed):
    gain, offset, joint, output, expand, inner, contract, outer = weights
    cosine, sine = tables
    standard, inverse, normed, queries, keys, values, mixture, hidden_pre, activated = stored
    upstream_low = upstream.astype(jnp.bfloat16)
    outer_grad = jnp.sum(upstream, axis=0)
    contract_grad = jnp.dot(activated.T, upstream_low, preferred_element_type=jnp.float32)
    output_grad = jnp.dot(mixture.T, upstream_low, preferred_element_type=jnp.float32)
    activated_grad = jnp.dot(upstream_low, contract.T, preferred_element_type=jnp.float32)
    pullback = jax.vjp(gelu_tanh, hidden_pre)[1]
    pre_grad = pullback(activated_grad)[0].astype(jnp.bfloat16)
    inner_grad = jnp.sum(pre_grad.astype(jnp.float32), axis=0)
    expand_grad = jnp.dot(normed.T, pre_grad, preferred_element_type=jnp.float32)
    mixture_grad = jnp.dot(upstream_low, output.T, preferred_element_type=jnp.float32)
    mixture_grad = mixture_grad.astype(jnp.bfloat16).reshape(values.shape)
    attention = attention_weights(queries, keys, allowed)
    value_grad = jnp.einsum(
        "shqk,sqhd->skhd",
        attention.astype(jnp.bfloat16),
        mixture_grad,
        preferred_element_type=jnp.float32,
    )
    weight_grad = jnp.einsum(
        "sqhd,skhd->shqk", mixture_grad, values, preferred_element_type=jnp.float32
    )
    score_grad = attention * (
        weight_grad - jnp.sum(attention * weight_grad, axis=-1, keepdims=True)
    )
    score_grad = score_grad.astype(jnp.bfloat16)
    scaling = HEAD_DIM ** (-0.5)
    query_grad = (
        jnp.einsum("shqk,skhd->sqhd", score_grad, keys, preferred_element_type=jnp.float32)
        * scaling
    )
    key_grad = (
        jnp.einsum("shqk,sqhd->skhd", score_grad, queries, preferred_element_type=jnp.float32)
        * scaling
    )
    query_grad = rotate(query_grad, cosine, -sine)
    key_grad = rotate(key_grad, cosine, -sine)
    joint_part = (
        jnp.stack([query_grad, key_grad, value_grad], axis=2)
        .reshape(upstream.shape[0], -1)
        .astype(jnp.bfloat16)
    )
    joint_grad = jnp.dot(normed.T, joint_part, preferred_element_type=jnp.float32)
    normed_grad = jnp.dot(joint_part, joint.T, preferred_element_type=jnp.float32)
    normed_grad = normed_grad + jnp.dot(pre_grad, expand.T, preferred_element_type=jnp.float32)
    gain_grad = jnp.sum(normed_grad * standard, axis=0)
    offset_grad = jnp.sum(normed_grad, axis=0)
    scaled_grad = normed_grad * gain.astype(jnp.float32)
    centered_grad = scaled_grad - jnp.mean(scaled_grad, axis=-1, keepdims=True)
    centered_grad = centered_grad - standard * jnp.mean(
        scaled_grad * standard, axis=-1, keepdims=True
    )
    stream_grad = upstream + inverse * centered_grad
    return (
        stream_grad,
        (
            gain_grad,
            offset_grad,
            joint_grad,
            output_grad,
            expand_grad,
            inner_grad,
            contract_grad,
            outer_grad,
        ),
    )


def select_section(is_first, early_tree, later_tree):
    return jax.tree.map(partial(jnp.where, is_first), early_tree, later_tree)


def local(
    hidden_in,
    cotangent,
    lengths,
    norm_gain,
    norm_offset,
    joint_weight,
    output_weight,
    expand_weight,
    inner_bias,
    contract_weight,
    outer_bias,
):
    section_index = lax.axis_index("section")
    is_first = section_index == 0
    gathered = (
        lax.all_gather(norm_gain, "batch", axis=1, tiled=True),
        lax.all_gather(norm_offset, "batch", axis=1, tiled=True),
        lax.all_gather(joint_weight, "batch", axis=1, tiled=True),
        lax.all_gather(output_weight, "batch", axis=1, tiled=True),
        lax.all_gather(expand_weight, "batch", axis=1, tiled=True),
        lax.all_gather(inner_bias, "batch", axis=1, tiled=True),
        lax.all_gather(contract_weight, "batch", axis=1, tiled=True),
        lax.all_gather(outer_bias, "batch", axis=1, tiled=True),
    )
    weights = tuple((member[0] for member in gathered))
    whole_in, whole_cotangent = (
        lax.all_gather(hidden_in, "section", axis=1, tiled=True),
        lax.all_gather(cotangent, "section", axis=1, tiled=True),
    )
    tables = rotary_tables()
    block_rows = whole_in.shape[0] // MICRO
    width = whole_in.shape[1]
    positions = jnp.arange(SLOT)
    valid = (positions[None, :] < lengths[:, None]).astype(jnp.float32).reshape(-1, 1)
    block_lengths = lengths.reshape(MICRO, -1)
    incoming = jnp.zeros((block_rows, width), jnp.bfloat16)
    memory = []
    finished = []
    for moment in range(MICRO + 1):
        first_block = min(moment, MICRO - 1)
        second_block = max(moment - 1, 0)
        block_in = jnp.where(
            is_first, whole_in[first_block * block_rows : (first_block + 1) * block_rows], incoming
        )
        lengths_now = jnp.where(is_first, block_lengths[first_block], block_lengths[second_block])
        result, stored = layer_forward(
            block_in.astype(jnp.float32), weights, tables, allowed_keys(lengths_now)
        )
        result_low = result.astype(jnp.bfloat16)
        if moment >= 1:
            finished.append(result_low)
        if moment < MICRO:
            incoming = shifted(result_low, "section", 1)
        memory.append((stored, lengths_now))
    returning = jnp.zeros((block_rows, width), jnp.bfloat16)
    totals = tuple((jnp.zeros(member.shape, jnp.float32) for member in weights))
    upstream_done = []
    for moment in range(MICRO + 1):
        later_block = min(moment, MICRO - 1)
        active = 1.0 if moment < MICRO else 0.0
        row_start = later_block * block_rows
        from_loss = (
            whole_cotangent[row_start : row_start + block_rows].astype(jnp.float32)
            * valid[row_start : row_start + block_rows]
            * active
        )
        upstream = jnp.where(is_first, returning.astype(jnp.float32), from_loss)
        picked = select_section(
            is_first, memory[max(moment - 1, 0)], memory[min(moment + 1, MICRO)]
        )
        saved_part, lengths_now = picked
        allowed = allowed_keys(lengths_now)
        stored = saved_part
        stream_grad, gradients = layer_backward(upstream, stored, weights, tables, allowed)
        grad_low = stream_grad.astype(jnp.bfloat16)
        if moment >= 1:
            upstream_done.append(grad_low)
        if moment < MICRO:
            returning = shifted(grad_low, "section", -1)
        totals = jax.tree.map(jnp.add, totals, gradients)
    lifted = tuple((member[None] for member in totals))
    reduced = (
        lax.psum_scatter(lifted[0], "batch", scatter_dimension=1, tiled=True),
        lax.psum_scatter(lifted[1], "batch", scatter_dimension=1, tiled=True),
        lax.psum_scatter(lifted[2], "batch", scatter_dimension=1, tiled=True),
        lax.psum_scatter(lifted[3], "batch", scatter_dimension=1, tiled=True),
        lax.psum_scatter(lifted[4], "batch", scatter_dimension=1, tiled=True),
        lax.psum_scatter(lifted[5], "batch", scatter_dimension=1, tiled=True),
        lax.psum_scatter(lifted[6], "batch", scatter_dimension=1, tiled=True),
        lax.psum_scatter(lifted[7], "batch", scatter_dimension=1, tiled=True),
    )
    whole_grads = (
        lax.all_gather(reduced[0].astype(jnp.bfloat16), "batch", axis=1, tiled=True).astype(
            jnp.float32
        ),
        lax.all_gather(reduced[1].astype(jnp.bfloat16), "batch", axis=1, tiled=True).astype(
            jnp.float32
        ),
        lax.all_gather(reduced[2].astype(jnp.bfloat16), "batch", axis=1, tiled=True).astype(
            jnp.float32
        ),
        lax.all_gather(reduced[3].astype(jnp.bfloat16), "batch", axis=1, tiled=True).astype(
            jnp.float32
        ),
        lax.all_gather(reduced[4].astype(jnp.bfloat16), "batch", axis=1, tiled=True).astype(
            jnp.float32
        ),
        lax.all_gather(reduced[5].astype(jnp.bfloat16), "batch", axis=1, tiled=True).astype(
            jnp.float32
        ),
        lax.all_gather(reduced[6].astype(jnp.bfloat16), "batch", axis=1, tiled=True).astype(
            jnp.float32
        ),
        lax.all_gather(reduced[7].astype(jnp.bfloat16), "batch", axis=1, tiled=True).astype(
            jnp.float32
        ),
    )
    final_out = jnp.concatenate(finished, axis=0)
    final_grad = jnp.concatenate(upstream_done, axis=0)
    half_width = width // lax.axis_size("section")
    outgoing = jnp.where(is_first, final_grad[:, half_width:], final_out[:, :half_width])
    arrived = partner(outgoing, "section", 0)
    hidden_out = jnp.where(is_first, arrived, final_out[:, half_width:])
    input_grad = jnp.where(is_first, final_grad[:, :half_width], arrived)
    return (
        hidden_out,
        input_grad,
        whole_grads[0],
        whole_grads[1],
        whole_grads[2],
        whole_grads[3],
        whole_grads[4],
        whole_grads[5],
        whole_grads[6],
        whole_grads[7],
    )


def solution(mesh):
    return jax.shard_map(
        local,
        mesh=mesh,
        in_specs=(
            P("batch", "section"),
            P("batch", "section"),
            P("batch"),
            P("section", "batch"),
            P("section", "batch"),
            P("section", "batch", None),
            P("section", "batch", None),
            P("section", "batch", None),
            P("section", "batch"),
            P("section", "batch", None),
            P("section", "batch"),
        ),
        out_specs=(
            P("batch", "section"),
            P("batch", "section"),
            P("section", None),
            P("section", None),
            P("section", None, None),
            P("section", None, None),
            P("section", None, None),
            P("section", None),
            P("section", None, None),
            P("section", None),
        ),
        check_vma=False,
    )
```

profile of v0, /device:TPU:1, one launch (start us, length us, event | category | flops | bytes accessed | tf_op | source)
XLA Modules:
  0.0 1641.6 jit_solution(9974080791331148481)
XLA Ops:
  17.1 23.2 %all_gather.61 = bf16[1,4096]{1,0:T(2,128)(2,1)S(1)} all-gather(bf16[1,256]{1,0:T(2,128)(2,1)} %param.19), channel_id=1, replica_groups=mesh['section'=2,'batch'=16] {'batch'}, dimensions={1}, use_global_device_ids=true | all-gather | bytes 8704 | tf_op jit(solution)/shard_map/all_gather | solution.py:197
  45.4 30.4 %all-reduce.7 = (bf16[1024]{0:T(1024)(128)(2,1)S(1)}, bf16[1024]{0:T(1024)(128)(2,1)S(1)}, bf16[1024]{0:T(1024)(128)(2,1)S(1)}) all-reduce(bf16[1024]{0:T(1024)(128)(2,1)S(1)} %dynamic-update-slice.1, bf16[1024]{0:T(1024)(128)(2,1)S(1)} %dynamic-update-slice, ...), channel_id=1, replica_groups=mesh['section'=2,'batch'=16] {'batch'}, use_global_device_ids=true, to_apply=%add.1 | all-reduce | flops 3072 | bytes 12288
  83.7 14.2 all-gather.15.cloned.1.call-done
  126.3 47.5 %all-gather.19.cloned.1.call-done = bf16[1,1024,4096]{2,1,0:T(8,128)(2,1)} async-done(((bf16[1,64,4096]{2,1,0:T(8,128)(2,1)}), bf16[1,1024,4096]{2,1,0:T(8,128)(2,1)}) %all-gather.19.cloned.1.call-update) | async-done | bytes 8388624 | tf_op jit(solution)/shard_map/all_gather | solution.py:196
  181.7 67.4 %all-gather.21.cloned.1.call-done = bf16[1,4096,1024]{2,1,0:T(8,128)(2,1)} async-done(((bf16[1,256,1024]{2,1,0:T(8,128)(2,1)}), bf16[1,4096,1024]{2,1,0:T(8,128)(2,1)}) %all-gather.21.cloned.1.call-update) | async-done | bytes 8388624 | tf_op jit(solution)/shard_map/all_gather | solution.py:198
  258.0 32.7 %all-gather.17.cloned.1.call-done = bf16[1,1024,1024]{2,1,0:T(8,128)(2,1)} async-done(((bf16[1,64,1024]{2,1,0:T(8,128)(2,1)}), bf16[1,1024,1024]{2,1,0:T(8,128)(2,1)}) %all-gather.17.cloned.1.call-update) | async-done | bytes 2097168 | tf_op jit(solution)/shard_map/all_gather | solution.py:195
  298.0 22.6 %all-gather.11.cloned.1.call-done = bf16[512,1024]{1,0:T(8,128)(2,1)} async-done(((bf16[512,512]{1,0:T(8,128)(2,1)}), bf16[512,1024]{1,0:T(8,128)(2,1)}) %all-gather.11.cloned.1.call-update) | async-done | bytes 1048592 | tf_op jit(solution)/shard_map/all_gather | solution.py:204
  602.8 14.7 add_bitcast_fusion.2
  646.1 20.4 %add_bitcast_fusion.1 = f32[1,1024,4096]{2,1,0:T(8,128)} fusion(f32[1024,4096]{1,0:T(8,128)} %fusion.290, f32[1024,4096]{1,0:T(8,128)} %fusion.292, bf16[256,4096]{1,0:T(8,128)(2,1)} %get-tuple-element.123, pred[]{:T(512)} %eq.3, bf16[256,1024]{1,0:T(8,128)(2,1)S(1)} %get-tuple-element.34, f32[1024]{0:T(1024)S(1)} %add.492, f32[1024]{0:T(1024)S(1)} %mul.1531, ...), kind=kOutput, calls=%fused_computation.7 | convolution fusion | flops 2159280128 | bytes 53489664 | tf_op jit(solution)/shard_map/dot_general | solution.py:113
  666.9 14.2 fusion.117
  689.4 22.4 %add_bitcast_fusion = f32[1,4096,1024]{2,1,0:T(8,128)} fusion(f32[4096,1024]{1,0:T(8,128)} %fusion.117, f32[4096,1024]{1,0:T(8,128)} %fusion.115, bf16[256,1024]{1,0:T(8,128)(2,1)S(1)} %copy-done.20, pred[]{:T(512)} %eq.3, f32[256,4096]{1,0:T(8,128)} %fusion.42, f32[256,4096]{1,0:T(8,128)} %copy-done.27), kind=kOutput, calls=%fused_computation.6 | convolution fusion | flops 2175795200 | bytes 59244544 | tf_op jit(solution)/shard_map/dot_general | solution.py:107
  732.0 25.7 %reduce-scatter.17.cloned.1.call-done = f32[1,64,3072]{2,1,0:T(8,128)} async-done(((f32[1,1024,3072]{2,1,0:T(8,128)}), f32[1,64,3072]{2,1,0:T(8,128)}) %reduce-scatter.17.cloned.1.call-update) | async-done | bytes 786448 | tf_op jit(solution)/shard_map/reduce_scatter | solution.py:261
  759.7 181.9 %reduce-scatter.21.cloned.1.call-done = f32[1,64,4096]{2,1,0:T(8,128)} async-done(((f32[1,1024,4096]{2,1,0:T(8,128)}), f32[1,64,4096]{2,1,0:T(8,128)}) %reduce-scatter.21.cloned.1.call-update) | async-done | bytes 1048592 | tf_op jit(solution)/shard_map/reduce_scatter | solution.py:263
  943.8 180.5 %reduce-scatter.23.cloned.1.call-done = f32[1,256,1024]{2,1,0:T(8,128)} async-done(((f32[1,4096,1024]{2,1,0:T(8,128)}), f32[1,256,1024]{2,1,0:T(8,128)}) %reduce-scatter.23.cloned.1.call-update) | async-done | bytes 1048592 | tf_op jit(solution)/shard_map/reduce_scatter | solution.py:265
  1138.1 43.6 %reduce-scatter.25.cloned.1.call-done = f32[64,1]{1,0:T(8,128)} async-done(((f32[1024,1]{1,0:T(8,128)}), f32[64,1]{1,0:T(8,128)}) %reduce-scatter.25.cloned.1.call-update) | async-done | bytes 272
  1182.5 57.4 %reduce-scatter.27.cloned.1.call-done = f32[64,1]{1,0:T(8,128)} async-done(((f32[1024,1]{1,0:T(8,128)}), f32[64,1]{1,0:T(8,128)}) %reduce-scatter.27.cloned.1.call-update) | async-done | bytes 272
  1240.8 58.0 %reduce-scatter.31.cloned.1.call-done = f32[64,1]{1,0:T(8,128)} async-done(((f32[1024,1]{1,0:T(8,128)}), f32[64,1]{1,0:T(8,128)}) %reduce-scatter.31.cloned.1.call-update) | async-done | bytes 272
  1300.2 31.9 %all-reduce.6 = (bf16[1024]{0:T(1024)(128)(2,1)S(1)}, bf16[1024]{0:T(1024)(128)(2,1)S(1)}, bf16[1024]{0:T(1024)(128)(2,1)S(1)}) all-reduce(bf16[1024]{0:T(1024)(128)(2,1)S(1)} %dynamic-update-slice.3, bf16[1024]{0:T(1024)(128)(2,1)S(1)} %dynamic-update-slice.4, ...), channel_id=1, replica_groups=mesh['section'=2,'batch'=16] {'batch'}, use_global_device_ids=true, to_apply=%add.3 | all-reduce | flops 3072 | bytes 12288
  1333.9 30.1 %reduce-scatter.29.cloned.1.call-done = f32[256,1]{1,0:T(8,128)} async-done(((f32[4096,1]{1,0:T(8,128)}), f32[256,1]{1,0:T(8,128)}) %reduce-scatter.29.cloned.1.call-update) | async-done | bytes 1040
  1364.9 21.6 %all_gather.69 = bf16[1,4096]{1,0:T(2,128)(2,1)S(1)} all-gather(bf16[1,256]{1,0:T(2,128)(2,1)S(1)} %copy.92), channel_id=1, replica_groups=mesh['section'=2,'batch'=16] {'batch'}, dimensions={1}, use_global_device_ids=true | all-gather | bytes 8704 | tf_op jit(solution)/shard_map/all_gather | solution.py:284
  1389.4 19.2 %all-gather.25.cloned.1.call-done = bf16[1,1024,1024]{2,1,0:T(8,128)(2,1)} async-done(((bf16[1,64,1024]{2,1,0:T(8,128)(2,1)}), bf16[1,1024,1024]{2,1,0:T(8,128)(2,1)}) %all-gather.25.cloned.1.call-update) | async-done | bytes 2097168 | tf_op jit(solution)/shard_map/all_gather | solution.py:278
  1412.6 59.0 %all-gather.23.cloned.1.call-done = bf16[1,1024,3072]{2,1,0:T(8,128)(2,1)} async-done(((bf16[1,64,3072]{2,1,0:T(8,128)(2,1)}), bf16[1,1024,3072]{2,1,0:T(8,128)(2,1)}) %all-gather.23.cloned.1.call-update) | async-done | bytes 6291472 | tf_op jit(solution)/shard_map/all_gather | solution.py:275
  1480.8 66.5 %all-gather.27.cloned.1.call-done = bf16[1,1024,4096]{2,1,0:T(8,128)(2,1)} async-done(((bf16[1,64,4096]{2,1,0:T(8,128)(2,1)}), bf16[1,1024,4096]{2,1,0:T(8,128)(2,1)}) %all-gather.27.cloned.1.call-update) | async-done | bytes 8388624 | tf_op jit(solution)/shard_map/all_gather | solution.py:281
  1559.2 63.6 %all-gather.29.cloned.1.call-done = bf16[1,4096,1024]{2,1,0:T(8,128)(2,1)} async-done(((bf16[1,256,1024]{2,1,0:T(8,128)(2,1)}), bf16[1,4096,1024]{2,1,0:T(8,128)(2,1)}) %all-gather.29.cloned.1.call-update) | async-done | bytes 8388624 | tf_op jit(solution)/shard_map/all_gather | solution.py:287
  (505 shorter events, 472.1 us)
Async XLA Ops:
  7.2 74.0 %all-gather.13.cloned.1.call-start = ((), (), s32[]{:S(2)}) async-start(), calls=%async_computation.9 | async-start | bytes 1572864 | tf_op jit(solution)/shard_map/all_gather | solution.py:203
  7.9 90.0 %all-gather.15.cloned.1.call-start = ((), (), s32[]{:S(2)}) async-start(), calls=%async_computation.10 | async-start | bytes 6684672 | tf_op jit(solution)/shard_map/all_gather | solution.py:194
  8.7 165.2 %all-gather.19.cloned.1.call-start = ((), (), s32[]{:S(2)}) async-start(), calls=%async_computation.12 | async-start | bytes 8912896 | tf_op jit(solution)/shard_map/all_gather | solution.py:196
  9.4 239.7 %all-gather.21.cloned.1.call-start = ((), (), s32[]{:S(2)}) async-start(), calls=%async_computation.13 | async-start | bytes 8912896 | tf_op jit(solution)/shard_map/all_gather | solution.py:198
  10.0 280.8 %all-gather.17.cloned.1.call-start = ((), (), s32[]{:S(2)}) async-start(), calls=%async_computation.11 | async-start | bytes 2228224 | tf_op jit(solution)/shard_map/all_gather | solution.py:195
  10.6 310.1 %all-gather.11.cloned.1.call-start = ((), (), s32[]{:S(2)}) async-start(), calls=%async_computation.8 | async-start | bytes 1572864 | tf_op jit(solution)/shard_map/all_gather | solution.py:204
  11.1 719.1 %reduce-scatter.19.cloned.1.call-start = ((), (), s32[]{:S(2)}) async-start(), calls=%async_computation.16 | async-start | bytes 4456448 | tf_op jit(solution)/shard_map/reduce_scatter | solution.py:262
  77.2 304.6 %copy-start.77 = (f32[1024]{0:T(1024)}, f32[1024]{0:T(1024)S(1)}, u32[]{:S(2)}) copy-start(f32[1024]{0:T(1024)S(1)} %add.493) | copy-start | bytes 12292
  294.1 30.0 %collective-permute-start = (bf16[256,1024]{1,0:T(8,128)(2,1)}, bf16[256,1024]{1,0:T(8,128)(2,1)S(1)}, u32[]{:S(2)}, u32[]{:S(2)}) collective-permute-start(bf16[256,1024]{1,0:T(8,128)(2,1)} %fusion.203), channel_id=1, source_target_pairs={{0,16},{1,17},{2,18},{3,19},{4,20},{5,21},{6,22},{7,23},{8,24},{9,... | collective-permute-start | bytes 1572872 | tf_op jit(solution)/shard_map/ppermute | solution.py:23
  382.9 42.9 %collective-permute-start.2 = (bf16[256,1024]{1,0:T(8,128)(2,1)S(1)}, bf16[256,1024]{1,0:T(8,128)(2,1)}, u32[]{:S(2)}, u32[]{:S(2)}) collective-permute-start(bf16[256,1024]{1,0:T(8,128)(2,1)S(1)} %fusion.200), channel_id=1, source_target_pairs={{0,16},{1,17},{2,18},{3,19},{4,20},{5,21},{6,22},{7,23},{8,24},{9,... | collective-permute-start | bytes 1572872 | tf_op jit(solution)/shard_map/ppermute | solution.py:23
  449.2 26.1 %collective-permute-start.1 = (bf16[256,1024]{1,0:T(8,128)(2,1)}, bf16[256,1024]{1,0:T(8,128)(2,1)}, u32[]{:S(2)}, u32[]{:S(2)}) collective-permute-start(bf16[256,1024]{1,0:T(8,128)(2,1)} %get-tuple-element.42), channel_id=1, source_target_pairs={{16,0},{17,1},{18,2},{19,3},{20,4},{21,5},{22,6},{23,7},{24,8},{25... | collective-permute-start | bytes 1572872 | tf_op jit(solution)/shard_map/ppermute | solution.py:23
  527.4 14.8 collective-permute-start.3
  548.2 209.5 %reduce-scatter.17.cloned.1.call-start = ((), (), s32[]{:S(2)}) async-start(), calls=%async_computation.14 | async-start | bytes 13369344 | tf_op jit(solution)/shard_map/reduce_scatter | solution.py:261
  617.6 324.0 %reduce-scatter.21.cloned.1.call-start = ((), (), s32[]{:S(2)}) async-start(), calls=%async_computation.18 | async-start | bytes 17825792 | tf_op jit(solution)/shard_map/reduce_scatter | solution.py:263
  666.5 457.8 %reduce-scatter.23.cloned.1.call-start = ((), (), s32[]{:S(2)}) async-start(), calls=%async_computation.20 | async-start | bytes 17825792 | tf_op jit(solution)/shard_map/reduce_scatter | solution.py:265
  711.8 469.9 %reduce-scatter.25.cloned.1.call-start = ((), (), s32[]{:S(2)}) async-start(), calls=%async_computation.22 | async-start | bytes 557056
  725.8 514.1 %reduce-scatter.27.cloned.1.call-start = ((), (), s32[]{:S(2)}) async-start(), calls=%async_computation.23 | async-start | bytes 557056
  727.0 571.8 %reduce-scatter.31.cloned.1.call-start = ((), (), s32[]{:S(2)}) async-start(), calls=%async_computation.25 | async-start | bytes 557056
  728.1 635.8 %reduce-scatter.29.cloned.1.call-start = ((), (), s32[]{:S(2)}) async-start(), calls=%async_computation.24 | async-start | bytes 2228224
  730.2 678.4 %all-gather.25.cloned.1.call-start = ((), (), s32[]{:S(2)}) async-start(), calls=%async_computation.17 | async-start | bytes 2228224 | tf_op jit(solution)/shard_map/all_gather | solution.py:278
  731.9 739.7 %all-gather.23.cloned.1.call-start = ((), (), s32[]{:S(2)}) async-start(), calls=%async_computation.15 | async-start | bytes 6684672 | tf_op jit(solution)/shard_map/all_gather | solution.py:275
  759.7 787.7 %all-gather.27.cloned.1.call-start = ((), (), s32[]{:S(2)}) async-start(), calls=%async_computation.19 | async-start | bytes 8912896 | tf_op jit(solution)/shard_map/all_gather | solution.py:281
  943.7 679.1 %all-gather.29.cloned.1.call-start = ((), (), s32[]{:S(2)}) async-start(), calls=%async_computation.21 | async-start | bytes 8912896 | tf_op jit(solution)/shard_map/all_gather | solution.py:287
  1137.0 250.1 %collective-permute-start.4 = (bf16[512,512]{1,0:T(8,128)(2,1)S(1)}, bf16[512,512]{1,0:T(8,128)(2,1)S(1)}, u32[]{:S(2)}, u32[]{:S(2)}) collective-permute-start(bf16[512,512]{1,0:T(8,128)(2,1)S(1)} %fusion.247), channel_id=1, source_target_pairs={{0,16},{16,0},{1,17},{17,1},{2,18},{18,2},{3,19},{19,3},{4,20},{20... | collective-permute-start | bytes 1572872 | tf_op jit(solution)/shard_map/ppermute | solution.py:29
  (112 other events, 1803.3 us)
Sparse Core Ops, SparseCore 0:
  9.6 23.3 all-gather.12
  35.3 62.6 all-gather.14
  100.1 73.7 all-gather.18
  175.9 73.1 all-gather.20
  251.1 39.6 all-gather.16
  292.1 28.4 all-gather.10
  548.3 69.6 reduce-scatter.18
  623.1 134.5 reduce-scatter.16
  762.9 178.5 reduce-scatter.20
  946.7 177.5 reduce-scatter.22
  1128.8 52.8 reduce-scatter.24
  1185.1 54.7 reduce-scatter.26
  1243.9 54.8 reduce-scatter.30
  1302.9 60.9 reduce-scatter.28
  1366.2 42.3 all-gather.24
  1411.0 60.6 all-gather.22
  1473.9 73.4 all-gather.26
  1549.6 73.1 all-gather.28
where the time goes:
time: 1650 us; the launch traced here: 1640 us
  waiting for transfers between devices  985 us (60%)
  matrix products  307 us (19%)
  other arithmetic  126 us (8%)
  blocking collectives  107 us (6%)
  local copies, waits for them, and re-layouts  82.1 us (5%)
  between operations  20.9 us (1%)
    unnamed x22, waiting for transfers between devices  193 us
    reduce_scatter x1, waiting for transfers between devices, local(): lax.psum_scatter(lifted[4], 'batch', scatter_dimension=1, tiled=True)  182 us
    reduce_scatter x1, waiting for transfers between devices, local(): lax.psum_scatter(lifted[6], 'batch', scatter_dimension=1, tiled=True)  181 us
    all_gather x1, waiting for transfers between devices, local(): lax.all_gather(contract_weight, 'batch', axis=1, tiled=True)  67.4 us
    all_gather x1, waiting for transfers between devices, local(): lax.all_gather(reduced[4].astype(jnp.bfloat16), 'batch', axis=1, tiled=True)  66.5 us
    all_gather x1, waiting for transfers between devices, local(): lax.all_gather(reduced[6].astype(jnp.bfloat16), 'batch', axis=1, tiled=True)  63.6 us
    unnamed x2, blocking collectives  62.2 us
    all_gather x1, waiting for transfers between devices, local(): lax.all_gather(reduced[2].astype(jnp.bfloat16), 'batch', axis=1, tiled=True)  59 us
  transfers between devices with their start and end apart: 23, of which 17 were waited for; matrix products, arithmetic and copies ran while one was open for 22% of the time, Pallas kernels for 0%

commit v1 on v0

--- a/solution.py
+++ b/solution.py
@@ -3,6 +3,8 @@
 import jax
 import jax.numpy as jnp
 from jax import lax
+from jax.experimental import pallas as pl
+from jax.experimental.pallas import tpu as pltpu
 from jax.sharding import PartitionSpec as P
 
 HEADS = 16
@@ -10,6 +12,417 @@
 ROT = 32
 SLOT = 256
 MICRO = 2
+SMALL_ROWS = 16
+LANES = 128
+MESH = pl.DeviceIdType.MESH
+ANY = pl.BlockSpec(memory_space=pl.ANY)
+
+
+class Place:
+    def __init__(self):
+        index = lax.axis_index("batch")
+        self.levels = lax.axis_size("batch") // 4
+        self.z, self.y, self.c = index // 4, index // 2 % 2, index % 2
+
+    def at(self, z=None, y=None, c=None):
+        z = self.z if z is None else z
+        y = self.y if y is None else y
+        c = self.c if c is None else c
+        return z * 4 + y * 2 + c
+
+
+def remote(source, target, send, receive, index):
+    return pltpu.make_async_remote_copy(
+        source, target, send, receive, device_id={"batch": index}, device_id_type=MESH
+    )
+
+
+def greet(here, with_section):
+    barrier = pltpu.get_barrier_semaphore()
+
+    def signal(**who):
+        pl.semaphore_signal(barrier, inc=1, device_id=who, device_id_type=MESH)
+
+    signal(batch=here.at(y=1 - here.y))
+    signal(batch=here.at(c=1 - here.c))
+    pl.when(here.z > 0)(lambda: signal(batch=here.at(z=here.z - 1)))
+    pl.when(here.z < here.levels - 1)(lambda: signal(batch=here.at(z=here.z + 1)))
+    waits = 2
+    if with_section:
+        signal(section=1 - lax.axis_index("section"))
+        waits = 3
+    below = jnp.minimum(here.z, 1)
+    above = jnp.minimum(here.levels - 1 - here.z, 1)
+    pl.semaphore_wait(barrier, waits + below + above)
+
+
+def spread_semaphores(pieces, levels):
+    dma = pltpu.SemaphoreType.DMA
+    return [
+        dma((pieces,)),
+        dma((pieces, levels, 2)),
+        dma((pieces, levels)),
+        dma((pieces, levels)),
+        dma((pieces, levels)),
+        dma((pieces, levels, 2)),
+        dma((pieces, levels, 2)),
+    ]
+
+
+class Spread:
+    def __init__(self, here, owns, outs, semaphores):
+        self.here, self.owns, self.outs = here, owns, outs
+        (self.keep, self.zs, self.zr, self.ys, self.yr, self.cs, self.cr) = semaphores
+
+    def block(self, p, z, y, c):
+        rows = self.outs[p].shape[0] // (4 * self.here.levels)
+        start = pl.multiple_of((z * 4 + y * 2 + c) * rows, rows)
+        return self.outs[p].at[pl.ds(start, rows), :]
+
+    def along(self, p, z, source, way):
+        here = self.here
+        target = self.block(p, z, here.y, here.c)
+        step = 1 if way == 0 else -1
+        return remote(
+            source, target, self.zs.at[p, z, way], self.zr.at[p, z], here.at(z=here.z + step)
+        )
+
+    def across(self, p, z, source):
+        here = self.here
+        target = self.block(p, z, here.y, here.c)
+        return remote(source, target, self.ys.at[p, z], self.yr.at[p, z], here.at(y=1 - here.y))
+
+    def beside(self, p, z, y, source):
+        here = self.here
+        target = self.block(p, z, y, here.c)
+        return remote(
+            source, target, self.cs.at[p, z, y], self.cr.at[p, z, y], here.at(c=1 - here.c)
+        )
+
+    def begin(self, p):
+        here = self.here
+        own, last = self.owns[p], here.levels - 1
+        pl.when(here.z < last)(lambda: self.along(p, here.z, own, 0).start())
+        pl.when(here.z > 0)(lambda: self.along(p, here.z, own, 1).start())
+        self.across(p, here.z, own).start()
+        self.beside(p, here.z, here.y, own).start()
+        pltpu.make_async_copy(
+            own, self.block(p, here.z, here.y, here.c), self.keep.at[p]
+        ).start()
+
+    def from_z(self, p, z, way):
+        here = self.here
+        block = self.block(p, z, here.y, here.c)
+        self.along(p, z, block, way).wait_recv()
+        more = here.z < here.levels - 1 if way == 0 else here.z > 0
+        pl.when(more)(lambda: self.along(p, z, block, way).start())
+        self.across(p, z, block).start()
+        self.beside(p, z, here.y, block).start()
+
+    def from_y(self, p, z):
+        here = self.here
+        block = self.block(p, z, 1 - here.y, here.c)
+        self.across(p, z, block).wait_recv()
+        self.beside(p, z, 1 - here.y, block).start()
+
+    def middle(self):
+        here, last = self.here, self.here.levels - 1
+        count = len(self.outs)
+
+        def y_events(distance):
+            @pl.when(here.z - distance >= 0)
+            def _():
+                for p in range(count):
+                    self.from_y(p, here.z - distance)
+
+            @pl.when((here.z + distance <= last) & (distance > 0))
+            def _():
+                for p in range(count):
+                    self.from_y(p, here.z + distance)
+
+        def step(distance, carry):
+            @pl.when(here.z - distance >= 0)
+            def _():
+                for p in range(count):
+                    self.from_z(p, here.z - distance, 0)
+
+            @pl.when(here.z + distance <= last)
+            def _():
+                for p in range(count):
+                    self.from_z(p, here.z + distance, 1)
+
+            y_events(distance - 1)
+            return carry
+
+        lax.fori_loop(1, here.levels, step, 0)
+        y_events(here.levels - 1)
+
+    def finish(self):
+        here, last = self.here, self.here.levels - 1
+
+        def level(z, carry):
+            for p in range(len(self.outs)):
+                own = self.block(p, z, here.y, here.c)
+                for y in range(2):
+                    self.beside(p, z, y, own).wait_send()
+                    self.beside(p, z, y, own).wait_recv()
+                self.across(p, z, own).wait_send()
+                pl.when((z <= here.z) & (here.z < last))(
+                    lambda p=p, own=own: self.along(p, z, own, 0).wait_send()
+                )
+                pl.when((z >= here.z) & (here.z > 0))(
+                    lambda p=p, own=own: self.along(p, z, own, 1).wait_send()
+                )
+            return carry
+
+        lax.fori_loop(0, here.levels, level, 0)
+        for p in range(len(self.outs)):
+            block = self.block(p, here.z, here.y, here.c)
+            pltpu.make_async_copy(block, block, self.keep.at[p]).wait()
+
+
+def gather_kernel(pieces, *refs):
+    owns, halves = refs[:pieces], refs[pieces : pieces + 2]
+    outs, wholes = refs[pieces + 2 : 2 * pieces + 2], refs[2 * pieces + 2 : 2 * pieces + 4]
+    half_send, half_receive, half_keep = refs[2 * pieces + 4 : 2 * pieces + 7]
+    here = Place()
+    section = lax.axis_index("section")
+    greet(here, True)
+    spread = Spread(here, owns, outs, refs[2 * pieces + 7 :])
+    for p in range(pieces):
+        spread.begin(p)
+    moves = []
+    for i, (half, whole) in enumerate(zip(halves, wholes)):
+        width = half.shape[1]
+        mine = whole.at[:, pl.ds(pl.multiple_of(section * width, width), width)]
+        send = pltpu.make_async_remote_copy(
+            half,
+            mine,
+            half_send.at[i],
+            half_receive.at[i],
+            device_id={"section": 1 - section},
+            device_id_type=MESH,
+        )
+        keep = pltpu.make_async_copy(half, mine, half_keep.at[i])
+        send.start()
+        keep.start()
+        moves.append((send, keep))
+    spread.middle()
+    spread.finish()
+    for send, keep in moves:
+        send.wait()
+        keep.wait()
+
+
+def gather_all(owns, halves, number):
+    levels = lax.axis_size("batch") // 4
+    pieces = len(owns)
+    shapes = [
+        jax.ShapeDtypeStruct((own.shape[0] * 4 * levels, own.shape[1]), own.dtype) for own in owns
+    ] + [jax.ShapeDtypeStruct((half.shape[0], half.shape[1] * 2), half.dtype) for half in halves]
+    dma = pltpu.SemaphoreType.DMA
+    results = pl.pallas_call(
+        partial(gather_kernel, pieces),
+        out_shape=shapes,
+        in_specs=[ANY] * (pieces + 2),
+        out_specs=[ANY] * (pieces + 2),
+        scratch_shapes=[dma((2,)), dma((2,)), dma((2,))] + spread_semaphores(pieces, levels),
+        compiler_params=pltpu.CompilerParams(collective_id=number, has_side_effects=True),
+        name="gather_weights",
+    )(*owns, *halves)
+    return results[:pieces], results[pieces:]
+
+
+def add_rows(target, other):
+    rows = target.shape[0]
+    step = min(rows, 16)
+
+    def body(i, carry):
+        at = pl.ds(pl.multiple_of(i * step, step), step)
+        total = target[at, :].astype(jnp.float32) + other[at, :].astype(jnp.float32)
+        target[at, :] = total.astype(target.dtype)
+        return carry
+
+    lax.fori_loop(0, rows // step, body, 0)
+
+
+class Reduce:
+    def __init__(self, here, partials, mine, beside, across, along, semaphores):
+        self.here, self.partials = here, partials
+        self.mine, self.sib, self.yb, self.zb = mine, beside, across, along
+        (self.ls, self.cs, self.cr, self.ys, self.yr, self.zs, self.zr) = semaphores
+
+    def block(self, p, z, y, c):
+        rows = self.partials[p].shape[0] // (4 * self.here.levels)
+        start = pl.multiple_of((z * 4 + y * 2 + c) * rows, rows)
+        return self.partials[p].at[pl.ds(start, rows), :]
+
+    def load(self, p, z, y):
+        return pltpu.make_async_copy(
+            self.block(p, z, y, self.here.c), self.mine[p].at[z, y], self.ls.at[p, z, y]
+        )
+
+    def to_core(self, p, z, y):
+        here = self.here
+        return remote(
+            self.block(p, z, y, 1 - here.c),
+            self.sib[p].at[z, y],
+            self.cs.at[p, z, y],
+            self.cr.at[p, z, y],
+            here.at(c=1 - here.c),
+        )
+
+    def to_y(self, p, z):
+        here = self.here
+        return remote(
+            self.mine[p].at[z, 1 - here.y],
+            self.yb[p].at[z],
+            self.ys.at[p, z],
+            self.yr.at[p, z],
+            here.at(y=1 - here.y),
+        )
+
+    def to_z(self, p, z, way):
+        here = self.here
+        return remote(
+            self.mine[p].at[z, here.y],
+            self.zb[p].at[way, z],
+            self.zs.at[p, z],
+            self.zr.at[p, way, z],
+            here.at(z=here.z + (1 if way == 0 else -1)),
+        )
+
+    def begin(self, p, z):
+        for y in range(2):
+            self.to_core(p, z, y).start()
+            self.load(p, z, y).start()
+
+    def cores(self, p, z):
+        here = self.here
+        for y in range(2):
+            self.to_core(p, z, y).wait_recv()
+            self.load(p, z, y).wait()
+            add_rows(self.mine[p].at[z, y], self.sib[p].at[z, y])
+        self.to_y(p, z).start()
+
+    def rows(self, p, z):
+        self.to_y(p, z).wait_recv()
+        add_rows(self.mine[p].at[z, self.here.y], self.yb[p].at[z])
+
+    def arrive(self, p, z, way):
+        self.to_z(p, z, way).wait_recv()
+        add_rows(self.mine[p].at[z, self.here.y], self.zb[p].at[way, z])
+
+    def both(self, distance, action):
+        here, last = self.here, self.here.levels - 1
+
+        @pl.when(here.z + distance <= last)
+        def _():
+            for p in range(len(self.partials)):
+                action(p, here.z + distance, 0)
+
+        @pl.when(here.z - distance >= 0)
+        def _():
+            for p in range(len(self.partials)):
+                action(p, here.z - distance, 1)
+
+    def pass_on(self, p, z, way):
+        here, last = self.here, self.here.levels - 1
+        self.rows(p, z)
+        pl.when(here.z > 0 if way == 0 else here.z < last)(lambda: self.arrive(p, z, way))
+        self.to_z(p, z, way).start()
+
+    def run(self):
+        here, last = self.here, self.here.levels - 1
+        count = len(self.partials)
+
+        def start(i, carry):
+            self.both(last - i, lambda p, z, way: self.begin(p, z))
+            return carry
+
+        lax.fori_loop(0, last, start, 0)
+        for p in range(count):
+            self.begin(p, here.z)
+
+        def step(i, carry):
+            distance = last - i
+            self.both(distance, lambda p, z, way: self.cores(p, z))
+            pl.when(i > 0)(lambda: self.both(distance + 1, self.pass_on))
+            return carry
+
+        lax.fori_loop(0, last, step, 0)
+        for p in range(count):
+            self.cores(p, here.z)
+        self.both(1, self.pass_on)
+
+    def own(self, p):
+        here, last = self.here, self.here.levels - 1
+        self.rows(p, here.z)
+        pl.when(here.z > 0)(lambda: self.arrive(p, here.z, 0))
+        pl.when(here.z < last)(lambda: self.arrive(p, here.z, 1))
+        return self.mine[p].at[here.z, here.y]
+
+    def finish(self):
+        here = self.here
+
+        def level(z, carry):
+            for p in range(len(self.partials)):
+                for y in range(2):
+                    self.to_core(p, z, y).wait_send()
+                self.to_y(p, z).wait_send()
+                pl.when(z > here.z)(lambda p=p: self.to_z(p, z, 0).wait_send())
+                pl.when(z < here.z)(lambda p=p: self.to_z(p, z, 1).wait_send())
+            return carry
+
+        lax.fori_loop(0, here.levels, level, 0)
+
+
+def reduce_kernel(pieces, *refs):
+    partials, outs, rest = refs[:pieces], refs[pieces : 2 * pieces], refs[2 * pieces :]
+    mine, beside, across, along = (rest[i * pieces : (i + 1) * pieces] for i in range(4))
+    rest = rest[4 * pieces :]
+    here = Place()
+    greet(here, False)
+    reduce = Reduce(here, partials, mine, beside, across, along, rest[:7])
+    reduce.run()
+    owns = [mine[p].at[here.z, here.y] for p in range(pieces)]
+    spread = Spread(here, owns, outs, rest[7:])
+    for p in range(pieces):
+        reduce.own(p)
+        spread.begin(p)
+    spread.middle()
+    reduce.finish()
+    spread.finish()
+
+
+def reduce_all(partials, number):
+    levels = lax.axis_size("batch") // 4
+    pieces = len(partials)
+    blocks = [(partial.shape[0] // (4 * levels), partial.shape[1]) for partial in partials]
+    dma = pltpu.SemaphoreType.DMA
+    scratch = []
+    for lead in ((levels, 2), (levels, 2), (levels,), (2, levels)):
+        scratch += [pltpu.VMEM(lead + block, jnp.bfloat16) for block in blocks]
+    scratch += [
+        dma((pieces, levels, 2)),
+        dma((pieces, levels, 2)),
+        dma((pieces, levels, 2)),
+        dma((pieces, levels)),
+        dma((pieces, levels)),
+        dma((pieces, levels)),
+        dma((pieces, 2, levels)),
+    ] + spread_semaphores(pieces, levels)
+    return pl.pallas_call(
+        partial(reduce_kernel, pieces),
+        out_shape=[jax.ShapeDtypeStruct(part.shape, jnp.bfloat16) for part in partials],
+        in_specs=[ANY] * pieces,
+        out_specs=[ANY] * pieces,
+        scratch_shapes=scratch,
+        compiler_params=pltpu.CompilerParams(
+            collective_id=number, has_side_effects=True, vmem_limit_bytes=60 * 2**20
+        ),
+        name="reduce_gradients",
+    )(*partials)
 
 
 norm_epsilon = 1e-05
@@ -27,6 +440,25 @@
     mask = 2**bit
     pairs = [(source, source ^ mask) for source in range(lax.axis_size(axis))]
     return lax.ppermute(value, axis, pairs)
+
+
+def pack_small(members):
+    flat = jnp.concatenate([member.astype(jnp.float32) for member in members], axis=1)
+    flat = jnp.pad(flat, ((0, 0), (0, SMALL_ROWS * LANES - flat.shape[1])))
+    return flat.reshape(-1, LANES).astype(jnp.bfloat16)
+
+
+def unpack_small(packed, widths, devices):
+    flat = packed.reshape(devices, -1)
+    members, start = [], 0
+    for width in widths:
+        members.append(flat[:, start : start + width].reshape(-1))
+        start += width
+    return members
+
+
+def partial_product(left, right):
+    return jnp.dot(left.T, right, preferred_element_type=jnp.float32).astype(jnp.bfloat16)
 
 
 def rotary_tables():
@@ -104,13 +536,10 @@
     standard, inverse, normed, queries, keys, values, mixture, hidden_pre, activated = stored
     upstream_low = upstream.astype(jnp.bfloat16)
     outer_grad = jnp.sum(upstream, axis=0)
-    contract_grad = jnp.dot(activated.T, upstream_low, preferred_element_type=jnp.float32)
-    output_grad = jnp.dot(mixture.T, upstream_low, preferred_element_type=jnp.float32)
     activated_grad = jnp.dot(upstream_low, contract.T, preferred_element_type=jnp.float32)
     pullback = jax.vjp(gelu_tanh, hidden_pre)[1]
     pre_grad = pullback(activated_grad)[0].astype(jnp.bfloat16)
     inner_grad = jnp.sum(pre_grad.astype(jnp.float32), axis=0)
-    expand_grad = jnp.dot(normed.T, pre_grad, preferred_element_type=jnp.float32)
     mixture_grad = jnp.dot(upstream_low, output.T, preferred_element_type=jnp.float32)
     mixture_grad = mixture_grad.astype(jnp.bfloat16).reshape(values.shape)
     attention = attention_weights(queries, keys, allowed)
@@ -143,7 +572,6 @@
         .reshape(upstream.shape[0], -1)
         .astype(jnp.bfloat16)
     )
-    joint_grad = jnp.dot(normed.T, joint_part, preferred_element_type=jnp.float32)
     normed_grad = jnp.dot(joint_part, joint.T, preferred_element_type=jnp.float32)
     normed_grad = normed_grad + jnp.dot(pre_grad, expand.T, preferred_element_type=jnp.float32)
     gain_grad = jnp.sum(normed_grad * standard, axis=0)
@@ -156,16 +584,8 @@
     stream_grad = upstream + inverse * centered_grad
     return (
         stream_grad,
-        (
-            gain_grad,
-            offset_grad,
-            joint_grad,
-            output_grad,
-            expand_grad,
-            inner_grad,
-            contract_grad,
-            outer_grad,
-        ),
+        (gain_grad, offset_grad, outer_grad, inner_grad),
+        (normed, mixture, activated, upstream_low, pre_grad, joint_part),
     )
 
 
@@ -188,21 +608,21 @@
 ):
     section_index = lax.axis_index("section")
     is_first = section_index == 0
-    gathered = (
-        lax.all_gather(norm_gain, "batch", axis=1, tiled=True),
-        lax.all_gather(norm_offset, "batch", axis=1, tiled=True),
-        lax.all_gather(joint_weight, "batch", axis=1, tiled=True),
-        lax.all_gather(output_weight, "batch", axis=1, tiled=True),
-        lax.all_gather(expand_weight, "batch", axis=1, tiled=True),
-        lax.all_gather(inner_bias, "batch", axis=1, tiled=True),
-        lax.all_gather(contract_weight, "batch", axis=1, tiled=True),
-        lax.all_gather(outer_bias, "batch", axis=1, tiled=True),
-    )
-    weights = tuple((member[0] for member in gathered))
-    whole_in, whole_cotangent = (
-        lax.all_gather(hidden_in, "section", axis=1, tiled=True),
-        lax.all_gather(cotangent, "section", axis=1, tiled=True),
-    )
+    small_own = pack_small((norm_gain, norm_offset, outer_bias, inner_bias))
+    (joint_all, output_all, expand_all, contract_all, small_all), (whole_in, whole_cotangent) = (
+        gather_all(
+            [joint_weight[0], output_weight[0], expand_weight[0], contract_weight[0], small_own],
+            [hidden_in, cotangent],
+            1,
+        )
+    )
+    devices = lax.axis_size("batch")
+    gain, offset, outer, inner = unpack_small(
+        small_all,
+        [member.shape[1] for member in (norm_gain, norm_offset, outer_bias, inner_bias)],
+        devices,
+    )
+    weights = (gain, offset, joint_all, output_all, expand_all, inner, contract_all, outer)
     tables = rotary_tables()
     block_rows = whole_in.shape[0] // MICRO
     width = whole_in.shape[1]
@@ -229,7 +649,7 @@
             incoming = shifted(result_low, "section", 1)
         memory.append((stored, lengths_now))
     returning = jnp.zeros((block_rows, width), jnp.bfloat16)
-    totals = tuple((jnp.zeros(member.shape, jnp.float32) for member in weights))
+    sums, factors = [], []
     upstream_done = []
     for moment in range(MICRO + 1):
         later_block = min(moment, MICRO - 1)
@@ -247,50 +667,53 @@
         saved_part, lengths_now = picked
         allowed = allowed_keys(lengths_now)
         stored = saved_part
-        stream_grad, gradients = layer_backward(upstream, stored, weights, tables, allowed)
+        stream_grad, small, pairs = layer_backward(upstream, stored, weights, tables, allowed)
+        sums.append(small)
+        factors.append(pairs)
         grad_low = stream_grad.astype(jnp.bfloat16)
         if moment >= 1:
             upstream_done.append(grad_low)
         if moment < MICRO:
             returning = shifted(grad_low, "section", -1)
-        totals = jax.tree.map(jnp.add, totals, gradients)
-    lifted = tuple((member[None] for member in totals))
-    reduced = (
-        lax.psum_scatter(lifted[0], "batch", scatter_dimension=1, tiled=True),
-        lax.psum_scatter(lifted[1], "batch", scatter_dimension=1, tiled=True),
-        lax.psum_scatter(lifted[2], "batch", scatter_dimension=1, tiled=True),
-        lax.psum_scatter(lifted[3], "batch", scatter_dimension=1, tiled=True),
-        lax.psum_scatter(lifted[4], "batch", scatter_dimension=1, tiled=True),
-        lax.psum_scatter(lifted[5], "batch", scatter_dimension=1, tiled=True),
-        lax.psum_scatter(lifted[6], "batch", scatter_dimension=1, tiled=True),
-        lax.psum_scatter(lifted[7], "batch", scatter_dimension=1, tiled=True),
-    )
-    whole_grads = (
-        lax.all_gather(reduced[0].astype(jnp.bfloat16), "batch", axis=1, tiled=True).astype(
-            jnp.float32
-        ),
-        lax.all_gather(reduced[1].astype(jnp.bfloat16), "batch", axis=1, tiled=True).astype(
-            jnp.float32
-        ),
-        lax.all_gather(reduced[2].astype(jnp.bfloat16), "batch", axis=1, tiled=True).astype(
-            jnp.float32
-        ),
-        lax.all_gather(reduced[3].astype(jnp.bfloat16), "batch", axis=1, tiled=True).astype(
-            jnp.float32
-        ),
-        lax.all_gather(reduced[4].astype(jnp.bfloat16), "batch", axis=1, tiled=True).astype(
-            jnp.float32
-        ),
-        lax.all_gather(reduced[5].astype(jnp.bfloat16), "batch", axis=1, tiled=True).astype(
-            jnp.float32
-        ),
-        lax.all_gather(reduced[6].astype(jnp.bfloat16), "batch", axis=1, tiled=True).astype(
-            jnp.float32
-        ),
-        lax.all_gather(reduced[7].astype(jnp.bfloat16), "batch", axis=1, tiled=True).astype(
-            jnp.float32
-        ),
-    )
+    normed, mixture, activated, upstream, pre_grad, joint_part = [
+        jnp.concatenate(
+            [
+                jnp.where(is_first, factors[block + 1][i], factors[block][i])
+                for block in range(MICRO)
+            ]
+        )
+        for i in range(6)
+    ]
+    small = [
+        sum(jnp.where(is_first, sums[block + 1][i], sums[block][i]) for block in range(MICRO))
+        for i in range(4)
+    ]
+    partials = [
+        partial_product(normed, joint_part),
+        partial_product(mixture, upstream),
+        partial_product(normed, pre_grad),
+        partial_product(activated, upstream),
+        pack_small([member.reshape(devices, -1) for member in small]),
+    ]
+    joint_sum, output_sum, expand_sum, contract_sum, small_sum = [
+        member.astype(jnp.float32) for member in reduce_all(partials, 2)
+    ]
+    gain_sum, offset_sum, outer_sum, inner_sum = unpack_small(
+        small_sum, [member.shape[0] // devices for member in small], devices
+    )
+    whole_grads = [
+        member[None]
+        for member in (
+            gain_sum,
+            offset_sum,
+            joint_sum,
+            output_sum,
+            expand_sum,
+            inner_sum,
+            contract_sum,
+            outer_sum,
+        )
+    ]
     final_out = jnp.concatenate(finished, axis=0)
     final_grad = jnp.concatenate(upstream_done, axis=0)
     half_width = width // lax.axis_size("section")

time: 1650 us -> 870 us (0.53)
  waiting for transfers between devices: 985 us -> 7.88 us
  Pallas kernels: 0 us -> 426 us
  blocking collectives: 107 us -> 0 us
  matrix products: 307 us -> 204 us
    pallas_call x0 -> x2, Pallas kernels: none -> 426 us  [the longest x1 282 us: reduce_all(): pl.pallas_call(partial(reduce_kernel, pieces), out_shape=[jax.ShapeDtypeS...]
    all_gather x10 -> x0, waiting for transfers between devices: 393 us -> none  [the longest x1 67.4 us: local(): lax.all_gather(contract_weight, 'batch', axis=1, tiled=True)]
    reduce_scatter x4 -> x0, waiting for transfers between devices: 388 us -> none  [the longest x1 182 us: local(): lax.psum_scatter(lifted[4], 'batch', scatter_dimension=1, tiled=True)]
    unnamed x22 -> x0, waiting for transfers between devices: 193 us -> none
    dot_general x12 -> x4, matrix products: 123 us -> 23.3 us  [partial_product(): jnp.dot(left.T, right, preferred_element_type=jnp.float32)]
    unnamed x2 -> x0, blocking collectives: 62.2 us -> none
    convert_element_type x16 -> x1, other arithmetic: 51.9 us -> 0.07 us  [layer_forward(): outer.astype(jnp.float32)]
    all_gather x2 -> x0, blocking collectives: 44.8 us -> none  [the longest x1 23.2 us: local(): lax.all_gather(inner_bias, 'batch', axis=1, tiled=True)]
  transfers between devices with their start and end apart: 23 -> 5, of which waited for: 17 -> 1; matrix products, arithmetic and copies ran while one was open for 22% -> 16% of each run, Pallas kernels for 0% -> 33%
where the time goes in v1:
time: 870 us; the launch traced here: 858 us
  Pallas kernels  426 us (49%)
  matrix products  204 us (23%)
  other arithmetic  134 us (15%)
  local copies, waits for them, and re-layouts  69.2 us (8%)
  starting transfers between devices  10.5 us (1%)
    pallas_call x1, Pallas kernels, reduce_all(): pl.pallas_call(partial(reduce_kernel, pieces), out_shape=[jax.ShapeDtypeS...  282 us
    pallas_call x1, Pallas kernels, gather_all(): pl.pallas_call(partial(gather_kernel, pieces), out_shape=shapes, in_specs...  144 us
    broadcast_in_dim x4, other arithmetic, local(): member[None]  36.8 us
    sub x6, matrix products, attention_weights(): return jax.nn.softmax(scores, axis=-1)  28.1 us
    dot_general x3, matrix products, layer_backward(): jnp.dot(upstream_low, contract.T, preferred_element_type=jnp.float32)  24.4 us
    dot_general x4, matrix products, partial_product(): jnp.dot(left.T, right, preferred_element_type=jnp.float32)  23.3 us
    dot_general x3, matrix products, layer_forward(): jnp.dot(normed, expand, preferred_element_type=jnp.float32)  21.1 us
    dot_general x3, matrix products, layer_backward(): jnp.dot(pre_grad, expand.T, preferred_element_type=jnp.float32)  19.2 us
  transfers between devices with their start and end apart: 5, of which 1 were waited for; matrix products, arithmetic and copies ran while one was open for 16% of the time, Pallas kernels for 33%

profile of v1, /device:TPU:1, one launch (start us, length us, event | category | flops | bytes accessed | tf_op | source)
XLA Modules:
  0.0 858.1 jit_solution(4921433956684322899)
XLA Ops:
  2.1 144.0 %gather_weights.1 = (bf16[1024,3072]{1,0:T(8,128)(2,1)}, bf16[1024,1024]{1,0:T(8,128)(2,1)}, bf16[1024,4096]{1,0:T(8,128)(2,1)}, bf16[4096,1024]{1,0:T(8,128)(2,...) custom-call(bf16[64,3072]{1,0:T(8,128)(2,1)} %bitcast.346, ...), custom_call_target="tpu_custom_call" | custom-call | tf_op jit(solution)/shard_map/gather_weights/pallas_call | solution.py:224
  149.8 5.7 fusion.247
  169.0 6.0 convolution_add_fusion.2
  198.4 5.6 fusion.241
  238.5 11.4 %multiply_convert_fusion.2 = bf16[16,256,256]{1,2,0:T(8,128)(2,1)S(1)} fusion(f32[16,256,256]{1,2,0:T(8,128)S(1)} %get-tuple-element.146, f32[16,256]{1,0:T(8,128)S(1)} %get-tuple-element.145, f32[16,256,256]{1,2,0:T(8,128)S(1)} %copy-done.18, f32[16,256]{1,0:T(8,128)S(1)} %copy-done.77), kind=kLoop, calls=%fused_computation.92 | loop fusion | flops 4194304 | bytes 10518528 | tf_op jit(solution)/shard_map/convert_element_type | solution.py:558
  262.0 6.7 convert_reduce_fusion.1
  296.3 5.9 fusion.268
  317.3 5.7 fusion.244
  326.8 12.6 %select_select_fusion.1 = (bf16[256,4096]{1,0:T(8,128)(2,1)}, bf16[256,4096]{1,0:T(8,128)(2,1)}, f32[256,4096]{1,0:T(8,128)}) fusion(pred[]{:T(512)} %eq.3, f32[256,4096]{1,0:T(8,128)S(1)} %copy-done.107, f32[256,4096]{1,0:T(8,128)S(1)} %copy-done.104, f32[4096]{0:T(1024)S(1)} %bitcast.355, bf16[1024,4096]{1,0:T(8,128)(2,1)S(1)} %bitcast.365, ...), kind=kOutput, calls=%fused_computation.110 | convolution fusion | flops 2183659520 | bytes 25716736 | tf_op jit(solution)/shard_map/dot_general | solution.py:517
  366.5 7.4 fusion.249
  402.0 6.1 convert_reduce_fusion.2
  420.0 6.5 fusion.269
  427.8 6.0 multiply_reduce_fusion.5
  443.7 7.9 collective-permute-done.3
  453.9 11.5 %convert_reduce_fusion = (f32[4096]{0:T(1024)S(1)}, bf16[256,4096]{1,0:T(8,128)(2,1)S(1)}) fusion(f32[256,4096]{1,0:T(8,128)} %copy-done.106, f32[256,4096]{1,0:T(8,128)} %get-tuple-element.160, pred[]{:T(512)} %eq.3, bf16[256,1024]{1,0:T(8,128)(2,1)S(1)} %get-tuple-element.56, bf16[4096,1024]{1,0:T(8,128)(2,1)} %get-tuple-element.28), kind=kOutput, calls=%fused_computation.75 | convolution fusion | flops 2171596800 | bytes 19415040 | tf_op jit(solution)/shard_map/dot_general | solution.py:539
  467.0 6.9 fusion.270
  498.5 5.6 multiply_reduce_fusion.3
  514.0 6.9 convolution_convert_fusion.refs_3_
  520.9 5.4 convolution_convert_fusion.2.refs_0_
  526.3 6.8 convolution_convert_fusion.1.refs_2_
  533.1 282.3 %reduce_gradients.1 = (bf16[1024,3072]{1,0:T(8,128)(2,1)}, bf16[1024,1024]{1,0:T(8,128)(2,1)}, bf16[1024,4096]{1,0:T(8,128)(2,1)}, bf16[4096,1024]{1,0:T(8,128)(2,1)}, bf16[256,128]{1,0:T(8,128)(2,1)}) custom-call(bf16[1024,3072]{1,0:T(8,128)(2,1)} %convolution_convert_fusion.2.refs_0_, bf16[1024,1024]{1,0:T(8,128)(2,1)} %convolution_convert_fusion.3.refs_1_, ...), custom_call_target="tpu_custom_call" | custom-call | tf_op jit(solution)/shard_map/reduce_gradients/pallas_call | solution.py:415
  817.0 9.2 %bitcast_convert_fusion.2 = f32[1,1024,3072]{2,1,0:T(8,128)} fusion(bf16[1024,3072]{1,0:T(8,128)(2,1)} %get-tuple-element.30), kind=kLoop, calls=%fused_computation.10 | loop fusion | flops 3145728 | bytes 18874368 | tf_op jit(solution)/shard_map/broadcast_in_dim | solution.py:705
  826.2 11.8 %bitcast_convert_fusion.1 = f32[1,1024,4096]{2,1,0:T(8,128)} fusion(bf16[1024,4096]{1,0:T(8,128)(2,1)} %get-tuple-element.32), kind=kLoop, calls=%fused_computation.7 | loop fusion | flops 4194304 | bytes 25165824 | tf_op jit(solution)/shard_map/broadcast_in_dim | solution.py:705
  838.0 11.7 %bitcast_convert_fusion = f32[1,4096,1024]{2,1,0:T(8,128)} fusion(bf16[4096,1024]{1,0:T(8,128)(2,1)} %get-tuple-element.33), kind=kLoop, calls=%fused_computation.6 | loop fusion | flops 4194304 | bytes 25165824 | tf_op jit(solution)/shard_map/broadcast_in_dim | solution.py:705
  (462 shorter events, 256.1 us)
Async XLA Ops:
  149.6 48.2 %copy-start.78 = (f32[256]{0:T(256)}, f32[256]{0:T(256)S(1)}, u32[]{:S(2)}) copy-start(f32[256]{0:T(256)S(1)} %fusion.149) | copy-start | bytes 3076
  155.8 68.8 %copy-start.20 = (bf16[256,16,32]{0,2,1:T(8,128)(2,1)}, bf16[256,16,32]{0,2,1:T(8,128)(2,1)S(1)}, u32[]{:S(2)}) copy-start(bf16[256,16,32]{0,2,1:T(8,128)(2,1)S(1)} %fusion.190) | copy-start | bytes 786436
  158.7 10.3 %copy-start.81 = (f32[2,2,8,128]{3,1,2,0:T(2,128)}, f32[2,2,8,128]{3,1,2,0:T(2,128)S(1)}, u32[]{:S(2)}) copy-start(f32[2,2,8,128]{3,1,2,0:T(2,128)S(1)} %copy.86) | copy-start | bytes 49156
  161.6 61.1 %copy-start.22 = (bf16[256,16,32]{0,2,1:T(8,128)(2,1)}, bf16[256,16,32]{0,2,1:T(8,128)(2,1)S(1)}, u32[]{:S(2)}) copy-start(bf16[256,16,32]{0,2,1:T(8,128)(2,1)S(1)} %concatenate.159) | copy-start | bytes 786436
  179.7 16.6 %collective-permute-start = (bf16[256,1024]{1,0:T(8,128)(2,1)}, bf16[256,1024]{1,0:T(8,128)(2,1)}, u32[]{:S(2)}, u32[]{:S(2)}) collective-permute-start(bf16[256,1024]{1,0:T(8,128)(2,1)} %fusion.105), channel_id=1, source_target_pairs={{0,16},{1,17},{2,18},{3,19},{4,20},{5,21},{6,22},{7,23},{8,24},{9,... | collective-permute-start | bytes 1572872 | tf_op jit(solution)/shard_map/ppermute | solution.py:436
  235.9 17.6 %slice-start.1 = ((s8[8388608]{0:T(1024)(128)(4,1)}), s8[4194304]{0:T(1024)(128)(4,1)S(1)}, s32[]{:S(2)}) async-start(s8[8388608]{0:T(1024)(128)(4,1)} %bitcast.362), calls=%async_computation.1 | async-start | bytes 8388608
  238.5 11.4 %copy-start.34 = (bf16[256,16,64]{0,2,1:T(8,128)(2,1)S(1)}, bf16[256,16,64]{0,2,1:T(8,128)(2,1)}, u32[]{:S(2)}) copy-start(bf16[256,16,64]{0,2,1:T(8,128)(2,1)} %broadcast_select_fusion.9) | copy-start | bytes 1572868
  238.5 12.2 %copy-start.33 = (bf16[256,16,64]{0,2,1:T(8,128)(2,1)S(1)}, bf16[256,16,64]{0,2,1:T(8,128)(2,1)}, u32[]{:S(2)}) copy-start(bf16[256,16,64]{0,2,1:T(8,128)(2,1)} %broadcast_select_fusion.10) | copy-start | bytes 1572868
  238.5 15.0 %slice-start.2 = ((s8[8388608]{0:T(1024)(128)(4,1)}), s8[4194304]{0:T(1024)(128)(4,1)S(1)}, s32[]{:S(2)}) async-start(s8[8388608]{0:T(1024)(128)(4,1)} %bitcast.362), calls=%async_computation.2 | async-start | bytes 8388608
  272.0 10.8 %copy-start.26 = (bf16[256,16,32]{0,2,1:T(8,128)(2,1)S(1)}, bf16[256,16,32]{0,2,1:T(8,128)(2,1)}, u32[]{:S(2)}) copy-start(bf16[256,16,32]{0,2,1:T(8,128)(2,1)} %fusion.191) | copy-start | bytes 786436
  272.0 10.8 %copy-start.28 = (bf16[256,16,32]{0,2,1:T(8,128)(2,1)S(1)}, bf16[256,16,32]{0,2,1:T(8,128)(2,1)}, u32[]{:S(2)}) copy-start(bf16[256,16,32]{0,2,1:T(8,128)(2,1)} %fusion.192) | copy-start | bytes 786436
  291.8 11.9 %slice-start.13 = ((s8[6291456]{0:T(1024)(128)(4,1)}), s8[4194304]{0:T(1024)(128)(4,1)S(1)}, s32[]{:S(2)}) async-start(s8[6291456]{0:T(1024)(128)(4,1)} %bitcast.374), calls=%async_computation.13 | async-start | bytes 8388608
  292.6 9.6 %copy-start.12 = (bf16[256,1024]{1,0:T(8,128)(2,1)}, bf16[256,1024]{1,0:T(8,128)(2,1)S(1)}, u32[]{:S(2)}) copy-start(bf16[256,1024]{1,0:T(8,128)(2,1)S(1)} %fusion.106) | copy-start | bytes 1572868
  292.6 18.5 %collective-permute-start.2 = (bf16[256,1024]{1,0:T(8,128)(2,1)S(1)}, bf16[256,1024]{1,0:T(8,128)(2,1)}, u32[]{:S(2)}, u32[]{:S(2)}) collective-permute-start(bf16[256,1024]{1,0:T(8,128)(2,1)S(1)} %fusion.106), channel_id=1, source_target_pairs={{0,16},{1,17},{2,18},{3,19},{4,20},{5,21},{6,22},{7,23},{8,24},{9,... | collective-permute-start | bytes 1572872 | tf_op jit(solution)/shard_map/ppermute | solution.py:436
  311.1 15.6 %slice-start.3 = ((s8[8388608]{0:T(1024)(128)(4,1)}), s8[4194304]{0:T(1024)(128)(4,1)S(1)}, s32[]{:S(2)}) async-start(s8[8388608]{0:T(1024)(128)(4,1)} %bitcast.364), calls=%async_computation.3 | async-start | bytes 8388608
  315.5 11.2 %copy-start.92 = (f32[256]{0:T(256)}, f32[256]{0:T(256)S(1)}, u32[]{:S(2)}) copy-start(f32[256]{0:T(256)S(1)} %get-tuple-element.133) | copy-start | bytes 3076
  317.3 9.4 %slice-start.4 = ((s8[8388608]{0:T(1024)(128)(4,1)}), s8[4194304]{0:T(1024)(128)(4,1)S(1)}, s32[]{:S(2)}) async-start(s8[8388608]{0:T(1024)(128)(4,1)} %bitcast.364), calls=%async_computation.4 | async-start | bytes 8388608
  317.3 9.4 %copy-start.107 = (f32[256,4096]{1,0:T(8,128)S(1)}, f32[256,4096]{1,0:T(8,128)}, u32[]{:S(2)}) copy-start(f32[256,4096]{1,0:T(8,128)} %copy-done.106) | copy-start | bytes 12582916
  339.4 42.9 %collective-permute-start.1 = (bf16[256,1024]{1,0:T(8,128)(2,1)}, bf16[256,1024]{1,0:T(8,128)(2,1)}, u32[]{:S(2)}, u32[]{:S(2)}) collective-permute-start(bf16[256,1024]{1,0:T(8,128)(2,1)} %get-tuple-element.78), channel_id=1, source_target_pairs={{16,0},{17,1},{18,2},{19,3},{20,4},{21,5},{22,6},{23,7},{24,8},{25... | collective-permute-start | bytes 1572872 | tf_op jit(solution)/shard_map/ppermute | solution.py:436
  427.8 10.1 %copy-start.38 = (bf16[256,1024]{1,0:T(8,128)(2,1)S(1)}, bf16[256,1024]{1,0:T(8,128)(2,1)}, u32[]{:S(2)}) copy-start(bf16[256,1024]{1,0:T(8,128)(2,1)} %copy.65) | copy-start | bytes 1572868
  427.8 10.1 %copy-start.39 = (bf16[256,1024]{1,0:T(8,128)(2,1)S(1)}, bf16[256,1024]{1,0:T(8,128)(2,1)}, u32[]{:S(2)}) copy-start(bf16[256,1024]{1,0:T(8,128)(2,1)} %copy.68) | copy-start | bytes 1572868
  427.8 10.1 %copy-start.40 = (bf16[256,1024]{1,0:T(8,128)(2,1)S(1)}, bf16[256,1024]{1,0:T(8,128)(2,1)}, u32[]{:S(2)}) copy-start(bf16[256,1024]{1,0:T(8,128)(2,1)} %copy.66) | copy-start | bytes 1572868
  436.4 15.1 %collective-permute-start.3 = (bf16[256,1024]{1,0:T(8,128)(2,1)}, bf16[256,1024]{1,0:T(8,128)(2,1)}, u32[]{:S(2)}, u32[]{:S(2)}) collective-permute-start(bf16[256,1024]{1,0:T(8,128)(2,1)} %add_convert_fusion.1), channel_id=1, source_target_pairs={{16,0},{17,1},{18,2},{19,3},{20,4},{21,5},{22,6},{23,7},{24,8},{25... | collective-permute-start | bytes 1572872 | tf_op jit(solution)/shard_map/ppermute | solution.py:436
  509.5 346.3 %collective-permute-start.4 = (bf16[512,512]{1,0:T(8,128)(2,1)S(1)}, bf16[512,512]{1,0:T(8,128)(2,1)S(1)}, u32[]{:S(2)}, u32[]{:S(2)}) collective-permute-start(bf16[512,512]{1,0:T(8,128)(2,1)S(1)} %fusion.161), channel_id=1, source_target_pairs={{0,16},{16,0},{1,17},{17,1},{2,18},{18,2},{3,19},{19,3},{4,20},{20... | collective-permute-start | bytes 1572872 | tf_op jit(solution)/shard_map/ppermute | solution.py:442
  (108 other events, 451.7 us)

commit v2 on v1

--- a/solution.py
+++ b/solution.py
@@ -2,6 +2,7 @@
 
 import jax
 import jax.numpy as jnp
+import numpy as np
 from jax import lax
 from jax.experimental import pallas as pl
 from jax.experimental.pallas import tpu as pltpu
@@ -14,6 +15,14 @@
 MICRO = 2
 SMALL_ROWS = 16
 LANES = 128
+ROW_STEP = 32
+FF_STEP = 1024
+JOINT_STEP = 512
+GELU_SCALE = (2.0 / np.pi) ** 0.5
+GELU_CUBE = 0.044715
+norm_epsilon = 1e-05
+rotary_base = 10000.0
+masked_score = -1e30
 MESH = pl.DeviceIdType.MESH
 ANY = pl.BlockSpec(memory_space=pl.ANY)
 
@@ -425,21 +434,397 @@
     )(*partials)
 
 
-norm_epsilon = 1e-05
-rotary_base = 10000.0
-masked_score = -1e30
-
-
-def shifted(value, axis, steps):
-    count = lax.axis_size(axis)
-    initial, last = (max(0, -steps), min(count, count - steps))
-    return lax.ppermute(value, axis, [(source, source + steps) for source in range(initial, last)])
-
-
-def partner(value, axis, bit):
-    mask = 2**bit
-    pairs = [(source, source ^ mask) for source in range(lax.axis_size(axis))]
-    return lax.ppermute(value, axis, pairs)
+def rotary_rows():
+    positions = np.arange(SLOT, dtype=np.float64)[:, None]
+    lane = np.arange(2 * HEAD_DIM)[None, :] % HEAD_DIM
+    angles = positions * rotary_base ** (-(lane // 2 * 2.0) / ROT)
+    turned = lane < ROT
+    cosine = np.where(turned, np.cos(angles), 1.0)
+    sine = np.where(turned, np.sin(angles), 0.0)
+    even = np.where(lane % 2 == 0, sine, 0.0)
+    odd = np.where(lane % 2 == 1, sine, 0.0)
+    return np.stack([cosine, even, odd]).astype(np.float32)
+
+
+def turn(pair, tables, back):
+    lanes = pair.shape[1]
+    following = pltpu.roll(pair, lanes - 1, 1)
+    preceding = pltpu.roll(pair, 1, 1)
+    side = following * tables[1] - preceding * tables[2]
+    return pair * tables[0] + (side if back else -side)
+
+
+def product(left, right, left_axis=1, right_axis=0):
+    return lax.dot_general(
+        left, right, (((left_axis,), (right_axis,)), ((), ())), preferred_element_type=jnp.float32
+    )
+
+
+def statistics(rows):
+    average = jnp.mean(rows, axis=-1, keepdims=True)
+    centered = rows - average
+    variance = jnp.mean(centered * centered, axis=-1, keepdims=True)
+    inverse = lax.rsqrt(variance + norm_epsilon)
+    return centered * inverse, inverse
+
+
+def low_lanes(width):
+    return lax.broadcasted_iota(jnp.int32, (1, width), 1) < HEAD_DIM
+
+
+def pair_lanes(index):
+    return pl.ds(pl.multiple_of(index * 2 * HEAD_DIM, 2 * HEAD_DIM), 2 * HEAD_DIM)
+
+
+def rows_at(index, step):
+    return pl.ds(pl.multiple_of(index * step, step), step)
+
+
+def forward_block(m, length, loads, refs):
+    (x, normed, qkv, attention, mixture, active, slope, total, result) = refs["state"]
+    joint, output, expand, contract = refs["weights"]
+    gain, offset, outer, inner = refs["vectors"]
+    tables = refs["tables"]
+    width = x.shape[2]
+
+    def norm(i, carry):
+        at = rows_at(i, ROW_STEP)
+        standard, _ = statistics(x[m, at, :].astype(jnp.float32))
+        normed[m, at, :] = (standard * gain[...] + offset[...]).astype(jnp.bfloat16)
+        return carry
+
+    lax.fori_loop(0, SLOT // ROW_STEP, norm, 0)
+    loads(0)
+    for part in range(3):
+        scale = HEAD_DIM**-0.5 if part == 0 else 1.0
+        total[...] = product(normed[m], joint[:, part * width : (part + 1) * width])
+        if part == 2:
+            qkv[m, :, 2 * width :] = total[...].astype(jnp.bfloat16)
+        else:
+
+            def rotary(i, carry, part=part, scale=scale):
+                pair = turn(total[:, pair_lanes(i)], tables, False)
+                at = pair_lanes(i + part * (width // (2 * HEAD_DIM)))
+                qkv[m, :, at] = pair.astype(jnp.bfloat16) * jnp.bfloat16(scale)
+                return carry
+
+            lax.fori_loop(0, width // (2 * HEAD_DIM), rotary, 0)
+
+    query = lax.broadcasted_iota(jnp.int32, (SLOT, SLOT), 0)
+    key = lax.broadcasted_iota(jnp.int32, (SLOT, SLOT), 1)
+    allowed = (key <= query) & (key < length)
+    pairs = width // (2 * HEAD_DIM)
+    low = low_lanes(2 * HEAD_DIM)
+
+    def heads(i, carry):
+        queries, keys = qkv[m, :, pair_lanes(i)], qkv[m, :, pair_lanes(i + pairs)]
+        values = qkv[m, :, pair_lanes(i + 2 * pairs)]
+        mixed = []
+        for half in range(2):
+            own = jnp.where(low == (half == 0), queries, jnp.zeros_like(queries))
+            scores = jnp.where(allowed, product(own, keys, 1, 1), masked_score)
+            raised = jnp.exp(scores - jnp.max(scores, axis=-1, keepdims=True))
+            share = raised / jnp.sum(raised, axis=-1, keepdims=True)
+            share = share.astype(jnp.bfloat16)
+            attention[m, 2 * i + half] = share
+            mixed.append(product(share, values))
+        mixture[m, :, pair_lanes(i)] = jnp.where(low, mixed[0], mixed[1]).astype(jnp.bfloat16)
+        return carry
+
+    lax.fori_loop(0, pairs, heads, 0)
+    loads(1)
+    total[...] = x[m].astype(jnp.float32) + outer[...] + product(mixture[m], output[...])
+    loads(2)
+    loads(3)
+
+    def hidden(i, carry):
+        at = rows_at(i, FF_STEP)
+        pre = product(normed[m], expand[:, at]) + inner[:, at]
+        square = pre * pre
+        bend = jnp.tanh(GELU_SCALE * (pre + GELU_CUBE * (square * pre)))
+        lifted = 0.5 * (1.0 + bend)
+        slant = (0.5 * GELU_SCALE) * (1.0 + (3.0 * GELU_CUBE) * square)
+        slope[m, :, at] = (lifted + pre * (1.0 - bend * bend) * slant).astype(jnp.bfloat16)
+        activated = (pre * lifted).astype(jnp.bfloat16)
+        active[m, :, at] = activated
+        total[...] += product(activated, contract[at, :])
+        return carry
+
+    lax.fori_loop(0, slope.shape[2] // FF_STEP, hidden, 0)
+    result[m] = total[...].astype(jnp.bfloat16)
+
+
+def backward_block(m, refs):
+    (x, _, qkv, attention, _, _, slope, total, result) = refs["state"]
+    joint, output, expand, contract = refs["weights"]
+    gain, offset, outer, inner = refs["vectors"]
+    upstream, mixture_grad = refs["gradients"]
+    gain_sum, offset_sum, outer_sum, inner_sum = refs["sums"]
+    tables = refs["tables"]
+    width = x.shape[2]
+    outer_sum[...] += jnp.sum(upstream[m].astype(jnp.float32), axis=0, keepdims=True)
+    mixture_grad[...] = product(upstream[m], output[...], 1, 1).astype(jnp.bfloat16)
+    total[...] = jnp.zeros_like(total)
+
+    def hidden(i, carry):
+        at = rows_at(i, FF_STEP)
+        active_grad = product(upstream[m], contract[at, :], 1, 1)
+        pre_grad = (active_grad * slope[m, :, at].astype(jnp.float32)).astype(jnp.bfloat16)
+        slope[m, :, at] = pre_grad
+        inner_sum[:, at] += jnp.sum(pre_grad.astype(jnp.float32), axis=0, keepdims=True)
+        total[...] += product(pre_grad, expand[:, at], 1, 1)
+        return carry
+
+    lax.fori_loop(0, slope.shape[2] // FF_STEP, hidden, 0)
+    pairs = width // (2 * HEAD_DIM)
+    low = low_lanes(2 * HEAD_DIM)
+
+    def heads(i, carry):
+        queries, keys = qkv[m, :, pair_lanes(i)], qkv[m, :, pair_lanes(i + pairs)]
+        values = qkv[m, :, pair_lanes(i + 2 * pairs)]
+        mixed_grad = mixture_grad[:, pair_lanes(i)]
+        query_grads, key_grads, value_grads = [], [], []
+        for half in range(2):
+            share = attention[m, 2 * i + half]
+            own = jnp.where(low == (half == 0), mixed_grad, jnp.zeros_like(mixed_grad))
+            value_grads.append(product(share, mixed_grad, 0, 0))
+            share_grad = product(own, values, 1, 1)
+            weight = share.astype(jnp.float32)
+            weighted = weight * share_grad
+            score_grad = weighted - weight * jnp.sum(weighted, axis=-1, keepdims=True)
+            score_grad = score_grad.astype(jnp.bfloat16)
+            query_grads.append(product(score_grad, keys))
+            key_grads.append(product(score_grad, queries, 0, 0))
+        query_grad = jnp.where(low, query_grads[0], query_grads[1]) * HEAD_DIM**-0.5
+        key_grad = jnp.where(low, key_grads[0], key_grads[1])
+        value_grad = jnp.where(low, value_grads[0], value_grads[1])
+        qkv[m, :, pair_lanes(i)] = turn(query_grad, tables, True).astype(jnp.bfloat16)
+        qkv[m, :, pair_lanes(i + pairs)] = turn(key_grad, tables, True).astype(jnp.bfloat16)
+        qkv[m, :, pair_lanes(i + 2 * pairs)] = value_grad.astype(jnp.bfloat16)
+        return carry
+
+    lax.fori_loop(0, pairs, heads, 0)
+
+    def project(i, carry):
+        at = rows_at(i, JOINT_STEP)
+        total[:, at] += product(qkv[m], joint[at, :], 1, 1)
+        return carry
+
+    lax.fori_loop(0, width // JOINT_STEP, project, 0)
+
+    def norm(i, carry):
+        at = rows_at(i, ROW_STEP)
+        standard, inverse = statistics(x[m, at, :].astype(jnp.float32))
+        normed_grad = total[at, :]
+        gain_sum[...] += jnp.sum(normed_grad * standard, axis=0, keepdims=True)
+        offset_sum[...] += jnp.sum(normed_grad, axis=0, keepdims=True)
+        scaled = normed_grad * gain[...]
+        inner_mean = jnp.mean(scaled, axis=-1, keepdims=True)
+        along = jnp.mean(scaled * standard, axis=-1, keepdims=True)
+        change = inverse * (scaled - inner_mean - standard * along)
+        result[m, at, :] = (upstream[m, at, :].astype(jnp.float32) + change).astype(jnp.bfloat16)
+        return carry
+
+    lax.fori_loop(0, SLOT // ROW_STEP, norm, 0)
+
+
+BLOCK_OUTPUTS = 12
+
+
+def blocks_kernel(*refs):
+    lengths, whole_in, cotangent, tables_in, gain, offset, outer, inner = refs[:8]
+    weight_sources = refs[8:12]
+    outs = refs[12:24]
+    weights = refs[24:28]
+    x, normed, qkv, attention, mixture, active, slope, total, result = refs[28:37]
+    upstream, mixture_grad, tables = refs[37:40]
+    weight_sem, in_sem, hand_send, hand_receive, half_send, half_receive, half_keep, out_sem = refs[
+        40:48
+    ]
+    hidden_out, input_grad = outs[:2]
+    factor_outs, sums = outs[2:8], outs[8:12]
+    section = lax.axis_index("section")
+    partner = {"section": 1 - section}
+    barrier = pltpu.get_barrier_semaphore()
+    pl.semaphore_signal(barrier, inc=1, device_id=partner, device_id_type=MESH)
+    pl.semaphore_wait(barrier, 1)
+    half = hidden_out.shape[1]
+
+    def loading(i):
+        return pltpu.make_async_copy(weight_sources[i], weights[i], weight_sem.at[i])
+
+    def taking(source, target, m):
+        return pltpu.make_async_copy(source.at[rows_at(m, SLOT), :], target.at[m], in_sem.at[m])
+
+    def handing(target, m):
+        return pltpu.make_async_remote_copy(
+            result.at[m],
+            target.at[m],
+            hand_send.at[m],
+            hand_receive.at[m],
+            device_id=partner,
+            device_id_type=MESH,
+        )
+
+    def away(target, start, m):
+        return pltpu.make_async_remote_copy(
+            result.at[m, :, pl.ds(start, half)],
+            target.at[rows_at(m, SLOT), :],
+            half_send.at[m],
+            half_receive.at[m],
+            device_id=partner,
+            device_id_type=MESH,
+        )
+
+    def kept(target, start, m):
+        return pltpu.make_async_copy(
+            result.at[m, :, pl.ds(start, half)], target.at[rows_at(m, SLOT), :], half_keep.at[m]
+        )
+
+    def giving(i, source, m):
+        return pltpu.make_async_copy(
+            source.at[m], factor_outs[i].at[rows_at(m, SLOT), :], out_sem.at[i, m]
+        )
+
+    pltpu.make_async_copy(tables_in, tables, weight_sem.at[4]).start()
+    for m in range(MICRO):
+        pl.when(section == 0)(lambda m=m: taking(whole_in, x, m).start())
+        pl.when(section == 1)(lambda m=m: taking(cotangent, upstream, m).start())
+    for i in range(4):
+        loading(i).start()
+    for total_sum in sums:
+        total_sum[...] = jnp.zeros_like(total_sum)
+    pltpu.make_async_copy(tables_in, tables, weight_sem.at[4]).wait()
+    shared = {
+        "state": (x, normed, qkv, attention, mixture, active, slope, total, result),
+        "weights": weights,
+        "vectors": (gain, offset, outer, inner),
+        "tables": tables,
+        "gradients": (upstream, mixture_grad),
+        "sums": sums,
+    }
+
+    def forward(m, carry):
+        pl.when(section == 0)(lambda: taking(whole_in, x, m).wait())
+        pl.when(section == 1)(lambda: handing(x, m).wait_recv())
+        forward_block(
+            m, lengths[m], lambda i: pl.when(m == 0)(lambda: loading(i).wait()), shared
+        )
+
+        @pl.when(section == 0)
+        def _():
+            handing(x, m).start()
+
+        @pl.when(section == 1)
+        def _():
+            away(hidden_out, 0, m).start()
+            kept(hidden_out, half, m).start()
+
+        for i, source in enumerate((normed, mixture, active)):
+            giving(i, source, m).start()
+        return carry
+
+    lax.fori_loop(0, MICRO, forward, 0)
+
+    def backward(m, carry):
+        @pl.when(section == 0)
+        def _():
+            handing(x, m).wait_send()
+            handing(upstream, m).wait_recv()
+
+        @pl.when(section == 1)
+        def _():
+            away(hidden_out, 0, m).wait_send()
+            kept(hidden_out, half, m).wait()
+            taking(cotangent, upstream, m).wait()
+            row = lax.broadcasted_iota(jnp.int32, (SLOT, 1), 0)
+            inside = (row < lengths[m]).astype(jnp.float32)
+            masked = upstream[m].astype(jnp.float32) * inside
+            upstream[m] = masked.astype(jnp.bfloat16)
+
+        backward_block(m, shared)
+
+        @pl.when(section == 1)
+        def _():
+            handing(upstream, m).start()
+
+        @pl.when(section == 0)
+        def _():
+            away(input_grad, half, m).start()
+            kept(input_grad, 0, m).start()
+
+        for i, source in enumerate((qkv, slope, upstream)):
+            giving(3 + i, source, m).start()
+        return carry
+
+    lax.fori_loop(0, MICRO, backward, 0)
+
+    def last(m, carry):
+        @pl.when(section == 0)
+        def _():
+            away(input_grad, half, m).wait_send()
+            kept(input_grad, 0, m).wait()
+            away(hidden_out, 0, m).wait_recv()
+
+        @pl.when(section == 1)
+        def _():
+            handing(upstream, m).wait_send()
+            away(input_grad, half, m).wait_recv()
+
+        for i, source in enumerate((normed, mixture, active, qkv, slope, upstream)):
+            giving(i, source, m).wait()
+        return carry
+
+    lax.fori_loop(0, MICRO, last, 0)
+
+
+def run_blocks(lengths, whole_in, cotangent, vectors, weights, number):
+    tokens, width = whole_in.shape
+    wide = weights[2].shape[1]
+    half = width // lax.axis_size("section")
+    low, full = jnp.bfloat16, jnp.float32
+    shape = jax.ShapeDtypeStruct
+    vmem = pltpu.VMEM
+    dma = pltpu.SemaphoreType.DMA
+    inside = pl.BlockSpec(memory_space=vmem)
+    outputs = [shape((tokens, half), low)] * 2
+    outputs += [shape((tokens, n), low) for n in (width, width, wide, 3 * width, wide, width)]
+    outputs += [shape((1, n), full) for n in (width, width, width, wide)]
+    scratch = [vmem(weight.shape, low) for weight in weights]
+    scratch += [
+        vmem((MICRO, SLOT, width), low),
+        vmem((MICRO, SLOT, width), low),
+        vmem((MICRO, SLOT, 3 * width), low),
+        vmem((MICRO, HEADS, SLOT, SLOT), low),
+        vmem((MICRO, SLOT, width), low),
+        vmem((MICRO, SLOT, wide), low),
+        vmem((MICRO, SLOT, wide), low),
+        vmem((SLOT, width), full),
+        vmem((MICRO, SLOT, width), low),
+        vmem((MICRO, SLOT, width), low),
+        vmem((SLOT, width), low),
+        vmem((3, SLOT, 2 * HEAD_DIM), full),
+        dma((5,)),
+        dma((MICRO,)),
+        dma((MICRO,)),
+        dma((MICRO,)),
+        dma((MICRO,)),
+        dma((MICRO,)),
+        dma((MICRO,)),
+        dma((6, MICRO)),
+    ]
+    vectors = [vector.astype(full).reshape(1, -1) for vector in vectors]
+    return pl.pallas_call(
+        blocks_kernel,
+        out_shape=outputs,
+        in_specs=[pl.BlockSpec(memory_space=pltpu.SMEM), ANY, ANY, ANY] + [inside] * 4 + [ANY] * 4,
+        out_specs=[ANY] * 8 + [inside] * 4,
+        scratch_shapes=scratch,
+        compiler_params=pltpu.CompilerParams(
+            collective_id=number, has_side_effects=True, vmem_limit_bytes=60 * 2**20
+        ),
+        name="two_blocks",
+    )(lengths, whole_in, cotangent, jnp.asarray(rotary_rows()), *vectors, *weights)
 
 
 def pack_small(members):
@@ -459,138 +844,6 @@
 
 def partial_product(left, right):
     return jnp.dot(left.T, right, preferred_element_type=jnp.float32).astype(jnp.bfloat16)
-
-
-def rotary_tables():
-    positions = jnp.arange(SLOT).astype(jnp.float32)
-    exponent = jnp.arange(ROT // 2).astype(jnp.float32) * (2.0 / ROT)
-    angles = positions[:, None] * (rotary_base ** (-exponent))[None, :]
-    return (jnp.cos(angles)[:, None, :], jnp.sin(angles)[:, None, :])
-
-
-def rotate(tensor, cosine, sine):
-    turned = tensor[..., :ROT].reshape(tensor.shape[:-1] + (ROT // 2, 2))
-    even_part = turned[..., 0]
-    odd_part = turned[..., 1]
-    paired = jnp.stack(
-        [even_part * cosine - odd_part * sine, odd_part * cosine + even_part * sine], axis=-1
-    )
-    return jnp.concatenate([paired.reshape(tensor.shape[:-1] + (ROT,)), tensor[..., ROT:]], axis=-1)
-
-
-def gelu_tanh(values):
-    return jax.nn.gelu(values, approximate=True)
-
-
-def allowed_keys(lengths_now):
-    positions = jnp.arange(SLOT)
-    causal = positions[None, :] <= positions[:, None]
-    inside = positions[None, None, :] < lengths_now[:, None, None]
-    return (causal[None] & inside)[:, None]
-
-
-def attention_weights(queries, keys, allowed):
-    scores = jnp.einsum(
-        "sqhd,skhd->shqk", queries, keys, preferred_element_type=jnp.float32
-    ) * HEAD_DIM ** (-0.5)
-    scores = jnp.where(allowed, scores, masked_score)
-    return jax.nn.softmax(scores, axis=-1)
-
-
-def layer_forward(stream, weights, tables, allowed):
-    gain, offset, joint, output, expand, inner, contract, outer = weights
-    cosine, sine = tables
-    average = jnp.mean(stream, axis=-1, keepdims=True)
-    centered = stream - average
-    variance = jnp.mean(centered * centered, axis=-1, keepdims=True)
-    inverse = lax.rsqrt(variance + norm_epsilon)
-    standard = centered * inverse
-    normed = (standard * gain.astype(jnp.float32) + offset.astype(jnp.float32)).astype(jnp.bfloat16)
-    projected = jnp.dot(normed, joint, preferred_element_type=jnp.float32)
-    heads = projected.reshape(-1, SLOT, 3, HEADS, HEAD_DIM)
-    queries = rotate(heads[:, :, 0], cosine, sine).astype(jnp.bfloat16)
-    keys = rotate(heads[:, :, 1], cosine, sine).astype(jnp.bfloat16)
-    values = heads[:, :, 2].astype(jnp.bfloat16)
-    attention = attention_weights(queries, keys, allowed).astype(jnp.bfloat16)
-    mixture = jnp.einsum("shqk,skhd->sqhd", attention, values, preferred_element_type=jnp.float32)
-    mixture = mixture.reshape(stream.shape).astype(jnp.bfloat16)
-    hidden_pre = jnp.dot(normed, expand, preferred_element_type=jnp.float32) + inner.astype(
-        jnp.float32
-    )
-    activated = gelu_tanh(hidden_pre).astype(jnp.bfloat16)
-    result = stream + jnp.dot(mixture, output, preferred_element_type=jnp.float32)
-    result = (
-        result
-        + jnp.dot(activated, contract, preferred_element_type=jnp.float32)
-        + outer.astype(jnp.float32)
-    )
-    return (
-        result,
-        (standard, inverse, normed, queries, keys, values, mixture, hidden_pre, activated),
-    )
-
-
-def layer_backward(upstream, stored, weights, tables, allowed):
-    gain, offset, joint, output, expand, inner, contract, outer = weights
-    cosine, sine = tables
-    standard, inverse, normed, queries, keys, values, mixture, hidden_pre, activated = stored
-    upstream_low = upstream.astype(jnp.bfloat16)
-    outer_grad = jnp.sum(upstream, axis=0)
-    activated_grad = jnp.dot(upstream_low, contract.T, preferred_element_type=jnp.float32)
-    pullback = jax.vjp(gelu_tanh, hidden_pre)[1]
-    pre_grad = pullback(activated_grad)[0].astype(jnp.bfloat16)
-    inner_grad = jnp.sum(pre_grad.astype(jnp.float32), axis=0)
-    mixture_grad = jnp.dot(upstream_low, output.T, preferred_element_type=jnp.float32)
-    mixture_grad = mixture_grad.astype(jnp.bfloat16).reshape(values.shape)
-    attention = attention_weights(queries, keys, allowed)
-    value_grad = jnp.einsum(
-        "shqk,sqhd->skhd",
-        attention.astype(jnp.bfloat16),
-        mixture_grad,
-        preferred_element_type=jnp.float32,
-    )
-    weight_grad = jnp.einsum(
-        "sqhd,skhd->shqk", mixture_grad, values, preferred_element_type=jnp.float32
-    )
-    score_grad = attention * (
-        weight_grad - jnp.sum(attention * weight_grad, axis=-1, keepdims=True)
-    )
-    score_grad = score_grad.astype(jnp.bfloat16)
-    scaling = HEAD_DIM ** (-0.5)
-    query_grad = (
-        jnp.einsum("shqk,skhd->sqhd", score_grad, keys, preferred_element_type=jnp.float32)
-        * scaling
-    )
-    key_grad = (
-        jnp.einsum("shqk,sqhd->skhd", score_grad, queries, preferred_element_type=jnp.float32)
-        * scaling
-    )
-    query_grad = rotate(query_grad, cosine, -sine)
-    key_grad = rotate(key_grad, cosine, -sine)
-    joint_part = (
-        jnp.stack([query_grad, key_grad, value_grad], axis=2)
-        .reshape(upstream.shape[0], -1)
-        .astype(jnp.bfloat16)
-    )
-    normed_grad = jnp.dot(joint_part, joint.T, preferred_element_type=jnp.float32)
-    normed_grad = normed_grad + jnp.dot(pre_grad, expand.T, preferred_element_type=jnp.float32)
-    gain_grad = jnp.sum(normed_grad * standard, axis=0)
-    offset_grad = jnp.sum(normed_grad, axis=0)
-    scaled_grad = normed_grad * gain.astype(jnp.float32)
-    centered_grad = scaled_grad - jnp.mean(scaled_grad, axis=-1, keepdims=True)
-    centered_grad = centered_grad - standard * jnp.mean(
-        scaled_grad * standard, axis=-1, keepdims=True
-    )
-    stream_grad = upstream + inverse * centered_grad
-    return (
-        stream_grad,
-        (gain_grad, offset_grad, outer_grad, inner_grad),
-        (normed, mixture, activated, upstream_low, pre_grad, joint_part),
-    )
-
-
-def select_section(is_first, early_tree, later_tree):
-    return jax.tree.map(partial(jnp.where, is_first), early_tree, later_tree)
 
 
 def local(
@@ -606,88 +859,24 @@
     contract_weight,
     outer_bias,
 ):
-    section_index = lax.axis_index("section")
-    is_first = section_index == 0
-    small_own = pack_small((norm_gain, norm_offset, outer_bias, inner_bias))
-    (joint_all, output_all, expand_all, contract_all, small_all), (whole_in, whole_cotangent) = (
-        gather_all(
-            [joint_weight[0], output_weight[0], expand_weight[0], contract_weight[0], small_own],
-            [hidden_in, cotangent],
-            1,
-        )
+    devices = lax.axis_size("batch")
+    vectors_own = (norm_gain, norm_offset, outer_bias, inner_bias)
+    (*weights, small_all), (whole_in, whole_cotangent) = gather_all(
+        [
+            joint_weight[0],
+            output_weight[0],
+            expand_weight[0],
+            contract_weight[0],
+            pack_small(vectors_own),
+        ],
+        [hidden_in, cotangent],
+        1,
     )
-    devices = lax.axis_size("batch")
-    gain, offset, outer, inner = unpack_small(
-        small_all,
-        [member.shape[1] for member in (norm_gain, norm_offset, outer_bias, inner_bias)],
-        devices,
-    )
-    weights = (gain, offset, joint_all, output_all, expand_all, inner, contract_all, outer)
-    tables = rotary_tables()
-    block_rows = whole_in.shape[0] // MICRO
-    width = whole_in.shape[1]
-    positions = jnp.arange(SLOT)
-    valid = (positions[None, :] < lengths[:, None]).astype(jnp.float32).reshape(-1, 1)
-    block_lengths = lengths.reshape(MICRO, -1)
-    incoming = jnp.zeros((block_rows, width), jnp.bfloat16)
-    memory = []
-    finished = []
-    for moment in range(MICRO + 1):
-        first_block = min(moment, MICRO - 1)
-        second_block = max(moment - 1, 0)
-        block_in = jnp.where(
-            is_first, whole_in[first_block * block_rows : (first_block + 1) * block_rows], incoming
-        )
-        lengths_now = jnp.where(is_first, block_lengths[first_block], block_lengths[second_block])
-        result, stored = layer_forward(
-            block_in.astype(jnp.float32), weights, tables, allowed_keys(lengths_now)
-        )
-        result_low = result.astype(jnp.bfloat16)
-        if moment >= 1:
-            finished.append(result_low)
-        if moment < MICRO:
-            incoming = shifted(result_low, "section", 1)
-        memory.append((stored, lengths_now))
-    returning = jnp.zeros((block_rows, width), jnp.bfloat16)
-    sums, factors = [], []
-    upstream_done = []
-    for moment in range(MICRO + 1):
-        later_block = min(moment, MICRO - 1)
-        active = 1.0 if moment < MICRO else 0.0
-        row_start = later_block * block_rows
-        from_loss = (
-            whole_cotangent[row_start : row_start + block_rows].astype(jnp.float32)
-            * valid[row_start : row_start + block_rows]
-            * active
-        )
-        upstream = jnp.where(is_first, returning.astype(jnp.float32), from_loss)
-        picked = select_section(
-            is_first, memory[max(moment - 1, 0)], memory[min(moment + 1, MICRO)]
-        )
-        saved_part, lengths_now = picked
-        allowed = allowed_keys(lengths_now)
-        stored = saved_part
-        stream_grad, small, pairs = layer_backward(upstream, stored, weights, tables, allowed)
-        sums.append(small)
-        factors.append(pairs)
-        grad_low = stream_grad.astype(jnp.bfloat16)
-        if moment >= 1:
-            upstream_done.append(grad_low)
-        if moment < MICRO:
-            returning = shifted(grad_low, "section", -1)
-    normed, mixture, activated, upstream, pre_grad, joint_part = [
-        jnp.concatenate(
-            [
-                jnp.where(is_first, factors[block + 1][i], factors[block][i])
-                for block in range(MICRO)
-            ]
-        )
-        for i in range(6)
-    ]
-    small = [
-        sum(jnp.where(is_first, sums[block + 1][i], sums[block][i]) for block in range(MICRO))
-        for i in range(4)
-    ]
+    vectors = unpack_small(small_all, [member.shape[1] for member in vectors_own], devices)
+    results = run_blocks(lengths, whole_in, whole_cotangent, vectors, weights, 2)
+    hidden_out, input_grad = results[:2]
+    normed, mixture, activated, joint_part, pre_grad, upstream = results[2:8]
+    small = results[8:]
     partials = [
         partial_product(normed, joint_part),
         partial_product(mixture, upstream),
@@ -696,42 +885,22 @@
         pack_small([member.reshape(devices, -1) for member in small]),
     ]
     joint_sum, output_sum, expand_sum, contract_sum, small_sum = [
-        member.astype(jnp.float32) for member in reduce_all(partials, 2)
+        member.astype(jnp.float32) for member in reduce_all(partials, 3)
     ]
     gain_sum, offset_sum, outer_sum, inner_sum = unpack_small(
-        small_sum, [member.shape[0] // devices for member in small], devices
+        small_sum, [member.shape[1] // devices for member in small], devices
     )
-    whole_grads = [
-        member[None]
-        for member in (
-            gain_sum,
-            offset_sum,
-            joint_sum,
-            output_sum,
-            expand_sum,
-            inner_sum,
-            contract_sum,
-            outer_sum,
-        )
-    ]
-    final_out = jnp.concatenate(finished, axis=0)
-    final_grad = jnp.concatenate(upstream_done, axis=0)
-    half_width = width // lax.axis_size("section")
-    outgoing = jnp.where(is_first, final_grad[:, half_width:], final_out[:, :half_width])
-    arrived = partner(outgoing, "section", 0)
-    hidden_out = jnp.where(is_first, arrived, final_out[:, half_width:])
-    input_grad = jnp.where(is_first, final_grad[:, :half_width], arrived)
     return (
         hidden_out,
         input_grad,
-        whole_grads[0],
-        whole_grads[1],
-        whole_grads[2],
-        whole_grads[3],
-        whole_grads[4],
-        whole_grads[5],
-        whole_grads[6],
-        whole_grads[7],
+        gain_sum[None],
+        offset_sum[None],
+        joint_sum[None],
+        output_sum[None],
+        expand_sum[None],
+        inner_sum[None],
+        contract_sum[None],
+        outer_sum[None],
     )
 
 

time: 870 us -> 651 us (0.75); the launches traced: 858 us -> 650 us
  matrix products: 204 us -> 25.4 us
  Pallas kernels: 426 us -> 578 us
  other arithmetic: 134 us -> 36.5 us
  local copies, waits for them, and re-layouts: 69.2 us -> 8.86 us
  starting transfers between devices: 10.5 us -> 0 us
    dot_general x39 -> x0, matrix products: 153 us -> none  [the longest x3 24.4 us: layer_backward(): jnp.dot(upstream_low, contract.T, preferred_element_type=jnp.float32)]
    pallas_call x0 -> x1, Pallas kernels: none -> 152 us  [run_blocks(): pl.pallas_call(blocks_kernel, out_shape=outputs, in_specs=[pl.BlockSpec(m...]
    another operation x31 -> x3, other arithmetic: 38.6 us -> 2.18 us
    sub x6 -> x0, matrix products: 28.1 us -> none  [attention_weights(): return jax.nn.softmax(scores, axis=-1)]
    reshape x18 -> x4, local copies, waits for them, and re-layouts: 24 us -> 0.25 us  [local(): member.reshape(devices, -1)]
    select_n x13 -> x0, other arithmetic: 22.9 us -> none  [the longest x6 12.4 us: local(): jnp.where(is_first, factors[block + 1][i], factors[block][i])]
    convert_element_type x7 -> x1, other arithmetic: 15.9 us -> 0.08 us  [run_blocks(): vectors = [vector.astype(full).reshape(1, -1) for vector in vectors]]
    reduce_sum x7 -> x0, other arithmetic: 10.9 us -> none  [the longest x3 5.97 us: layer_forward(): average = jnp.mean(stream, axis=-1, keepdims=True)]
  transfers between devices with their start and end apart: 5 -> 0, of which waited for: 1 -> 0; matrix products, arithmetic and copies ran while one was open for 16% -> 0% of each run, Pallas kernels for 33% -> 0%
where the time goes in v2:
time: 651 us; the launch traced here: 650 us
  Pallas kernels  578 us (89%)
  other arithmetic  36.5 us (6%)
  matrix products  25.4 us (4%)
  local copies, waits for them, and re-layouts  8.86 us (1%)
    pallas_call x1, Pallas kernels, reduce_all(): pl.pallas_call(partial(reduce_kernel, pieces), out_shape=[jax.ShapeDtypeS...  282 us
    pallas_call x1, Pallas kernels, run_blocks(): pl.pallas_call(blocks_kernel, out_shape=outputs, in_specs=[pl.BlockSpec(m...  152 us
    pallas_call x1, Pallas kernels, gather_all(): pl.pallas_call(partial(gather_kernel, pieces), out_shape=shapes, in_specs...  144 us
    dot_general x4, matrix products, partial_product(): jnp.dot(left.T, right, preferred_element_type=jnp.float32)  25.4 us

profile of v2, /device:TPU:1, one launch (start us, length us, event | category | flops | bytes accessed | tf_op | source)
XLA Modules:
  0.0 649.9 jit_solution(10978837836127741663)
XLA Ops:
  0.6 1.4 fusion.7
  2.0 144.0 %gather_weights.1 = (bf16[1024,3072]{1,0:T(8,128)(2,1)}, bf16[1024,1024]{1,0:T(8,128)(2,1)}, bf16[1024,4096]{1,0:T(8,128)(2,1)}, bf16[4096,1024]{1,0:T(8,128)(2,...) custom-call(bf16[64,3072]{1,0:T(8,128)(2,1)} %bitcast.37, ...), custom_call_target="tpu_custom_call" | custom-call | tf_op jit(solution)/shard_map/gather_weights/pallas_call | solution.py:233
  146.0 0.9 reshape.105
  147.0 0.7 reshape.112.refs_4_
  147.6 0.7 reshape.113.refs_5_
  148.3 0.7 reshape.114.refs_6_
  149.7 152.2 %two_blocks.1 = (bf16[512,512]{1,0:T(8,128)(2,1)}, bf16[512,512]{1,0:T(8,128)(2,1)}, bf16[512,1024]{1,0:T(8,128)(2,1)}, bf16[512,1024]{1,0:T(8,128)(2,1)}, bf16[...) custom-call(s32[2]{0:T(128)} %refs_0_.1, ...), custom_call_target="tpu_custom_call" | custom-call | tf_op jit(solution)/shard_map/two_blocks/pallas_call | solution.py:817
  301.9 0.7 convert_reduce_fusion.1
  302.7 0.8 convert_reduce_fusion
  303.5 0.7 convert_reduce_fusion.3
  305.0 10.6 %convolution_convert_fusion.refs_3_ = bf16[4096,1024]{1,0:T(8,128)(2,1)} fusion(bf16[512,4096]{1,0:T(8,128)(2,1)} %get-tuple-element.48, bf16[512,1024]{1,0:T(8,128)(2,1)} %get-tuple-element.46), kind=kOutput, calls=%fused_computation.2 | convolution fusion | flops 4299161600 | bytes 13631488 | tf_op jit(solution)/shard_map/dot_general | solution.py:846
  315.7 6.8 %convolution_convert_fusion.1.refs_2_ = bf16[1024,4096]{1,0:T(8,128)(2,1)} fusion(bf16[512,1024]{1,0:T(8,128)(2,1)S(1)} %copy-done.6, bf16[512,4096]{1,0:T(8,128)(2,1)S(1)} %copy-done.4), kind=kOutput, calls=%fused_computation.3 | convolution fusion | flops 4299161600 | bytes 13631488 | tf_op jit(solution)/shard_map/dot_general | solution.py:846
  322.5 2.6 convolution_convert_fusion.3.refs_1_
  325.1 5.4 convolution_convert_fusion.2.refs_0_
  330.5 282.3 %reduce_gradients.1 = (bf16[1024,3072]{1,0:T(8,128)(2,1)}, bf16[1024,1024]{1,0:T(8,128)(2,1)}, bf16[1024,4096]{1,0:T(8,128)(2,1)}, bf16[4096,1024]{1,0:T(8,128)(2,1)}, bf16[256,128]{1,0:T(8,128)(2,1)}) custom-call(bf16[1024,3072]{1,0:T(8,128)(2,1)} %convolution_convert_fusion.2.refs_0_, bf16[1024,1024]{1,0:T(8,128)(2,1)} %convolution_convert_fusion.3.refs_1_, ...), custom_call_target="tpu_custom_call" | custom-call | tf_op jit(solution)/shard_map/reduce_gradients/pallas_call | solution.py:424
  612.8 11.8 %bitcast_convert_fusion = f32[1,4096,1024]{2,1,0:T(8,128)} fusion(bf16[4096,1024]{1,0:T(8,128)(2,1)} %get-tuple-element.57), kind=kLoop, calls=%fused_computation | loop fusion | flops 4194304 | bytes 25165824 | tf_op jit(solution)/shard_map/broadcast_in_dim | solution.py:902
  624.6 12.0 %bitcast_convert_fusion.1 = f32[1,1024,4096]{2,1,0:T(8,128)} fusion(bf16[1024,4096]{1,0:T(8,128)(2,1)} %get-tuple-element.56), kind=kLoop, calls=%fused_computation.1 | loop fusion | flops 4194304 | bytes 25165824 | tf_op jit(solution)/shard_map/broadcast_in_dim | solution.py:900
  636.6 6.4 bitcast_convert_fusion.2
  643.1 2.5 bitcast_convert_fusion.3
  646.3 0.7 broadcast_in_dim_reshape.12
  647.0 0.7 broadcast_in_dim_reshape.13
  647.7 0.7 broadcast_in_dim_reshape.15
  648.4 0.8 copy.26
  649.2 0.8 copy.27
  (36 shorter events, 2.6 us)
Async XLA Ops:
  305.0 10.6 %copy-start.4 = (bf16[512,4096]{1,0:T(8,128)(2,1)S(1)}, bf16[512,4096]{1,0:T(8,128)(2,1)}, u32[]{:S(2)}) copy-start(bf16[512,4096]{1,0:T(8,128)(2,1)} %get-tuple-element.47) | copy-start | bytes 12582916
  305.0 10.6 %copy-start.6 = (bf16[512,1024]{1,0:T(8,128)(2,1)S(1)}, bf16[512,1024]{1,0:T(8,128)(2,1)}, u32[]{:S(2)}) copy-start(bf16[512,1024]{1,0:T(8,128)(2,1)} %get-tuple-element.43) | copy-start | bytes 3145732
  315.7 6.8 %copy-start.7 = (bf16[512,1024]{1,0:T(8,128)(2,1)S(1)}, bf16[512,1024]{1,0:T(8,128)(2,1)}, u32[]{:S(2)}) copy-start(bf16[512,1024]{1,0:T(8,128)(2,1)} %get-tuple-element.45) | copy-start | bytes 3145732
  315.7 6.8 %copy-start.8 = (bf16[512,1024]{1,0:T(8,128)(2,1)S(1)}, bf16[512,1024]{1,0:T(8,128)(2,1)}, u32[]{:S(2)}) copy-start(bf16[512,1024]{1,0:T(8,128)(2,1)} %get-tuple-element.46) | copy-start | bytes 3145732
  322.5 2.6 copy-start.5
  612.8 23.8 %slice-start = ((s8[6291456]{0:T(1024)(128)(4,1)}), s8[4194304]{0:T(1024)(128)(4,1)S(1)}, s32[]{:S(2)}) async-start(s8[6291456]{0:T(1024)(128)(4,1)} %bitcast.33), calls=%async_computation | async-start | bytes 8388608
  624.6 12.0 %slice-start.1 = ((s8[6291456]{0:T(1024)(128)(4,1)}), s8[2097152]{0:T(1024)(128)(4,1)S(1)}, s32[]{:S(2)}) async-start(s8[6291456]{0:T(1024)(128)(4,1)} %bitcast.33), calls=%async_computation.1 | async-start | bytes 4194304
  636.6 6.4 copy-start
  643.0 2.5 copy-start.3
  643.0 5.3 copy-start.2
  643.0 6.1 copy-start.1

commit v3 on v2

--- a/solution.py
+++ b/solution.py
@@ -15,9 +15,9 @@
 MICRO = 2
 SMALL_ROWS = 16
 LANES = 128
-ROW_STEP = 32
-FF_STEP = 1024
-JOINT_STEP = 512
+ROW_STEP = 256
+FF_STEP = 4096
+JOINT_STEP = 1024
 GELU_SCALE = (2.0 / np.pi) ** 0.5
 GELU_CUBE = 0.044715
 norm_epsilon = 1e-05
@@ -524,14 +524,14 @@
             own = jnp.where(low == (half == 0), queries, jnp.zeros_like(queries))
             scores = jnp.where(allowed, product(own, keys, 1, 1), masked_score)
             raised = jnp.exp(scores - jnp.max(scores, axis=-1, keepdims=True))
-            share = raised / jnp.sum(raised, axis=-1, keepdims=True)
+            share = raised * (1.0 / jnp.sum(raised, axis=-1, keepdims=True))
             share = share.astype(jnp.bfloat16)
             attention[m, 2 * i + half] = share
             mixed.append(product(share, values))
         mixture[m, :, pair_lanes(i)] = jnp.where(low, mixed[0], mixed[1]).astype(jnp.bfloat16)
         return carry
 
-    lax.fori_loop(0, pairs, heads, 0)
+    lax.fori_loop(0, pairs, heads, 0, unroll=8)
     loads(1)
     total[...] = x[m].astype(jnp.float32) + outer[...] + product(mixture[m], output[...])
     loads(2)
@@ -603,7 +603,7 @@
         qkv[m, :, pair_lanes(i + 2 * pairs)] = value_grad.astype(jnp.bfloat16)
         return carry
 
-    lax.fori_loop(0, pairs, heads, 0)
+    lax.fori_loop(0, pairs, heads, 0, unroll=2)
 
     def project(i, carry):
         at = rows_at(i, JOINT_STEP)

time: 651 us -> 630 us (0.968); the launches traced: 650 us -> 620 us
  Pallas kernels: 578 us -> 549 us
    pallas_call x1, Pallas kernels: 152 us -> 122 us  [run_blocks(): pl.pallas_call(blocks_kernel, out_shape=outputs, in_specs=[pl.BlockSpec(m...]
where the time goes in v3:
time: 630 us; the launch traced here: 620 us
  Pallas kernels  549 us (87%)
  other arithmetic  36.5 us (6%)
  matrix products  25.4 us (4%)
  local copies, waits for them, and re-layouts  8.86 us (1%)
    pallas_call x1, Pallas kernels, reduce_all(): pl.pallas_call(partial(reduce_kernel, pieces), out_shape=[jax.ShapeDtypeS...  282 us
    pallas_call x1, Pallas kernels, gather_all(): pl.pallas_call(partial(gather_kernel, pieces), out_shape=shapes, in_specs...  144 us
    pallas_call x1, Pallas kernels, run_blocks(): pl.pallas_call(blocks_kernel, out_shape=outputs, in_specs=[pl.BlockSpec(m...  122 us
    dot_general x4, matrix products, partial_product(): jnp.dot(left.T, right, preferred_element_type=jnp.float32)  25.4 us

profile of v3, /device:TPU:1, one launch (start us, length us, event | category | flops | bytes accessed | tf_op | source)
XLA Modules:
  0.0 620.5 jit_solution(13004587004959681873)
XLA Ops:
  0.6 1.4 fusion.7
  2.0 144.0 %gather_weights.1 = (bf16[1024,3072]{1,0:T(8,128)(2,1)}, bf16[1024,1024]{1,0:T(8,128)(2,1)}, bf16[1024,4096]{1,0:T(8,128)(2,1)}, bf16[4096,1024]{1,0:T(8,128)(2,...) custom-call(bf16[64,3072]{1,0:T(8,128)(2,1)} %bitcast.37, ...), custom_call_target="tpu_custom_call" | custom-call | tf_op jit(solution)/shard_map/gather_weights/pallas_call | solution.py:233
  146.0 0.9 reshape.105
  147.0 0.7 reshape.112.refs_4_
  147.6 0.7 reshape.113.refs_5_
  148.3 0.7 reshape.114.refs_6_
  149.7 122.4 %two_blocks.1 = (bf16[512,512]{1,0:T(8,128)(2,1)}, bf16[512,512]{1,0:T(8,128)(2,1)}, bf16[512,1024]{1,0:T(8,128)(2,1)}, bf16[512,1024]{1,0:T(8,128)(2,1)}, bf16[...) custom-call(s32[2]{0:T(128)} %refs_0_.1, ...), custom_call_target="tpu_custom_call" | custom-call | tf_op jit(solution)/shard_map/two_blocks/pallas_call | solution.py:817
  272.0 0.7 convert_reduce_fusion.1
  272.9 0.8 convert_reduce_fusion
  273.7 0.7 convert_reduce_fusion.3
  275.2 10.6 %convolution_convert_fusion.refs_3_ = bf16[4096,1024]{1,0:T(8,128)(2,1)} fusion(bf16[512,4096]{1,0:T(8,128)(2,1)} %get-tuple-element.48, bf16[512,1024]{1,0:T(8,128)(2,1)} %get-tuple-element.46), kind=kOutput, calls=%fused_computation.2 | convolution fusion | flops 4299161600 | bytes 13631488 | tf_op jit(solution)/shard_map/dot_general | solution.py:846
  285.8 6.8 %convolution_convert_fusion.1.refs_2_ = bf16[1024,4096]{1,0:T(8,128)(2,1)} fusion(bf16[512,1024]{1,0:T(8,128)(2,1)S(1)} %copy-done.6, bf16[512,4096]{1,0:T(8,128)(2,1)S(1)} %copy-done.4), kind=kOutput, calls=%fused_computation.3 | convolution fusion | flops 4299161600 | bytes 13631488 | tf_op jit(solution)/shard_map/dot_general | solution.py:846
  292.7 2.6 convolution_convert_fusion.3.refs_1_
  295.3 5.4 convolution_convert_fusion.2.refs_0_
  300.6 282.2 %reduce_gradients.1 = (bf16[1024,3072]{1,0:T(8,128)(2,1)}, bf16[1024,1024]{1,0:T(8,128)(2,1)}, bf16[1024,4096]{1,0:T(8,128)(2,1)}, bf16[4096,1024]{1,0:T(8,128)(2,1)}, bf16[256,128]{1,0:T(8,128)(2,1)}) custom-call(bf16[1024,3072]{1,0:T(8,128)(2,1)} %convolution_convert_fusion.2.refs_0_, bf16[1024,1024]{1,0:T(8,128)(2,1)} %convolution_convert_fusion.3.refs_1_, ...), custom_call_target="tpu_custom_call" | custom-call | tf_op jit(solution)/shard_map/reduce_gradients/pallas_call | solution.py:424
  582.9 11.8 %bitcast_convert_fusion = f32[1,4096,1024]{2,1,0:T(8,128)} fusion(bf16[4096,1024]{1,0:T(8,128)(2,1)} %get-tuple-element.57), kind=kLoop, calls=%fused_computation | loop fusion | flops 4194304 | bytes 25165824 | tf_op jit(solution)/shard_map/broadcast_in_dim | solution.py:902
  594.7 12.0 %bitcast_convert_fusion.1 = f32[1,1024,4096]{2,1,0:T(8,128)} fusion(bf16[1024,4096]{1,0:T(8,128)(2,1)} %get-tuple-element.56), kind=kLoop, calls=%fused_computation.1 | loop fusion | flops 4194304 | bytes 25165824 | tf_op jit(solution)/shard_map/broadcast_in_dim | solution.py:900
  606.7 6.4 %bitcast_convert_fusion.2 = f32[1,1024,3072]{2,1,0:T(8,128)} fusion(bf16[1024,3072]{1,0:T(8,128)(2,1)S(1)} %bitcast.34), kind=kLoop, calls=%fused_computation.4 | loop fusion | flops 3145728 | bytes 18874368 | tf_op jit(solution)/shard_map/broadcast_in_dim | solution.py:898
  613.2 2.5 bitcast_convert_fusion.3
  616.5 0.7 broadcast_in_dim_reshape.12
  617.1 0.7 broadcast_in_dim_reshape.13
  617.8 0.7 broadcast_in_dim_reshape.15
  618.5 0.8 copy.26
  619.3 0.8 copy.27
  (36 shorter events, 2.6 us)
Async XLA Ops:
  275.2 10.6 %copy-start.4 = (bf16[512,4096]{1,0:T(8,128)(2,1)S(1)}, bf16[512,4096]{1,0:T(8,128)(2,1)}, u32[]{:S(2)}) copy-start(bf16[512,4096]{1,0:T(8,128)(2,1)} %get-tuple-element.47) | copy-start | bytes 12582916
  275.2 10.6 %copy-start.6 = (bf16[512,1024]{1,0:T(8,128)(2,1)S(1)}, bf16[512,1024]{1,0:T(8,128)(2,1)}, u32[]{:S(2)}) copy-start(bf16[512,1024]{1,0:T(8,128)(2,1)} %get-tuple-element.43) | copy-start | bytes 3145732
  285.8 6.8 %copy-start.7 = (bf16[512,1024]{1,0:T(8,128)(2,1)S(1)}, bf16[512,1024]{1,0:T(8,128)(2,1)}, u32[]{:S(2)}) copy-start(bf16[512,1024]{1,0:T(8,128)(2,1)} %get-tuple-element.45) | copy-start | bytes 3145732
  285.8 6.8 %copy-start.8 = (bf16[512,1024]{1,0:T(8,128)(2,1)S(1)}, bf16[512,1024]{1,0:T(8,128)(2,1)}, u32[]{:S(2)}) copy-start(bf16[512,1024]{1,0:T(8,128)(2,1)} %get-tuple-element.46) | copy-start | bytes 3145732
  292.7 2.6 copy-start.5
  582.9 23.8 %slice-start = ((s8[6291456]{0:T(1024)(128)(4,1)}), s8[4194304]{0:T(1024)(128)(4,1)S(1)}, s32[]{:S(2)}) async-start(s8[6291456]{0:T(1024)(128)(4,1)} %bitcast.33), calls=%async_computation | async-start | bytes 8388608
  594.7 12.0 %slice-start.1 = ((s8[6291456]{0:T(1024)(128)(4,1)}), s8[2097152]{0:T(1024)(128)(4,1)S(1)}, s32[]{:S(2)}) async-start(s8[6291456]{0:T(1024)(128)(4,1)} %bitcast.33), calls=%async_computation.1 | async-start | bytes 4194304
  606.7 6.4 %copy-start = (bf16[1024,1024]{1,0:T(8,128)(2,1)S(1)}, bf16[1024,1024]{1,0:T(8,128)(2,1)}, u32[]{:S(2)}) copy-start(bf16[1024,1024]{1,0:T(8,128)(2,1)} %get-tuple-element.55) | copy-start | bytes 6291460
  613.2 2.5 copy-start.3
  613.2 5.3 copy-start.2
  613.2 6.1 copy-start.1

commit v4 on v3

--- a/solution.py
+++ b/solution.py
@@ -31,6 +31,7 @@
     def __init__(self):
         index = lax.axis_index("batch")
         self.levels = lax.axis_size("batch") // 4
+        self.last = self.levels - 1
         self.z, self.y, self.c = index // 4, index // 2 % 2, index % 2
 
     def at(self, z=None, y=None, c=None):
@@ -40,6 +41,28 @@
         return z * 4 + y * 2 + c
 
 
+class Piece:
+    def __init__(self, array, offset, rows, columns, direct):
+        self.array, self.offset, self.rows, self.columns = array, offset, rows, columns
+        self.direct = direct
+
+    def sides(self, y):
+        return (y,) if self.direct else (y, 1 - y)
+
+
+def pieces_of(blocks):
+    joint, output, expand, contract, small = blocks
+    cut = contract[0] // 4
+    return [
+        Piece(1, 0, *output, False),
+        Piece(3, 0, cut, contract[1], False),
+        Piece(0, 0, *joint, True),
+        Piece(2, 0, *expand, True),
+        Piece(3, cut, contract[0] - cut, contract[1], True),
+        Piece(4, 0, *small, True),
+    ]
+
+
 def remote(source, target, send, receive, index):
     return pltpu.make_async_remote_copy(
         source, target, send, receive, device_id={"batch": index}, device_id_type=MESH
@@ -55,45 +78,49 @@
     signal(batch=here.at(y=1 - here.y))
     signal(batch=here.at(c=1 - here.c))
     pl.when(here.z > 0)(lambda: signal(batch=here.at(z=here.z - 1)))
-    pl.when(here.z < here.levels - 1)(lambda: signal(batch=here.at(z=here.z + 1)))
+    pl.when(here.z < here.last)(lambda: signal(batch=here.at(z=here.z + 1)))
     waits = 2
     if with_section:
         signal(section=1 - lax.axis_index("section"))
         waits = 3
     below = jnp.minimum(here.z, 1)
-    above = jnp.minimum(here.levels - 1 - here.z, 1)
+    above = jnp.minimum(here.last - here.z, 1)
     pl.semaphore_wait(barrier, waits + below + above)
 
 
-def spread_semaphores(pieces, levels):
+def spread_semaphores(count, levels):
     dma = pltpu.SemaphoreType.DMA
     return [
-        dma((pieces,)),
-        dma((pieces, levels, 2)),
-        dma((pieces, levels)),
-        dma((pieces, levels)),
-        dma((pieces, levels)),
-        dma((pieces, levels, 2)),
-        dma((pieces, levels, 2)),
+        dma((count,)),
+        dma((count, levels, 2, 2)),
+        dma((count, levels, 2)),
+        dma((count, levels)),
+        dma((count, levels)),
+        dma((count, levels, 2)),
+        dma((count, levels, 2)),
     ]
 
 
 class Spread:
-    def __init__(self, here, owns, outs, semaphores):
-        self.here, self.owns, self.outs = here, owns, outs
+    def __init__(self, here, pieces, owns, outs, semaphores):
+        self.here, self.pieces, self.owns, self.outs = here, pieces, owns, outs
         (self.keep, self.zs, self.zr, self.ys, self.yr, self.cs, self.cr) = semaphores
 
     def block(self, p, z, y, c):
-        rows = self.outs[p].shape[0] // (4 * self.here.levels)
-        start = pl.multiple_of((z * 4 + y * 2 + c) * rows, rows)
-        return self.outs[p].at[pl.ds(start, rows), :]
-
-    def along(self, p, z, source, way):
-        here = self.here
-        target = self.block(p, z, here.y, here.c)
-        step = 1 if way == 0 else -1
+        piece = self.pieces[p]
+        out = self.outs[piece.array]
+        rows = out.shape[0] // (4 * self.here.levels)
+        start = (z * 4 + y * 2 + c) * rows + piece.offset
+        return out.at[pl.ds(pl.multiple_of(start, 8), piece.rows), :]
+
+    def along(self, p, z, y, source, way):
+        here = self.here
         return remote(
-            source, target, self.zs.at[p, z, way], self.zr.at[p, z], here.at(z=here.z + step)
+            source,
+            self.block(p, z, y, here.c),
+            self.zs.at[p, z, y, way],
+            self.zr.at[p, z, y],
+            here.at(z=here.z + (1 if way == 0 else -1)),
         )
 
     def across(self, p, z, source):
@@ -108,97 +135,108 @@
             source, target, self.cs.at[p, z, y], self.cr.at[p, z, y], here.at(c=1 - here.c)
         )
 
+    def both_ways(self, p, y, source):
+        here = self.here
+        pl.when(here.z < here.last)(lambda: self.along(p, here.z, y, source, 0).start())
+        pl.when(here.z > 0)(lambda: self.along(p, here.z, y, source, 1).start())
+
     def begin(self, p):
-        here = self.here
-        own, last = self.owns[p], here.levels - 1
-        pl.when(here.z < last)(lambda: self.along(p, here.z, own, 0).start())
-        pl.when(here.z > 0)(lambda: self.along(p, here.z, own, 1).start())
+        here, own = self.here, self.owns[p]
         self.across(p, here.z, own).start()
+        self.both_ways(p, here.y, own)
         self.beside(p, here.z, here.y, own).start()
-        pltpu.make_async_copy(
-            own, self.block(p, here.z, here.y, here.c), self.keep.at[p]
-        ).start()
-
-    def from_z(self, p, z, way):
-        here = self.here
-        block = self.block(p, z, here.y, here.c)
-        self.along(p, z, block, way).wait_recv()
-        more = here.z < here.levels - 1 if way == 0 else here.z > 0
-        pl.when(more)(lambda: self.along(p, z, block, way).start())
-        self.across(p, z, block).start()
-        self.beside(p, z, here.y, block).start()
+        target = self.block(p, here.z, here.y, here.c)
+        pltpu.make_async_copy(own, target, self.keep.at[p]).start()
+
+    def from_z(self, p, z, y, way):
+        here = self.here
+        block = self.block(p, z, y, here.c)
+        self.along(p, z, y, block, way).wait_recv()
+        more = here.z < here.last if way == 0 else here.z > 0
+        pl.when(more)(lambda: self.along(p, z, y, block, way).start())
+        if self.pieces[p].direct:
+            self.across(p, z, block).start()
+        self.beside(p, z, y, block).start()
 
     def from_y(self, p, z):
         here = self.here
         block = self.block(p, z, 1 - here.y, here.c)
         self.across(p, z, block).wait_recv()
+        if not self.pieces[p].direct:
+            self.both_ways(p, 1 - here.y, block)
         self.beside(p, z, 1 - here.y, block).start()
 
+    def swap(self):
+        for p, piece in enumerate(self.pieces):
+            if not piece.direct:
+                self.from_y(p, self.here.z)
+
+    def z_events(self, z, way):
+        here = self.here
+        for p in range(len(self.pieces)):
+            self.from_z(p, z, here.y, way)
+        for p, piece in enumerate(self.pieces):
+            if not piece.direct:
+                self.from_z(p, z, 1 - here.y, way)
+
+    def y_events(self, z):
+        for p, piece in enumerate(self.pieces):
+            if piece.direct:
+                self.from_y(p, z)
+
     def middle(self):
-        here, last = self.here, self.here.levels - 1
-        count = len(self.outs)
-
-        def y_events(distance):
-            @pl.when(here.z - distance >= 0)
-            def _():
-                for p in range(count):
-                    self.from_y(p, here.z - distance)
-
-            @pl.when((here.z + distance <= last) & (distance > 0))
-            def _():
-                for p in range(count):
-                    self.from_y(p, here.z + distance)
+        here = self.here
+
+        def y_pair(distance):
+            pl.when(here.z - distance >= 0)(lambda: self.y_events(here.z - distance))
+            pl.when((here.z + distance <= here.last) & (distance > 0))(
+                lambda: self.y_events(here.z + distance)
+            )
 
         def step(distance, carry):
-            @pl.when(here.z - distance >= 0)
-            def _():
-                for p in range(count):
-                    self.from_z(p, here.z - distance, 0)
-
-            @pl.when(here.z + distance <= last)
-            def _():
-                for p in range(count):
-                    self.from_z(p, here.z + distance, 1)
-
-            y_events(distance - 1)
+            pl.when(here.z - distance >= 0)(lambda: self.z_events(here.z - distance, 0))
+            pl.when(here.z + distance <= here.last)(lambda: self.z_events(here.z + distance, 1))
+            y_pair(distance - 1)
             return carry
 
         lax.fori_loop(1, here.levels, step, 0)
-        y_events(here.levels - 1)
+        y_pair(here.last)
 
     def finish(self):
-        here, last = self.here, self.here.levels - 1
+        here = self.here
 
         def level(z, carry):
-            for p in range(len(self.outs)):
+            for p, piece in enumerate(self.pieces):
                 own = self.block(p, z, here.y, here.c)
                 for y in range(2):
                     self.beside(p, z, y, own).wait_send()
                     self.beside(p, z, y, own).wait_recv()
-                self.across(p, z, own).wait_send()
-                pl.when((z <= here.z) & (here.z < last))(
-                    lambda p=p, own=own: self.along(p, z, own, 0).wait_send()
-                )
-                pl.when((z >= here.z) & (here.z > 0))(
-                    lambda p=p, own=own: self.along(p, z, own, 1).wait_send()
-                )
+                crossed = z >= 0 if piece.direct else z == here.z
+                pl.when(crossed)(lambda p=p, own=own: self.across(p, z, own).wait_send())
+                for y in piece.sides(here.y):
+                    pl.when((z <= here.z) & (here.z < here.last))(
+                        lambda p=p, y=y, own=own: self.along(p, z, y, own, 0).wait_send()
+                    )
+                    pl.when((z >= here.z) & (here.z > 0))(
+                        lambda p=p, y=y, own=own: self.along(p, z, y, own, 1).wait_send()
+                    )
             return carry
 
         lax.fori_loop(0, here.levels, level, 0)
-        for p in range(len(self.outs)):
+        for p in range(len(self.pieces)):
             block = self.block(p, here.z, here.y, here.c)
             pltpu.make_async_copy(block, block, self.keep.at[p]).wait()
 
 
 def gather_kernel(pieces, *refs):
-    owns, halves = refs[:pieces], refs[pieces : pieces + 2]
-    outs, wholes = refs[pieces + 2 : 2 * pieces + 2], refs[2 * pieces + 2 : 2 * pieces + 4]
-    half_send, half_receive, half_keep = refs[2 * pieces + 4 : 2 * pieces + 7]
+    sources, halves, outs, wholes = refs[:5], refs[5:7], refs[7:12], refs[12:14]
+    half_send, half_receive, half_keep = refs[14:17]
     here = Place()
     section = lax.axis_index("section")
     greet(here, True)
-    spread = Spread(here, owns, outs, refs[2 * pieces + 7 :])
-    for p in range(pieces):
+    owns = [sources[piece.array].at[pl.ds(piece.offset, piece.rows), :] for piece in pieces]
+    spread = Spread(here, pieces, owns, outs, refs[17:])
+    for p in range(len(pieces)):
         spread.begin(p)
     moves = []
     for i, (half, whole) in enumerate(zip(halves, wholes)):
@@ -216,6 +254,7 @@
         send.start()
         keep.start()
         moves.append((send, keep))
+    spread.swap()
     spread.middle()
     spread.finish()
     for send, keep in moves:
@@ -225,7 +264,7 @@
 
 def gather_all(owns, halves, number):
     levels = lax.axis_size("batch") // 4
-    pieces = len(owns)
+    pieces = pieces_of([own.shape for own in owns])
     shapes = [
         jax.ShapeDtypeStruct((own.shape[0] * 4 * levels, own.shape[1]), own.dtype) for own in owns
     ] + [jax.ShapeDtypeStruct((half.shape[0], half.shape[1] * 2), half.dtype) for half in halves]
@@ -233,13 +272,13 @@
     results = pl.pallas_call(
         partial(gather_kernel, pieces),
         out_shape=shapes,
-        in_specs=[ANY] * (pieces + 2),
-        out_specs=[ANY] * (pieces + 2),
-        scratch_shapes=[dma((2,)), dma((2,)), dma((2,))] + spread_semaphores(pieces, levels),
+        in_specs=[ANY] * 7,
+        out_specs=[ANY] * 7,
+        scratch_shapes=[dma((2,)), dma((2,)), dma((2,))] + spread_semaphores(len(pieces), levels),
         compiler_params=pltpu.CompilerParams(collective_id=number, has_side_effects=True),
         name="gather_weights",
     )(*owns, *halves)
-    return results[:pieces], results[pieces:]
+    return results[:5], results[5:]
 
 
 def add_rows(target, other):
@@ -255,29 +294,35 @@
     lax.fori_loop(0, rows // step, body, 0)
 
 
+FACTORS = ((0, 3), (1, 5), (0, 4), (2, 5))
+MAKE_ORDER = (1, 3, 0, 2, 4)
+COLUMN_STEP = 1024
+
+
 class Reduce:
-    def __init__(self, here, partials, mine, beside, across, along, semaphores):
-        self.here, self.partials = here, partials
-        self.mine, self.sib, self.yb, self.zb = mine, beside, across, along
-        (self.ls, self.cs, self.cr, self.ys, self.yr, self.zs, self.zr) = semaphores
-
-    def block(self, p, z, y, c):
-        rows = self.partials[p].shape[0] // (4 * self.here.levels)
-        start = pl.multiple_of((z * 4 + y * 2 + c) * rows, rows)
-        return self.partials[p].at[pl.ds(start, rows), :]
-
-    def load(self, p, z, y):
-        return pltpu.make_async_copy(
-            self.block(p, z, y, self.here.c), self.mine[p].at[z, y], self.ls.at[p, z, y]
-        )
-
-    def to_core(self, p, z, y):
+    def __init__(self, here, pieces, factors, small, product_rows, buffers, semaphores):
+        self.here, self.pieces, self.factors, self.small = here, pieces, factors, small
+        self.made = product_rows
+        self.mine, self.sent, self.sib, self.yb, self.zb = buffers
+        (self.load, self.cs, self.cr, self.ys, self.yr, self.zs, self.zr, self.credit) = semaphores
+
+    def level(self, i):
+        here = self.here
+        above, below = here.last - here.z, here.z
+        lead = jnp.maximum(above, below) - jnp.minimum(above, below)
+        single = jnp.where(above > below, here.last - i, i)
+        later = i - lead
+        distance = jnp.minimum(above, below) - later // 2
+        paired = jnp.where(later % 2 == 0, here.z + distance, here.z - distance)
+        return jnp.where(i < lead, single, paired)
+
+    def to_core(self, p, slot, y):
         here = self.here
         return remote(
-            self.block(p, z, y, 1 - here.c),
-            self.sib[p].at[z, y],
-            self.cs.at[p, z, y],
-            self.cr.at[p, z, y],
+            self.sent[p].at[slot, y],
+            self.sib[p].at[slot, y],
+            self.cs.at[p, slot, y],
+            self.cr.at[p, slot, y],
             here.at(c=1 - here.c),
         )
 
@@ -285,153 +330,262 @@
         here = self.here
         return remote(
             self.mine[p].at[z, 1 - here.y],
-            self.yb[p].at[z],
+            self.yb[p].at[z if self.pieces[p].direct else 0],
             self.ys.at[p, z],
             self.yr.at[p, z],
             here.at(y=1 - here.y),
         )
 
-    def to_z(self, p, z, way):
-        here = self.here
+    def slot(self, z, at_z, way):
+        if way == 0:
+            return z
+        return jnp.where(z == at_z, self.here.levels, z)
+
+    def to_z(self, p, z, y, way):
+        here = self.here
+        step = 1 if way == 0 else -1
+        slot = self.slot(z, here.z + step, way)
+        side = 0 if self.pieces[p].direct else y
         return remote(
-            self.mine[p].at[z, here.y],
-            self.zb[p].at[way, z],
-            self.zs.at[p, z],
-            self.zr.at[p, way, z],
-            here.at(z=here.z + (1 if way == 0 else -1)),
+            self.mine[p].at[z, y],
+            self.zb[p].at[slot, side],
+            self.zs.at[p, z, side],
+            self.zr.at[p, slot, side],
+            here.at(z=here.z + step),
         )
 
-    def begin(self, p, z):
-        for y in range(2):
-            self.to_core(p, z, y).start()
-            self.load(p, z, y).start()
-
-    def cores(self, p, z):
-        here = self.here
-        for y in range(2):
-            self.to_core(p, z, y).wait_recv()
-            self.load(p, z, y).wait()
-            add_rows(self.mine[p].at[z, y], self.sib[p].at[z, y])
-        self.to_y(p, z).start()
+    def arrive(self, p, z, y, way):
+        here = self.here
+        slot = self.slot(z, here.z, way)
+        side = 0 if self.pieces[p].direct else y
+        block = self.zb[p].at[slot, side]
+        remote(
+            block, block, self.zs.at[p, z, side], self.zr.at[p, slot, side], here.at(y=1 - here.y)
+        ).wait_recv()
+        add_rows(self.mine[p].at[z, y], block)
+
+    def store(self, array, z, slot, y, own, value, column):
+        at = pl.ds(column, value.shape[1])
+        for p, piece in enumerate(self.pieces):
+            if piece.array == array:
+                target = self.mine[p].at[z, y] if own else self.sent[p].at[slot, y]
+                rows = value[piece.offset : piece.offset + piece.rows]
+                target[:, at] = rows.astype(jnp.bfloat16)
+
+    def make(self, array, z, slot):
+        here = self.here
+        rows = sum(piece.rows for piece in self.pieces if piece.array == array)
+        cores = ((False, 1 - here.c), (True, here.c))
+        if array == 4:
+            for own, c in cores:
+                for y in range(2):
+                    at = pl.multiple_of((z * 4 + y * 2 + c) * rows, 16)
+                    self.store(array, z, slot, y, own, self.small[pl.ds(at, rows), :], 0)
+            return
+        left, right = (self.factors[i] for i in FACTORS[array])
+        columns = right.shape[1]
+        tiles = range(0, columns, COLUMN_STEP)
+        if rows % 128 == 0:
+            for own, c in cores:
+                for y in range(2):
+                    at = pl.multiple_of((z * 4 + y * 2 + c) * rows, 128)
+                    turned = left[:, pl.ds(at, rows)].T
+                    for tile in tiles:
+                        value = product(turned, right[:, tile : tile + COLUMN_STEP])
+                        self.store(array, z, slot, y, own, value, tile)
+            return
+        span = max(4 * rows, 128)
+        start = z * 4 * rows // span * span
+        turned = left[:, pl.ds(pl.multiple_of(start, 128), span)].T
+        for tile in tiles:
+            self.made[:span, :] = product(turned, right[:, tile : tile + COLUMN_STEP])
+            for own, c in cores:
+                for y in range(2):
+                    at = pl.multiple_of((z * 4 + y * 2 + c) * rows - start, 8)
+                    self.store(array, z, slot, y, own, self.made[pl.ds(at, rows), :], tile)
+
+    def of(self, array):
+        return [p for p, piece in enumerate(self.pieces) if piece.array == array]
+
+    def build(self, i, waits):
+        here = self.here
+        z, slot = self.level(i), i % 2
+
+        @pl.when(i >= 2)
+        def _():
+            for p in range(len(self.pieces)):
+                for y in range(2):
+                    self.to_core(p, slot, y).wait_send()
+            pl.semaphore_wait(self.credit, 1)
+
+        def add(array):
+            for p in self.of(array):
+                for y in range(2):
+                    self.to_core(p, slot, y).wait_recv()
+                    add_rows(self.mine[p].at[z, y], self.sib[p].at[slot, y])
+                if self.pieces[p].direct:
+                    self.to_y(p, z).start()
+
+        for step, array in enumerate(MAKE_ORDER):
+            waits(i, array)
+            self.make(array, z, slot)
+            for p in self.of(array):
+                for y in range(2):
+                    self.to_core(p, slot, y).start()
+            if step > 0:
+                add(MAKE_ORDER[step - 1])
+        add(MAKE_ORDER[-1])
+
+        @pl.when(i < here.levels - 2)
+        def _():
+            other = {"batch": here.at(c=1 - here.c)}
+            pl.semaphore_signal(self.credit, inc=1, device_id=other, device_id_type=MESH)
 
     def rows(self, p, z):
         self.to_y(p, z).wait_recv()
-        add_rows(self.mine[p].at[z, self.here.y], self.yb[p].at[z])
-
-    def arrive(self, p, z, way):
-        self.to_z(p, z, way).wait_recv()
-        add_rows(self.mine[p].at[z, self.here.y], self.zb[p].at[way, z])
-
-    def both(self, distance, action):
-        here, last = self.here, self.here.levels - 1
-
-        @pl.when(here.z + distance <= last)
+        source = self.yb[p].at[z if self.pieces[p].direct else 0]
+        add_rows(self.mine[p].at[z, self.here.y], source)
+
+    def pass_on(self, z):
+        here = self.here
+
+        def hop(way):
+            further = here.z > 0 if way == 0 else here.z < here.last
+            for direct in (False, True):
+                for p, piece in enumerate(self.pieces):
+                    if piece.direct != direct:
+                        continue
+                    if direct:
+                        self.rows(p, z)
+                    for y in piece.sides(here.y):
+                        pl.when(further)(lambda p=p, y=y: self.arrive(p, z, y, way))
+                        self.to_z(p, z, y, way).start()
+
+        pl.when(z > here.z)(lambda: hop(0))
+        pl.when(z < here.z)(lambda: hop(1))
+
+    def run(self, waits):
+        here = self.here
+
+        def step(i, carry):
+            self.build(i, waits)
+            pl.when(i > 0)(lambda: self.pass_on(self.level(i - 1)))
+            return carry
+
+        lax.fori_loop(0, here.levels, step, 0)
+
+    def settle(self, p):
+        here = self.here
+        for y in self.pieces[p].sides(here.y):
+            pl.when(here.z > 0)(lambda y=y: self.arrive(p, here.z, y, 0))
+            pl.when(here.z < here.last)(lambda y=y: self.arrive(p, here.z, y, 1))
+
+    def finish(self):
+        here = self.here
+        for slot in range(min(2, here.levels)):
+            for p in range(len(self.pieces)):
+                for y in range(2):
+                    self.to_core(p, slot, y).wait_send()
+
+        def level(z, carry):
+            for p, piece in enumerate(self.pieces):
+                crossed = z >= 0 if piece.direct else z == here.z
+                pl.when(crossed)(lambda p=p: self.to_y(p, z).wait_send())
+                for y in piece.sides(here.y):
+                    pl.when(z > here.z)(lambda p=p, y=y: self.to_z(p, z, y, 0).wait_send())
+                    pl.when(z < here.z)(lambda p=p, y=y: self.to_z(p, z, y, 1).wait_send())
+            return carry
+
+        lax.fori_loop(0, here.levels, level, 0)
+
+
+def reduce_kernel(pieces, *refs):
+    count = len(pieces)
+    sources, outs, rest = refs[:7], refs[7:12], refs[12:]
+    factors, small, made = rest[:6], rest[6], rest[7]
+    rest = rest[8:]
+    buffers = [rest[i * count : (i + 1) * count] for i in range(5)]
+    rest = rest[5 * count :]
+    here = Place()
+    loads = [
+        pltpu.make_async_copy(source, target, rest[0].at[i])
+        for i, (source, target) in enumerate(zip(sources, [*factors, small]))
+    ]
+    order = (1, 5, 2, 0, 3, 4, 6)
+    for i in order:
+        loads[i].start()
+    greet(here, False)
+    reduce = Reduce(here, pieces, factors, small, made, buffers, rest[:8])
+    needs = {1: (1, 5), 3: (2,), 0: (0, 3), 2: (4,), 4: (6,)}
+
+    def waits(i, array):
+        @pl.when(i == 0)
         def _():
-            for p in range(len(self.partials)):
-                action(p, here.z + distance, 0)
-
-        @pl.when(here.z - distance >= 0)
-        def _():
-            for p in range(len(self.partials)):
-                action(p, here.z - distance, 1)
-
-    def pass_on(self, p, z, way):
-        here, last = self.here, self.here.levels - 1
-        self.rows(p, z)
-        pl.when(here.z > 0 if way == 0 else here.z < last)(lambda: self.arrive(p, z, way))
-        self.to_z(p, z, way).start()
-
-    def run(self):
-        here, last = self.here, self.here.levels - 1
-        count = len(self.partials)
-
-        def start(i, carry):
-            self.both(last - i, lambda p, z, way: self.begin(p, z))
-            return carry
-
-        lax.fori_loop(0, last, start, 0)
-        for p in range(count):
-            self.begin(p, here.z)
-
-        def step(i, carry):
-            distance = last - i
-            self.both(distance, lambda p, z, way: self.cores(p, z))
-            pl.when(i > 0)(lambda: self.both(distance + 1, self.pass_on))
-            return carry
-
-        lax.fori_loop(0, last, step, 0)
-        for p in range(count):
-            self.cores(p, here.z)
-        self.both(1, self.pass_on)
-
-    def own(self, p):
-        here, last = self.here, self.here.levels - 1
-        self.rows(p, here.z)
-        pl.when(here.z > 0)(lambda: self.arrive(p, here.z, 0))
-        pl.when(here.z < last)(lambda: self.arrive(p, here.z, 1))
-        return self.mine[p].at[here.z, here.y]
-
-    def finish(self):
-        here = self.here
-
-        def level(z, carry):
-            for p in range(len(self.partials)):
-                for y in range(2):
-                    self.to_core(p, z, y).wait_send()
-                self.to_y(p, z).wait_send()
-                pl.when(z > here.z)(lambda p=p: self.to_z(p, z, 0).wait_send())
-                pl.when(z < here.z)(lambda p=p: self.to_z(p, z, 1).wait_send())
-            return carry
-
-        lax.fori_loop(0, here.levels, level, 0)
-
-
-def reduce_kernel(pieces, *refs):
-    partials, outs, rest = refs[:pieces], refs[pieces : 2 * pieces], refs[2 * pieces :]
-    mine, beside, across, along = (rest[i * pieces : (i + 1) * pieces] for i in range(4))
-    rest = rest[4 * pieces :]
-    here = Place()
-    greet(here, False)
-    reduce = Reduce(here, partials, mine, beside, across, along, rest[:7])
-    reduce.run()
-    owns = [mine[p].at[here.z, here.y] for p in range(pieces)]
-    spread = Spread(here, owns, outs, rest[7:])
-    for p in range(pieces):
-        reduce.own(p)
+            for k in needs[array]:
+                loads[k].wait()
+
+    reduce.run(waits)
+    owns = [buffers[0][p].at[here.z, here.y] for p in range(count)]
+    spread = Spread(here, pieces, owns, outs, rest[8:])
+    turned = [p for p in range(count) if not pieces[p].direct]
+    for p in turned:
+        reduce.settle(p)
+        reduce.to_y(p, here.z).start()
+    for p in range(count):
+        if pieces[p].direct:
+            reduce.rows(p, here.z)
+            reduce.settle(p)
+            spread.begin(p)
+    for p in turned:
+        reduce.rows(p, here.z)
         spread.begin(p)
+    spread.swap()
     spread.middle()
     reduce.finish()
     spread.finish()
 
 
-def reduce_all(partials, number):
+def reduce_all(factors, small, shapes, number):
     levels = lax.axis_size("batch") // 4
-    pieces = len(partials)
-    blocks = [(partial.shape[0] // (4 * levels), partial.shape[1]) for partial in partials]
+    shapes = [*shapes, small.shape]
+    pieces = pieces_of([(rows // (4 * levels), columns) for rows, columns in shapes])
+    count = len(pieces)
     dma = pltpu.SemaphoreType.DMA
-    scratch = []
-    for lead in ((levels, 2), (levels, 2), (levels,), (2, levels)):
-        scratch += [pltpu.VMEM(lead + block, jnp.bfloat16) for block in blocks]
+    low = jnp.bfloat16
+    scratch = [pltpu.VMEM(factor.shape, low) for factor in factors]
+    scratch += [pltpu.VMEM(small.shape, low), pltpu.VMEM((256, COLUMN_STEP), jnp.float32)]
+    blocks = [(piece.rows, piece.columns) for piece in pieces]
+    scratch += [pltpu.VMEM((levels, 2) + block, low) for block in blocks]
+    scratch += [pltpu.VMEM((2, 2) + block, low) for block in blocks] * 2
     scratch += [
-        dma((pieces, levels, 2)),
-        dma((pieces, levels, 2)),
-        dma((pieces, levels, 2)),
-        dma((pieces, levels)),
-        dma((pieces, levels)),
-        dma((pieces, levels)),
-        dma((pieces, 2, levels)),
-    ] + spread_semaphores(pieces, levels)
+        pltpu.VMEM((levels if piece.direct else 1,) + block, low)
+        for piece, block in zip(pieces, blocks)
+    ]
+    scratch += [
+        pltpu.VMEM((levels + 1, 1 if piece.direct else 2) + block, low)
+        for piece, block in zip(pieces, blocks)
+    ]
+    scratch += [
+        dma((7,)),
+        dma((count, 2, 2)),
+        dma((count, 2, 2)),
+        dma((count, levels)),
+        dma((count, levels)),
+        dma((count, levels, 2)),
+        dma((count, levels + 1, 2)),
+        pltpu.SemaphoreType.REGULAR,
+    ] + spread_semaphores(count, levels)
     return pl.pallas_call(
         partial(reduce_kernel, pieces),
-        out_shape=[jax.ShapeDtypeStruct(part.shape, jnp.bfloat16) for part in partials],
-        in_specs=[ANY] * pieces,
-        out_specs=[ANY] * pieces,
+        out_shape=[jax.ShapeDtypeStruct(shape, low) for shape in shapes],
+        in_specs=[ANY] * 7,
+        out_specs=[ANY] * 5,
         scratch_shapes=scratch,
         compiler_params=pltpu.CompilerParams(
             collective_id=number, has_side_effects=True, vmem_limit_bytes=60 * 2**20
         ),
         name="reduce_gradients",
-    )(*partials)
+    )(*factors, small)
 
 
 def rotary_rows():
@@ -842,10 +996,6 @@
     return members
 
 
-def partial_product(left, right):
-    return jnp.dot(left.T, right, preferred_element_type=jnp.float32).astype(jnp.bfloat16)
-
-
 def local(
     hidden_in,
     cotangent,
@@ -875,17 +1025,11 @@
     vectors = unpack_small(small_all, [member.shape[1] for member in vectors_own], devices)
     results = run_blocks(lengths, whole_in, whole_cotangent, vectors, weights, 2)
     hidden_out, input_grad = results[:2]
-    normed, mixture, activated, joint_part, pre_grad, upstream = results[2:8]
     small = results[8:]
-    partials = [
-        partial_product(normed, joint_part),
-        partial_product(mixture, upstream),
-        partial_product(normed, pre_grad),
-        partial_product(activated, upstream),
-        pack_small([member.reshape(devices, -1) for member in small]),
-    ]
+    small_packed = pack_small([member.reshape(devices, -1) for member in small])
+    shapes = [weight.shape for weight in weights]
     joint_sum, output_sum, expand_sum, contract_sum, small_sum = [
-        member.astype(jnp.float32) for member in reduce_all(partials, 3)
+        member.astype(jnp.float32) for member in reduce_all(results[2:8], small_packed, shapes, 3)
     ]
     gain_sum, offset_sum, outer_sum, inner_sum = unpack_small(
         small_sum, [member.shape[1] // devices for member in small], devices

time: 630 us -> 588 us (0.933); the launches traced: 620 us -> 587 us
  matrix products: 25.4 us -> 0 us
  Pallas kernels: 549 us -> 539 us
    dot_general x4 -> x0, matrix products: 25.4 us -> none  [partial_product(): jnp.dot(left.T, right, preferred_element_type=jnp.float32)]
    pallas_call x1, Pallas kernels: 144 us -> 135 us  [gather_all(): pl.pallas_call(partial(gather_kernel, pieces), out_shape=shapes, in_specs...]
where the time goes in v4:
time: 588 us; the launch traced here: 587 us
  Pallas kernels  539 us (92%)
  other arithmetic  36.5 us (6%)
  local copies, waits for them, and re-layouts  11 us (2%)
    pallas_call x1, Pallas kernels, reduce_all(): pl.pallas_call(partial(reduce_kernel, pieces), out_shape=[jax.ShapeDtypeS...  281 us
    pallas_call x1, Pallas kernels, gather_all(): pl.pallas_call(partial(gather_kernel, pieces), out_shape=shapes, in_specs...  135 us
    pallas_call x1, Pallas kernels, run_blocks(): pl.pallas_call(blocks_kernel, out_shape=outputs, in_specs=[pl.BlockSpec(m...  122 us
    broadcast_in_dim x1, other arithmetic, local(): expand_sum[None]  12 us
    broadcast_in_dim x1, other arithmetic, local(): contract_sum[None]  11.8 us

profile of v4, /device:TPU:1, one launch (start us, length us, event | category | flops | bytes accessed | tf_op | source)
XLA Modules:
  0.0 586.8 jit_solution(17489042032166370038)
XLA Ops:
  0.6 1.4 fusion.7
  2.0 135.1 %gather_weights.1 = (bf16[1024,3072]{1,0:T(8,128)(2,1)}, bf16[1024,1024]{1,0:T(8,128)(2,1)}, bf16[1024,4096]{1,0:T(8,128)(2,1)}, bf16[4096,1024]{1,0:T(8,128)(2,...) custom-call(bf16[64,3072]{1,0:T(8,128)(2,1)} %bitcast.29, ...), custom_call_target="tpu_custom_call" | custom-call | tf_op jit(solution)/shard_map/gather_weights/pallas_call | solution.py:272
  137.1 0.9 reshape.105
  138.1 0.7 reshape.112.refs_4_
  138.7 0.7 reshape.113.refs_5_
  139.4 0.7 reshape.114.refs_6_
  140.1 0.6 copy.22
  140.8 122.2 %two_blocks.1 = (bf16[512,512]{1,0:T(8,128)(2,1)}, bf16[512,512]{1,0:T(8,128)(2,1)}, bf16[512,1024]{1,0:T(8,128)(2,1)}, bf16[512,1024]{1,0:T(8,128)(2,1)}, bf16[...) custom-call(s32[2]{0:T(128)} %refs_0_.1, ...), custom_call_target="tpu_custom_call" | custom-call | tf_op jit(solution)/shard_map/two_blocks/pallas_call | solution.py:971
  263.0 0.7 convert_reduce_fusion.1
  263.8 0.8 convert_reduce_fusion
  264.6 0.7 convert_reduce_fusion.3
  265.4 0.1 fusion.6
  265.5 0.7 convert_element_type.80.refs_6_
  266.1 281.4 %reduce_gradients.1 = (bf16[1024,3072]{1,0:T(8,128)(2,1)}, bf16[1024,1024]{1,0:T(8,128)(2,1)}, bf16[1024,4096]{1,0:T(8,128)(2,1)}, bf16[4096,1024]{1,0:T(8,128)(2,1)}, bf16[256,128]{1,0:T(8,128)(2,1)}) custom-call(bf16[512,1024]{1,0:T(8,128)(2,1)} %get-tuple-element.43.refs_0_, bf16[512,1024]{1,0:T(8,128)(2,1)} %get-tuple-element.44.refs_1_, ...), custom_call_target="tpu_custom_call" | custom-call | tf_op jit(solution)/shard_map/reduce_gradients/pallas_call | solution.py:578
  547.5 11.8 %bitcast_convert_fusion = f32[1,4096,1024]{2,1,0:T(8,128)} fusion(bf16[4096,1024]{1,0:T(8,128)(2,1)} %get-tuple-element.57), kind=kLoop, calls=%fused_computation | loop fusion | flops 4194304 | bytes 25165824 | tf_op jit(solution)/shard_map/broadcast_in_dim | solution.py:1046
  559.4 12.0 %bitcast_convert_fusion.1 = f32[1,1024,4096]{2,1,0:T(8,128)} fusion(bf16[1024,4096]{1,0:T(8,128)(2,1)} %get-tuple-element.56), kind=kLoop, calls=%fused_computation.1 | loop fusion | flops 4194304 | bytes 25165824 | tf_op jit(solution)/shard_map/broadcast_in_dim | solution.py:1044
  571.4 6.4 %bitcast_convert_fusion.2 = f32[1,1024,3072]{2,1,0:T(8,128)} fusion(bf16[1024,3072]{1,0:T(8,128)(2,1)S(1)} %bitcast.26), kind=kLoop, calls=%fused_computation.2 | loop fusion | flops 3145728 | bytes 18874368 | tf_op jit(solution)/shard_map/broadcast_in_dim | solution.py:1042
  577.8 2.5 bitcast_convert_fusion.3
  580.4 0.6 copy.23
  581.1 0.7 broadcast_in_dim_reshape.12
  581.8 0.7 broadcast_in_dim_reshape.13
  582.4 0.7 broadcast_in_dim_reshape.15
  583.1 1.9 copy.26
  585.0 1.9 copy.27
  (18 shorter events, 0.6 us)
Async XLA Ops:
  547.5 23.8 %slice-start = ((s8[6291456]{0:T(1024)(128)(4,1)}), s8[4194304]{0:T(1024)(128)(4,1)S(1)}, s32[]{:S(2)}) async-start(s8[6291456]{0:T(1024)(128)(4,1)} %bitcast.25), calls=%async_computation | async-start | bytes 8388608
  559.4 12.0 %slice-start.1 = ((s8[6291456]{0:T(1024)(128)(4,1)}), s8[2097152]{0:T(1024)(128)(4,1)S(1)}, s32[]{:S(2)}) async-start(s8[6291456]{0:T(1024)(128)(4,1)} %bitcast.25), calls=%async_computation.1 | async-start | bytes 4194304
  571.3 6.4 %copy-start = (bf16[1024,1024]{1,0:T(8,128)(2,1)S(1)}, bf16[1024,1024]{1,0:T(8,128)(2,1)}, u32[]{:S(2)}) copy-start(bf16[1024,1024]{1,0:T(8,128)(2,1)} %get-tuple-element.55) | copy-start | bytes 6291460
  571.4 8.9 %copy-start.1 = (bf16[256,128]{1,0:T(8,128)(2,1)S(1)}, bf16[256,128]{1,0:T(8,128)(2,1)}, u32[]{:S(2)}) copy-start(bf16[256,128]{1,0:T(8,128)(2,1)} %get-tuple-element.53) | copy-start | bytes 196612

commit v5 on v4

--- a/solution.py
+++ b/solution.py
@@ -140,10 +140,11 @@
         pl.when(here.z < here.last)(lambda: self.along(p, here.z, y, source, 0).start())
         pl.when(here.z > 0)(lambda: self.along(p, here.z, y, source, 1).start())
 
-    def begin(self, p):
+    def begin(self, p, held=False):
         here, own = self.here, self.owns[p]
         self.across(p, here.z, own).start()
-        self.both_ways(p, here.y, own)
+        if not held:
+            self.both_ways(p, here.y, own)
         self.beside(p, here.z, here.y, own).start()
         target = self.block(p, here.z, here.y, here.c)
         pltpu.make_async_copy(own, target, self.keep.at[p]).start()
@@ -173,11 +174,13 @@
 
     def z_events(self, z, way):
         here = self.here
-        for p in range(len(self.pieces)):
-            self.from_z(p, z, here.y, way)
         for p, piece in enumerate(self.pieces):
-            if not piece.direct:
-                self.from_z(p, z, 1 - here.y, way)
+            if piece.direct:
+                self.from_z(p, z, here.y, way)
+        for side in range(2):
+            for p, piece in enumerate(self.pieces):
+                if not piece.direct:
+                    self.from_z(p, z, piece.sides(here.y)[side], way)
 
     def y_events(self, z):
         for p, piece in enumerate(self.pieces):
@@ -236,8 +239,11 @@
     greet(here, True)
     owns = [sources[piece.array].at[pl.ds(piece.offset, piece.rows), :] for piece in pieces]
     spread = Spread(here, pieces, owns, outs, refs[17:])
-    for p in range(len(pieces)):
-        spread.begin(p)
+    turned = [p for p, piece in enumerate(pieces) if not piece.direct]
+    for p, piece in enumerate(pieces):
+        spread.begin(p, held=not piece.direct)
+    for p in turned:
+        spread.both_ways(p, here.y, owns[p])
     moves = []
     for i, (half, whole) in enumerate(zip(halves, wholes)):
         width = half.shape[1]
@@ -313,7 +319,8 @@
         single = jnp.where(above > below, here.last - i, i)
         later = i - lead
         distance = jnp.minimum(above, below) - later // 2
-        paired = jnp.where(later % 2 == 0, here.z + distance, here.z - distance)
+        outer = jnp.where(above > below, here.z - distance, here.z + distance)
+        paired = jnp.where(later % 2 == 0, outer, 2 * here.z - outer)
         return jnp.where(i < lead, single, paired)
 
     def to_core(self, p, slot, y):
@@ -425,6 +432,8 @@
                     add_rows(self.mine[p].at[z, y], self.sib[p].at[slot, y])
                 if self.pieces[p].direct:
                     self.to_y(p, z).start()
+                else:
+                    self.pass_on(z, [p])
 
         for step, array in enumerate(MAKE_ORDER):
             waits(i, array)
@@ -446,30 +455,29 @@
         source = self.yb[p].at[z if self.pieces[p].direct else 0]
         add_rows(self.mine[p].at[z, self.here.y], source)
 
-    def pass_on(self, z):
+    def pass_on(self, z, chosen):
         here = self.here
 
         def hop(way):
             further = here.z > 0 if way == 0 else here.z < here.last
-            for direct in (False, True):
-                for p, piece in enumerate(self.pieces):
-                    if piece.direct != direct:
-                        continue
-                    if direct:
-                        self.rows(p, z)
-                    for y in piece.sides(here.y):
-                        pl.when(further)(lambda p=p, y=y: self.arrive(p, z, y, way))
-                        self.to_z(p, z, y, way).start()
+            for p in chosen:
+                if self.pieces[p].direct:
+                    self.rows(p, z)
+                for y in self.pieces[p].sides(here.y):
+                    pl.when(further)(lambda p=p, y=y: self.arrive(p, z, y, way))
+                    self.to_z(p, z, y, way).start()
 
         pl.when(z > here.z)(lambda: hop(0))
         pl.when(z < here.z)(lambda: hop(1))
 
     def run(self, waits):
         here = self.here
+        made = [p for array in MAKE_ORDER for p in self.of(array)]
+        direct = [p for p in made if self.pieces[p].direct]
 
         def step(i, carry):
             self.build(i, waits)
-            pl.when(i > 0)(lambda: self.pass_on(self.level(i - 1)))
+            pl.when(i > 0)(lambda: self.pass_on(self.level(i - 1), direct))
             return carry
 
         lax.fori_loop(0, here.levels, step, 0)

time: 588 us -> 567 us (0.964)
  Pallas kernels: 539 us -> 518 us
    pallas_call x1, Pallas kernels: 281 us -> 264 us  [reduce_all(): pl.pallas_call(partial(reduce_kernel, pieces), out_shape=[jax.ShapeDtypeS...]
where the time goes in v5:
time: 567 us
  Pallas kernels  518 us (91%)
  other arithmetic  36.5 us (6%)
  local copies, waits for them, and re-layouts  11 us (2%)
    pallas_call x1, Pallas kernels, reduce_all(): pl.pallas_call(partial(reduce_kernel, pieces), out_shape=[jax.ShapeDtypeS...  264 us
    pallas_call x1, Pallas kernels, gather_all(): pl.pallas_call(partial(gather_kernel, pieces), out_shape=shapes, in_specs...  132 us
    pallas_call x1, Pallas kernels, run_blocks(): pl.pallas_call(blocks_kernel, out_shape=outputs, in_specs=[pl.BlockSpec(m...  122 us
    broadcast_in_dim x1, other arithmetic, local(): expand_sum[None]  12 us
    broadcast_in_dim x1, other arithmetic, local(): contract_sum[None]  11.8 us

profile of v5, /device:TPU:1, one launch (start us, length us, event | category | flops | bytes accessed | tf_op | source)
XLA Modules:
  0.0 566.5 jit_solution(6923444999866840017)
XLA Ops:
  0.6 1.4 fusion.7
  2.0 131.9 %gather_weights.1 = (bf16[1024,3072]{1,0:T(8,128)(2,1)}, bf16[1024,1024]{1,0:T(8,128)(2,1)}, bf16[1024,4096]{1,0:T(8,128)(2,1)}, bf16[4096,1024]{1,0:T(8,128)(2,...) custom-call(bf16[64,3072]{1,0:T(8,128)(2,1)} %bitcast.29, ...), custom_call_target="tpu_custom_call" | custom-call | tf_op jit(solution)/shard_map/gather_weights/pallas_call | solution.py:278
  133.9 0.9 reshape.105
  134.9 0.7 reshape.112.refs_4_
  135.5 0.7 reshape.113.refs_5_
  136.2 0.7 reshape.114.refs_6_
  136.9 0.6 copy.22
  137.6 122.2 %two_blocks.1 = (bf16[512,512]{1,0:T(8,128)(2,1)}, bf16[512,512]{1,0:T(8,128)(2,1)}, bf16[512,1024]{1,0:T(8,128)(2,1)}, bf16[512,1024]{1,0:T(8,128)(2,1)}, bf16[...) custom-call(s32[2]{0:T(128)} %refs_0_.1, ...), custom_call_target="tpu_custom_call" | custom-call | tf_op jit(solution)/shard_map/two_blocks/pallas_call | solution.py:979
  259.7 0.7 convert_reduce_fusion.1
  260.6 0.8 convert_reduce_fusion
  261.4 0.7 convert_reduce_fusion.3
  262.2 0.1 fusion.6
  262.3 0.7 convert_element_type.80.refs_6_
  262.9 264.3 %reduce_gradients.1 = (bf16[1024,3072]{1,0:T(8,128)(2,1)}, bf16[1024,1024]{1,0:T(8,128)(2,1)}, bf16[1024,4096]{1,0:T(8,128)(2,1)}, bf16[4096,1024]{1,0:T(8,128)(2,1)}, bf16[256,128]{1,0:T(8,128)(2,1)}) custom-call(bf16[512,1024]{1,0:T(8,128)(2,1)} %get-tuple-element.43.refs_0_, bf16[512,1024]{1,0:T(8,128)(2,1)} %get-tuple-element.44.refs_1_, ...), custom_call_target="tpu_custom_call" | custom-call | tf_op jit(solution)/shard_map/reduce_gradients/pallas_call | solution.py:586
  527.2 11.8 %bitcast_convert_fusion = f32[1,4096,1024]{2,1,0:T(8,128)} fusion(bf16[4096,1024]{1,0:T(8,128)(2,1)} %get-tuple-element.57), kind=kLoop, calls=%fused_computation | loop fusion | flops 4194304 | bytes 25165824 | tf_op jit(solution)/shard_map/broadcast_in_dim | solution.py:1054
  539.1 12.0 %bitcast_convert_fusion.1 = f32[1,1024,4096]{2,1,0:T(8,128)} fusion(bf16[1024,4096]{1,0:T(8,128)(2,1)} %get-tuple-element.56), kind=kLoop, calls=%fused_computation.1 | loop fusion | flops 4194304 | bytes 25165824 | tf_op jit(solution)/shard_map/broadcast_in_dim | solution.py:1052
  551.1 6.4 %bitcast_convert_fusion.2 = f32[1,1024,3072]{2,1,0:T(8,128)} fusion(bf16[1024,3072]{1,0:T(8,128)(2,1)S(1)} %bitcast.26), kind=kLoop, calls=%fused_computation.2 | loop fusion | flops 3145728 | bytes 18874368 | tf_op jit(solution)/shard_map/broadcast_in_dim | solution.py:1050
  557.5 2.5 bitcast_convert_fusion.3
  560.1 0.6 copy.23
  560.8 0.7 broadcast_in_dim_reshape.12
  561.5 0.7 broadcast_in_dim_reshape.13
  562.1 0.7 broadcast_in_dim_reshape.15
  562.8 1.9 copy.26
  564.7 1.9 copy.27
  (18 shorter events, 0.6 us)
Async XLA Ops:
  527.2 23.8 %slice-start = ((s8[6291456]{0:T(1024)(128)(4,1)}), s8[4194304]{0:T(1024)(128)(4,1)S(1)}, s32[]{:S(2)}) async-start(s8[6291456]{0:T(1024)(128)(4,1)} %bitcast.25), calls=%async_computation | async-start | bytes 8388608
  539.1 12.0 %slice-start.1 = ((s8[6291456]{0:T(1024)(128)(4,1)}), s8[2097152]{0:T(1024)(128)(4,1)S(1)}, s32[]{:S(2)}) async-start(s8[6291456]{0:T(1024)(128)(4,1)} %bitcast.25), calls=%async_computation.1 | async-start | bytes 4194304
  551.1 6.4 %copy-start = (bf16[1024,1024]{1,0:T(8,128)(2,1)S(1)}, bf16[1024,1024]{1,0:T(8,128)(2,1)}, u32[]{:S(2)}) copy-start(bf16[1024,1024]{1,0:T(8,128)(2,1)} %get-tuple-element.55) | copy-start | bytes 6291460
  551.1 8.9 %copy-start.1 = (bf16[256,128]{1,0:T(8,128)(2,1)S(1)}, bf16[256,128]{1,0:T(8,128)(2,1)}, u32[]{:S(2)}) copy-start(bf16[256,128]{1,0:T(8,128)(2,1)} %get-tuple-element.53) | copy-start | bytes 196612

commit v6 on v5

--- a/solution.py
+++ b/solution.py
@@ -42,25 +42,34 @@
 
 
 class Piece:
-    def __init__(self, array, offset, rows, columns, direct):
-        self.array, self.offset, self.rows, self.columns = array, offset, rows, columns
-        self.direct = direct
+    def __init__(self, array, offset, rows, column, columns, direct):
+        self.array, self.offset, self.rows = array, offset, rows
+        self.column, self.columns, self.direct = column, columns, direct
 
     def sides(self, y):
         return (y,) if self.direct else (y, 1 - y)
+
+    def of(self, block):
+        return block.at[pl.ds(self.offset, self.rows), pl.ds(self.column, self.columns)]
 
 
 def pieces_of(blocks):
     joint, output, expand, contract, small = blocks
     cut = contract[0] // 4
-    return [
-        Piece(1, 0, *output, False),
-        Piece(3, 0, cut, contract[1], False),
-        Piece(0, 0, *joint, True),
-        Piece(2, 0, *expand, True),
-        Piece(3, cut, contract[0] - cut, contract[1], True),
-        Piece(4, 0, *small, True),
+    pieces = [
+        Piece(1, 0, output[0], 0, output[1], False),
+        Piece(3, 0, cut, 0, contract[1], False),
     ]
+    for array, offset, (rows, columns), parts in (
+        (0, 0, joint, 1),
+        (2, 0, expand, 1),
+        (3, cut, contract, 1),
+        (4, 0, small, 1),
+    ):
+        for i in range(parts):
+            width = columns // parts
+            pieces.append(Piece(array, offset, rows - offset, i * width, width, True))
+    return pieces
 
 
 def remote(source, target, send, receive, index):
@@ -111,7 +120,9 @@
         out = self.outs[piece.array]
         rows = out.shape[0] // (4 * self.here.levels)
         start = (z * 4 + y * 2 + c) * rows + piece.offset
-        return out.at[pl.ds(pl.multiple_of(start, 8), piece.rows), :]
+        return out.at[
+            pl.ds(pl.multiple_of(start, 8), piece.rows), pl.ds(piece.column, piece.columns)
+        ]
 
     def along(self, p, z, y, source, way):
         here = self.here
@@ -149,6 +160,14 @@
         target = self.block(p, here.z, here.y, here.c)
         pltpu.make_async_copy(own, target, self.keep.at[p]).start()
 
+    def begin_all(self, chosen):
+        order = sorted(chosen, key=lambda p: self.pieces[p].direct)
+        for p in order:
+            self.begin(p, held=not self.pieces[p].direct)
+        for p in order:
+            if not self.pieces[p].direct:
+                self.both_ways(p, self.here.y, self.owns[p])
+
     def from_z(self, p, z, y, way):
         here = self.here
         block = self.block(p, z, y, here.c)
@@ -167,45 +186,67 @@
             self.both_ways(p, 1 - here.y, block)
         self.beside(p, z, 1 - here.y, block).start()
 
-    def swap(self):
-        for p, piece in enumerate(self.pieces):
-            if not piece.direct:
-                self.from_y(p, self.here.z)
-
-    def z_events(self, z, way):
-        here = self.here
-        for p, piece in enumerate(self.pieces):
-            if piece.direct:
-                self.from_z(p, z, here.y, way)
+    def z_events(self, chosen, distance):
+        here = self.here
+
+        def pair(p, side):
+            y = self.pieces[p].sides(here.y)[side]
+            pl.when(here.z - distance >= 0)(lambda: self.from_z(p, here.z - distance, y, 0))
+            pl.when(here.z + distance <= here.last)(
+                lambda: self.from_z(p, here.z + distance, y, 1)
+            )
+
+        for p in chosen:
+            if self.pieces[p].direct:
+                pair(p, 0)
         for side in range(2):
-            for p, piece in enumerate(self.pieces):
-                if not piece.direct:
-                    self.from_z(p, z, piece.sides(here.y)[side], way)
-
-    def y_events(self, z):
-        for p, piece in enumerate(self.pieces):
-            if piece.direct:
+            for p in chosen:
+                if not self.pieces[p].direct:
+                    pair(p, side)
+
+    def y_events(self, chosen, z):
+        for p in chosen:
+            if self.pieces[p].direct:
                 self.from_y(p, z)
 
-    def middle(self):
-        here = self.here
+    def middle(self, chosen, then=None):
+        here = self.here
+        for p in chosen:
+            if not self.pieces[p].direct:
+                self.from_y(p, here.z)
 
         def y_pair(distance):
-            pl.when(here.z - distance >= 0)(lambda: self.y_events(here.z - distance))
+            pl.when(here.z - distance >= 0)(lambda: self.y_events(chosen, here.z - distance))
             pl.when((here.z + distance <= here.last) & (distance > 0))(
-                lambda: self.y_events(here.z + distance)
+                lambda: self.y_events(chosen, here.z + distance)
             )
 
         def step(distance, carry):
-            pl.when(here.z - distance >= 0)(lambda: self.z_events(here.z - distance, 0))
-            pl.when(here.z + distance <= here.last)(lambda: self.z_events(here.z + distance, 1))
+            self.z_events(chosen, distance)
             y_pair(distance - 1)
             return carry
 
         lax.fori_loop(1, here.levels, step, 0)
+        if then is not None:
+            then()
         y_pair(here.last)
 
-    def finish(self):
+    def received(self, chosen):
+        here = self.here
+
+        def level(z, carry):
+            for p in chosen:
+                own = self.block(p, z, here.y, here.c)
+                for y in range(2):
+                    self.beside(p, z, y, own).wait_recv()
+            return carry
+
+        lax.fori_loop(0, here.levels, level, 0)
+        for p in chosen:
+            block = self.block(p, here.z, here.y, here.c)
+            pltpu.make_async_copy(block, block, self.keep.at[p]).wait()
+
+    def sent(self):
         here = self.here
 
         def level(z, carry):
@@ -213,7 +254,6 @@
                 own = self.block(p, z, here.y, here.c)
                 for y in range(2):
                     self.beside(p, z, y, own).wait_send()
-                    self.beside(p, z, y, own).wait_recv()
                 crossed = z >= 0 if piece.direct else z == here.z
                 pl.when(crossed)(lambda p=p, own=own: self.across(p, z, own).wait_send())
                 for y in piece.sides(here.y):
@@ -226,65 +266,6 @@
             return carry
 
         lax.fori_loop(0, here.levels, level, 0)
-        for p in range(len(self.pieces)):
-            block = self.block(p, here.z, here.y, here.c)
-            pltpu.make_async_copy(block, block, self.keep.at[p]).wait()
-
-
-def gather_kernel(pieces, *refs):
-    sources, halves, outs, wholes = refs[:5], refs[5:7], refs[7:12], refs[12:14]
-    half_send, half_receive, half_keep = refs[14:17]
-    here = Place()
-    section = lax.axis_index("section")
-    greet(here, True)
-    owns = [sources[piece.array].at[pl.ds(piece.offset, piece.rows), :] for piece in pieces]
-    spread = Spread(here, pieces, owns, outs, refs[17:])
-    turned = [p for p, piece in enumerate(pieces) if not piece.direct]
-    for p, piece in enumerate(pieces):
-        spread.begin(p, held=not piece.direct)
-    for p in turned:
-        spread.both_ways(p, here.y, owns[p])
-    moves = []
-    for i, (half, whole) in enumerate(zip(halves, wholes)):
-        width = half.shape[1]
-        mine = whole.at[:, pl.ds(pl.multiple_of(section * width, width), width)]
-        send = pltpu.make_async_remote_copy(
-            half,
-            mine,
-            half_send.at[i],
-            half_receive.at[i],
-            device_id={"section": 1 - section},
-            device_id_type=MESH,
-        )
-        keep = pltpu.make_async_copy(half, mine, half_keep.at[i])
-        send.start()
-        keep.start()
-        moves.append((send, keep))
-    spread.swap()
-    spread.middle()
-    spread.finish()
-    for send, keep in moves:
-        send.wait()
-        keep.wait()
-
-
-def gather_all(owns, halves, number):
-    levels = lax.axis_size("batch") // 4
-    pieces = pieces_of([own.shape for own in owns])
-    shapes = [
-        jax.ShapeDtypeStruct((own.shape[0] * 4 * levels, own.shape[1]), own.dtype) for own in owns
-    ] + [jax.ShapeDtypeStruct((half.shape[0], half.shape[1] * 2), half.dtype) for half in halves]
-    dma = pltpu.SemaphoreType.DMA
-    results = pl.pallas_call(
-        partial(gather_kernel, pieces),
-        out_shape=shapes,
-        in_specs=[ANY] * 7,
-        out_specs=[ANY] * 7,
-        scratch_shapes=[dma((2,)), dma((2,)), dma((2,))] + spread_semaphores(len(pieces), levels),
-        compiler_params=pltpu.CompilerParams(collective_id=number, has_side_effects=True),
-        name="gather_weights",
-    )(*owns, *halves)
-    return results[:5], results[5:]
 
 
 def add_rows(target, other):
@@ -372,16 +353,17 @@
         add_rows(self.mine[p].at[z, y], block)
 
     def store(self, array, z, slot, y, own, value, column):
-        at = pl.ds(column, value.shape[1])
         for p, piece in enumerate(self.pieces):
-            if piece.array == array:
+            first = max(column, piece.column)
+            end = min(column + value.shape[1], piece.column + piece.columns)
+            if piece.array == array and first < end:
                 target = self.mine[p].at[z, y] if own else self.sent[p].at[slot, y]
-                rows = value[piece.offset : piece.offset + piece.rows]
-                target[:, at] = rows.astype(jnp.bfloat16)
+                part = value[piece.offset : piece.offset + piece.rows, first - column : end - column]
+                target[:, first - piece.column : end - piece.column] = part.astype(jnp.bfloat16)
 
     def make(self, array, z, slot):
         here = self.here
-        rows = sum(piece.rows for piece in self.pieces if piece.array == array)
+        rows = max(p.offset + p.rows for p in self.pieces if p.array == array)
         cores = ((False, 1 - here.c), (True, here.c))
         if array == 4:
             for own, c in cores:
@@ -547,10 +529,10 @@
     for p in turned:
         reduce.rows(p, here.z)
         spread.begin(p)
-    spread.swap()
-    spread.middle()
+    spread.middle(range(count))
     reduce.finish()
-    spread.finish()
+    spread.received(range(count))
+    spread.sent()
 
 
 def reduce_all(factors, small, shapes, number):
@@ -642,7 +624,7 @@
     return pl.ds(pl.multiple_of(index * step, step), step)
 
 
-def forward_block(m, length, loads, refs):
+def attend(m, length, refs):
     (x, normed, qkv, attention, mixture, active, slope, total, result) = refs["state"]
     joint, output, expand, contract = refs["weights"]
     gain, offset, outer, inner = refs["vectors"]
@@ -656,7 +638,6 @@
         return carry
 
     lax.fori_loop(0, SLOT // ROW_STEP, norm, 0)
-    loads(0)
     for part in range(3):
         scale = HEAD_DIM**-0.5 if part == 0 else 1.0
         total[...] = product(normed[m], joint[:, part * width : (part + 1) * width])
@@ -694,10 +675,13 @@
         return carry
 
     lax.fori_loop(0, pairs, heads, 0, unroll=8)
-    loads(1)
+
+
+def feed(m, refs):
+    (x, normed, _, _, mixture, active, slope, total, result) = refs["state"]
+    joint, output, expand, contract = refs["weights"]
+    gain, offset, outer, inner = refs["vectors"]
     total[...] = x[m].astype(jnp.float32) + outer[...] + product(mixture[m], output[...])
-    loads(2)
-    loads(3)
 
     def hidden(i, carry):
         at = rows_at(i, FF_STEP)
@@ -790,33 +774,103 @@
     lax.fori_loop(0, SLOT // ROW_STEP, norm, 0)
 
 
-BLOCK_OUTPUTS = 12
-
-
-def blocks_kernel(*refs):
-    lengths, whole_in, cotangent, tables_in, gain, offset, outer, inner = refs[:8]
-    weight_sources = refs[8:12]
-    outs = refs[12:24]
-    weights = refs[24:28]
-    x, normed, qkv, attention, mixture, active, slope, total, result = refs[28:37]
-    upstream, mixture_grad, tables = refs[37:40]
-    weight_sem, in_sem, hand_send, hand_receive, half_send, half_receive, half_keep, out_sem = refs[
-        40:48
-    ]
-    hidden_out, input_grad = outs[:2]
-    factor_outs, sums = outs[2:8], outs[8:12]
+def vector_rows(width):
+    return max(1, width // LANES), max(1, LANES // width)
+
+
+def lane_range(device, width):
+    lane = lax.broadcasted_iota(jnp.int32, (1, LANES), 1)
+    start = device * width % LANES
+    return (lane >= start) & (lane < start + width)
+
+
+def unpack_vectors(small, devices, vectors):
+    width = vectors[0].shape[1] // devices
+    wide = vectors[3].shape[1] // devices
+
+    def gathered(index, shared):
+        rows = small[pl.ds(pl.multiple_of(index * shared * SMALL_ROWS, SMALL_ROWS), SMALL_ROWS), :]
+        total = rows.astype(jnp.float32)
+        for other in range(1, shared):
+            at = pl.multiple_of((index * shared + other) * SMALL_ROWS, SMALL_ROWS)
+            total += small[pl.ds(at, SMALL_ROWS), :].astype(jnp.float32)
+        return total
+
+    _, shared = vector_rows(width)
+
+    def narrow(index, carry):
+        total = gathered(index, shared)
+        at = rows_at(index, LANES)
+        for i in range(3):
+            vectors[i][:, at] = total[i : i + 1]
+        return carry
+
+    lax.fori_loop(0, devices // shared, narrow, 0)
+    count, shared_wide = vector_rows(wide)
+
+    def broad(index, carry):
+        total = gathered(index, shared_wide)
+        for i in range(count):
+            vectors[3][:, rows_at(index * count + i, LANES)] = total[3 + i : 4 + i]
+        return carry
+
+    lax.fori_loop(0, devices // shared_wide, broad, 0)
+
+
+def pack_sums(sums, devices, packed):
+    width = sums[0].shape[1] // devices
+    wide = sums[3].shape[1] // devices
+    count, _ = vector_rows(wide)
+    row = lax.broadcasted_iota(jnp.int32, (SMALL_ROWS, LANES), 0)
+
+    def device(index, carry):
+        rows = []
+        inside = lane_range(index, width)
+        for i in range(3):
+            rows.append(jnp.where(inside, sums[i][:, rows_at(index * width // LANES, LANES)], 0.0))
+        for i in range(count):
+            line = sums[3][:, rows_at(index * wide // LANES + i, LANES)]
+            rows.append(line if wide >= LANES else jnp.where(lane_range(index, wide), line, 0.0))
+        block = jnp.zeros((SMALL_ROWS, LANES), jnp.float32)
+        for i, line in enumerate(rows):
+            block = jnp.where(row == i, line, block)
+        packed[rows_at(index, SMALL_ROWS), :] = block.astype(jnp.bfloat16)
+        return carry
+
+    lax.fori_loop(0, devices, device, 0)
+
+
+def blocks_kernel(pieces, *refs):
+    lengths, hidden_in, cotangent, tables_in = refs[:4]
+    sources = refs[4:9]
+    hidden_out, input_grad = refs[9:11]
+    factor_outs, packed = refs[11:17], refs[17]
+    weights, small = refs[18:22], refs[22]
+    x, normed, qkv, attention, mixture, active, slope, total, result = refs[23:32]
+    upstream, mixture_grad, tables = refs[32:35]
+    vectors, sums = refs[35:39], refs[39:43]
+    table_sem, in_keep, in_send, in_receive, hand_send, hand_receive = refs[43:49]
+    half_send, half_receive, half_keep, out_sem = refs[49:53]
+    here = Place()
     section = lax.axis_index("section")
     partner = {"section": 1 - section}
-    barrier = pltpu.get_barrier_semaphore()
-    pl.semaphore_signal(barrier, inc=1, device_id=partner, device_id_type=MESH)
-    pl.semaphore_wait(barrier, 1)
     half = hidden_out.shape[1]
-
-    def loading(i):
-        return pltpu.make_async_copy(weight_sources[i], weights[i], weight_sem.at[i])
-
-    def taking(source, target, m):
-        return pltpu.make_async_copy(source.at[rows_at(m, SLOT), :], target.at[m], in_sem.at[m])
+    devices = 4 * here.levels
+
+    def keeping(source, target, start, m):
+        return pltpu.make_async_copy(
+            source.at[rows_at(m, SLOT), :], target.at[m, :, pl.ds(start, half)], in_keep.at[m]
+        )
+
+    def halving(source, target, start, m):
+        return pltpu.make_async_remote_copy(
+            source.at[rows_at(m, SLOT), :],
+            target.at[m, :, pl.ds(start, half)],
+            in_send.at[m],
+            in_receive.at[m],
+            device_id=partner,
+            device_id_type=MESH,
+        )
 
     def handing(target, m):
         return pltpu.make_async_remote_copy(
@@ -848,30 +902,55 @@
             source.at[m], factor_outs[i].at[rows_at(m, SLOT), :], out_sem.at[i, m]
         )
 
-    pltpu.make_async_copy(tables_in, tables, weight_sem.at[4]).start()
+    reading = pltpu.make_async_copy(tables_in, tables, table_sem.at[0])
+    reading.start()
     for m in range(MICRO):
-        pl.when(section == 0)(lambda m=m: taking(whole_in, x, m).start())
-        pl.when(section == 1)(lambda m=m: taking(cotangent, upstream, m).start())
-    for i in range(4):
-        loading(i).start()
+        pl.when(section == 0)(lambda m=m: keeping(hidden_in, x, 0, m).start())
+        pl.when(section == 1)(lambda m=m: keeping(cotangent, upstream, half, m).start())
     for total_sum in sums:
         total_sum[...] = jnp.zeros_like(total_sum)
-    pltpu.make_async_copy(tables_in, tables, weight_sem.at[4]).wait()
+    greet(here, True)
+    owns = [piece.of(sources[piece.array]) for piece in pieces]
+    spread = Spread(here, pieces, owns, [*weights, small], refs[53:])
+    early = [p for p, piece in enumerate(pieces) if piece.array in (0, 1, 4)]
+    late = [p for p, piece in enumerate(pieces) if piece.array in (2, 3)]
+    spread.begin_all(early)
+    for m in range(MICRO):
+        pl.when(section == 1)(lambda m=m: halving(hidden_in, x, half, m).start())
+        pl.when(section == 0)(lambda m=m: halving(cotangent, upstream, 0, m).start())
     shared = {
         "state": (x, normed, qkv, attention, mixture, active, slope, total, result),
         "weights": weights,
-        "vectors": (gain, offset, outer, inner),
+        "vectors": vectors,
         "tables": tables,
         "gradients": (upstream, mixture_grad),
         "sums": sums,
     }
+    spread.middle(early, lambda: spread.begin_all(late))
+    spread.received(early)
+    unpack_vectors(small, devices, vectors)
+    reading.wait()
+
+    @pl.when(section == 0)
+    def _():
+        def ahead(m, carry):
+            keeping(hidden_in, x, 0, m).wait()
+            halving(hidden_in, x, half, m).wait_recv()
+            attend(m, lengths[m], shared)
+            return carry
+
+        lax.fori_loop(0, MICRO, ahead, 0)
+
+    spread.middle(late)
+    spread.received(late)
 
     def forward(m, carry):
-        pl.when(section == 0)(lambda: taking(whole_in, x, m).wait())
-        pl.when(section == 1)(lambda: handing(x, m).wait_recv())
-        forward_block(
-            m, lengths[m], lambda i: pl.when(m == 0)(lambda: loading(i).wait()), shared
-        )
+        @pl.when(section == 1)
+        def _():
+            handing(x, m).wait_recv()
+            attend(m, lengths[m], shared)
+
+        feed(m, shared)
 
         @pl.when(section == 0)
         def _():
@@ -898,7 +977,8 @@
         def _():
             away(hidden_out, 0, m).wait_send()
             kept(hidden_out, half, m).wait()
-            taking(cotangent, upstream, m).wait()
+            keeping(cotangent, upstream, half, m).wait()
+            halving(cotangent, upstream, 0, m).wait_recv()
             row = lax.broadcasted_iota(jnp.int32, (SLOT, 1), 0)
             inside = (row < lengths[m]).astype(jnp.float32)
             masked = upstream[m].astype(jnp.float32) * inside
@@ -920,16 +1000,19 @@
         return carry
 
     lax.fori_loop(0, MICRO, backward, 0)
+    pack_sums(sums, devices, packed)
 
     def last(m, carry):
         @pl.when(section == 0)
         def _():
+            halving(cotangent, upstream, 0, m).wait_send()
             away(input_grad, half, m).wait_send()
             kept(input_grad, 0, m).wait()
             away(hidden_out, 0, m).wait_recv()
 
         @pl.when(section == 1)
         def _():
+            halving(hidden_in, x, half, m).wait_send()
             handing(upstream, m).wait_send()
             away(input_grad, half, m).wait_recv()
 
@@ -938,21 +1021,24 @@
         return carry
 
     lax.fori_loop(0, MICRO, last, 0)
-
-
-def run_blocks(lengths, whole_in, cotangent, vectors, weights, number):
-    tokens, width = whole_in.shape
-    wide = weights[2].shape[1]
-    half = width // lax.axis_size("section")
+    spread.sent()
+
+
+def run_blocks(lengths, hidden_in, cotangent, owns, number):
+    levels = lax.axis_size("batch") // 4
+    devices = 4 * levels
+    tokens, half = hidden_in.shape
+    width = half * lax.axis_size("section")
+    wide = owns[2].shape[1]
     low, full = jnp.bfloat16, jnp.float32
     shape = jax.ShapeDtypeStruct
     vmem = pltpu.VMEM
     dma = pltpu.SemaphoreType.DMA
-    inside = pl.BlockSpec(memory_space=vmem)
+    pieces = pieces_of([own.shape for own in owns])
     outputs = [shape((tokens, half), low)] * 2
     outputs += [shape((tokens, n), low) for n in (width, width, wide, 3 * width, wide, width)]
-    outputs += [shape((1, n), full) for n in (width, width, width, wide)]
-    scratch = [vmem(weight.shape, low) for weight in weights]
+    outputs += [shape((devices * SMALL_ROWS, LANES), low)]
+    scratch = [vmem((devices * own.shape[0], own.shape[1]), low) for own in owns]
     scratch += [
         vmem((MICRO, SLOT, width), low),
         vmem((MICRO, SLOT, width), low),
@@ -966,42 +1052,45 @@
         vmem((MICRO, SLOT, width), low),
         vmem((SLOT, width), low),
         vmem((3, SLOT, 2 * HEAD_DIM), full),
-        dma((5,)),
-        dma((MICRO,)),
-        dma((MICRO,)),
-        dma((MICRO,)),
-        dma((MICRO,)),
-        dma((MICRO,)),
-        dma((MICRO,)),
-        dma((6, MICRO)),
     ]
-    vectors = [vector.astype(full).reshape(1, -1) for vector in vectors]
+    scratch += [vmem((1, n), full) for n in (width, width, width, wide)] * 2
+    scratch += [dma((1,))] + [dma((MICRO,))] * 8 + [dma((6, MICRO))]
+    scratch += spread_semaphores(len(pieces), levels)
     return pl.pallas_call(
-        blocks_kernel,
+        partial(blocks_kernel, pieces),
         out_shape=outputs,
-        in_specs=[pl.BlockSpec(memory_space=pltpu.SMEM), ANY, ANY, ANY] + [inside] * 4 + [ANY] * 4,
-        out_specs=[ANY] * 8 + [inside] * 4,
+        in_specs=[pl.BlockSpec(memory_space=pltpu.SMEM)] + [ANY] * 8,
+        out_specs=[ANY] * 8 + [pl.BlockSpec(memory_space=vmem)],
         scratch_shapes=scratch,
         compiler_params=pltpu.CompilerParams(
             collective_id=number, has_side_effects=True, vmem_limit_bytes=60 * 2**20
         ),
         name="two_blocks",
-    )(lengths, whole_in, cotangent, jnp.asarray(rotary_rows()), *vectors, *weights)
-
-
-def pack_small(members):
-    flat = jnp.concatenate([member.astype(jnp.float32) for member in members], axis=1)
-    flat = jnp.pad(flat, ((0, 0), (0, SMALL_ROWS * LANES - flat.shape[1])))
-    return flat.reshape(-1, LANES).astype(jnp.bfloat16)
-
-
-def unpack_small(packed, widths, devices):
-    flat = packed.reshape(devices, -1)
-    members, start = [], 0
-    for width in widths:
-        members.append(flat[:, start : start + width].reshape(-1))
-        start += width
-    return members
+    )(lengths, hidden_in, cotangent, jnp.asarray(rotary_rows()), *owns)
+
+
+def pack_vectors(vectors):
+    device = lax.axis_index("batch")
+    rows = []
+    for vector in vectors:
+        width = vector.shape[1]
+        if width >= LANES:
+            rows.append(vector.reshape(-1, LANES))
+            continue
+        lines = jnp.tile(vector, (1, LANES // width))
+        rows.append(jnp.where(lane_range(device, width), lines, jnp.zeros_like(lines)))
+    rows = jnp.concatenate(rows)
+    return jnp.pad(rows, ((0, SMALL_ROWS - rows.shape[0]), (0, 0)))
+
+
+def unpack_sums(packed, width, wide, devices):
+    rows = packed.astype(jnp.float32).reshape(devices, SMALL_ROWS, LANES)
+    _, shared = vector_rows(width)
+    narrow = rows.reshape(-1, shared, SMALL_ROWS, LANES).sum(axis=1)
+    count, shared_wide = vector_rows(wide)
+    broad = rows.reshape(-1, shared_wide, SMALL_ROWS, LANES).sum(axis=1)
+    members = [narrow[:, i].reshape(1, -1) for i in range(3)]
+    return members + [broad[:, 3 : 3 + count].reshape(1, -1)]
 
 
 def local(
@@ -1018,41 +1107,37 @@
     outer_bias,
 ):
     devices = lax.axis_size("batch")
-    vectors_own = (norm_gain, norm_offset, outer_bias, inner_bias)
-    (*weights, small_all), (whole_in, whole_cotangent) = gather_all(
-        [
-            joint_weight[0],
-            output_weight[0],
-            expand_weight[0],
-            contract_weight[0],
-            pack_small(vectors_own),
-        ],
-        [hidden_in, cotangent],
-        1,
+    owns = [
+        joint_weight[0],
+        output_weight[0],
+        expand_weight[0],
+        contract_weight[0],
+        pack_vectors((norm_gain, norm_offset, outer_bias, inner_bias)),
+    ]
+    results = run_blocks(lengths, hidden_in, cotangent, owns, 1)
+    hidden_out, input_grad = results[:2]
+    shapes = [(own.shape[0] * devices, own.shape[1]) for own in owns[:4]]
+    joint_sum, output_sum, expand_sum, contract_sum, small_sum = reduce_all(
+        results[2:8], results[8], shapes, 2
     )
-    vectors = unpack_small(small_all, [member.shape[1] for member in vectors_own], devices)
-    results = run_blocks(lengths, whole_in, whole_cotangent, vectors, weights, 2)
-    hidden_out, input_grad = results[:2]
-    small = results[8:]
-    small_packed = pack_small([member.reshape(devices, -1) for member in small])
-    shapes = [weight.shape for weight in weights]
-    joint_sum, output_sum, expand_sum, contract_sum, small_sum = [
-        member.astype(jnp.float32) for member in reduce_all(results[2:8], small_packed, shapes, 3)
+    gain_sum, offset_sum, outer_sum, inner_sum = unpack_sums(
+        small_sum, norm_gain.shape[1], inner_bias.shape[1], devices
+    )
+    joint_sum, output_sum, expand_sum, contract_sum = [
+        member.astype(jnp.float32)[None]
+        for member in (joint_sum, output_sum, expand_sum, contract_sum)
     ]
-    gain_sum, offset_sum, outer_sum, inner_sum = unpack_small(
-        small_sum, [member.shape[1] // devices for member in small], devices
-    )
     return (
         hidden_out,
         input_grad,
-        gain_sum[None],
-        offset_sum[None],
-        joint_sum[None],
-        output_sum[None],
-        expand_sum[None],
-        inner_sum[None],
-        contract_sum[None],
-        outer_sum[None],
+        gain_sum,
+        offset_sum,
+        joint_sum,
+        output_sum,
+        expand_sum,
+        inner_sum,
+        contract_sum,
+        outer_sum,
     )
 
 

time: 567 us -> 561 us (0.989)
    pallas_call x2 -> x1, Pallas kernels: 254 us -> 249 us  [run_blocks(): pl.pallas_call(partial(blocks_kernel, pieces), out_shape=outputs, in_spec...]
where the time goes in v6:
time: 561 us; the launch traced here: 556 us
  Pallas kernels  514 us (92%)
  other arithmetic  34.1 us (6%)
  local copies, waits for them, and re-layouts  7.2 us (1%)
    pallas_call x1, Pallas kernels, reduce_all(): pl.pallas_call(partial(reduce_kernel, pieces), out_shape=[jax.ShapeDtypeS...  265 us
    pallas_call x1, Pallas kernels, run_blocks(): pl.pallas_call(partial(blocks_kernel, pieces), out_shape=outputs, in_spec...  249 us
    broadcast_in_dim x4, other arithmetic, local(): member.astype(jnp.float32)[None]  32.7 us

profile of v6, /device:TPU:1, one launch (start us, length us, event | category | flops | bytes accessed | tf_op | source)
XLA Modules:
  0.0 556.1 jit_solution(15944290279610787309)
XLA Ops:
  0.7 0.7 tile.34
  1.3 0.1 tile.35
  1.4 0.7 tile.37
  2.1 0.1 tile.38
  2.2 0.7 tile.40
  2.8 0.1 tile.41
  2.9 0.7 reduce
  3.6 0.6 fusion.6.refs_8_
  4.2 248.8 %two_blocks.1 = (bf16[512,512]{1,0:T(8,128)(2,1)}, bf16[512,512]{1,0:T(8,128)(2,1)}, bf16[512,1024]{1,0:T(8,128)(2,1)}, bf16[512,1024]{1,0:T(8,128)(2,1)}, bf16[...) custom-call(s32[2]{0:T(128)} %refs_0_.1, ...), custom_call_target="tpu_custom_call" | custom-call | tf_op jit(solution)/shard_map/two_blocks/pallas_call | solution.py:1059
  253.0 265.1 %reduce_gradients.1 = (bf16[1024,3072]{1,0:T(8,128)(2,1)}, bf16[1024,1024]{1,0:T(8,128)(2,1)}, bf16[1024,4096]{1,0:T(8,128)(2,1)}, bf16[4096,1024]{1,0:T(8,128)(2,1)}, bf16[256,128]{1,0:T(8,128)(2,1)}) custom-call(bf16[512,1024]{1,0:T(8,128)(2,1)} %get-tuple-element.26.refs_0_, bf16[512,1024]{1,0:T(8,128)(2,1)} %get-tuple-element.27.refs_1_, ...), custom_call_target="tpu_custom_call" | custom-call | tf_op jit(solution)/shard_map/reduce_gradients/pallas_call | solution.py:568
  518.1 0.0 slice-start
  518.1 11.8 %bitcast_convert_fusion = f32[1,4096,1024]{2,1,0:T(8,128)} fusion(bf16[4096,1024]{1,0:T(8,128)(2,1)} %get-tuple-element.37), kind=kLoop, calls=%fused_computation | loop fusion | flops 4194304 | bytes 25165824 | tf_op jit(solution)/shard_map/broadcast_in_dim | solution.py:1127
  529.9 12.0 %bitcast_convert_fusion.1 = f32[1,1024,4096]{2,1,0:T(8,128)} fusion(bf16[1024,4096]{1,0:T(8,128)(2,1)} %get-tuple-element.36), kind=kLoop, calls=%fused_computation.1 | loop fusion | flops 4194304 | bytes 25165824 | tf_op jit(solution)/shard_map/broadcast_in_dim | solution.py:1127
  541.9 0.0 slice-done
  541.9 0.0 slice-done.1
  541.9 0.0 copy-start.1
  541.9 6.4 %bitcast_convert_fusion.2 = f32[1,1024,3072]{2,1,0:T(8,128)} fusion(bf16[1024,3072]{1,0:T(8,128)(2,1)S(1)} %bitcast.30), kind=kLoop, calls=%fused_computation.2 | loop fusion | flops 3145728 | bytes 18874368 | tf_op jit(solution)/shard_map/broadcast_in_dim | solution.py:1127
  548.3 0.0 copy-done
  548.4 2.5 bitcast_convert_fusion.3
  550.8 0.0 copy-done.1
  550.9 0.6 slice_bitcast_fusion
  551.5 0.6 slice.18
  552.1 1.9 copy.24
  554.0 1.9 copy.25
  (7 shorter events, 0.0 us)
Async XLA Ops:
  518.1 23.8 %slice-start = ((s8[6291456]{0:T(1024)(128)(4,1)}), s8[4194304]{0:T(1024)(128)(4,1)S(1)}, s32[]{:S(2)}) async-start(s8[6291456]{0:T(1024)(128)(4,1)} %bitcast.29), calls=%async_computation | async-start | bytes 8388608
  529.9 12.0 %slice-start.1 = ((s8[6291456]{0:T(1024)(128)(4,1)}), s8[2097152]{0:T(1024)(128)(4,1)S(1)}, s32[]{:S(2)}) async-start(s8[6291456]{0:T(1024)(128)(4,1)} %bitcast.29), calls=%async_computation.1 | async-start | bytes 4194304
  541.9 6.4 %copy-start = (bf16[1024,1024]{1,0:T(8,128)(2,1)S(1)}, bf16[1024,1024]{1,0:T(8,128)(2,1)}, u32[]{:S(2)}) copy-start(bf16[1024,1024]{1,0:T(8,128)(2,1)} %get-tuple-element.35) | copy-start | bytes 6291460
  541.9 8.9 %copy-start.1 = (bf16[256,128]{1,0:T(8,128)(2,1)S(1)}, bf16[256,128]{1,0:T(8,128)(2,1)}, u32[]{:S(2)}) copy-start(bf16[256,128]{1,0:T(8,128)(2,1)} %get-tuple-element.33) | copy-start | bytes 196612

commit v7 on v6

--- a/solution.py
+++ b/solution.py
@@ -1071,26 +1071,54 @@
 
 def pack_vectors(vectors):
     device = lax.axis_index("batch")
-    rows = []
+    size = SMALL_ROWS * LANES
+    total = jnp.zeros((1, size), jnp.float32)
+    row = 0
     for vector in vectors:
         width = vector.shape[1]
-        if width >= LANES:
-            rows.append(vector.reshape(-1, LANES))
-            continue
-        lines = jnp.tile(vector, (1, LANES // width))
-        rows.append(jnp.where(lane_range(device, width), lines, jnp.zeros_like(lines)))
-    rows = jnp.concatenate(rows)
-    return jnp.pad(rows, ((0, SMALL_ROWS - rows.shape[0]), (0, 0)))
-
-
-def unpack_sums(packed, width, wide, devices):
-    rows = packed.astype(jnp.float32).reshape(devices, SMALL_ROWS, LANES)
-    _, shared = vector_rows(width)
-    narrow = rows.reshape(-1, shared, SMALL_ROWS, LANES).sum(axis=1)
-    count, shared_wide = vector_rows(wide)
-    broad = rows.reshape(-1, shared_wide, SMALL_ROWS, LANES).sum(axis=1)
-    members = [narrow[:, i].reshape(1, -1) for i in range(3)]
-    return members + [broad[:, 3 : 3 + count].reshape(1, -1)]
+        used = min(width, LANES)
+        slot = device * width % LANES // used
+        for i in range(LANES // used):
+            start = row * LANES + i * used
+            moved = jnp.pad(vector.astype(jnp.float32), ((0, 0), (start, size - start - width)))
+            total = total + jnp.where(slot == i, moved, 0.0)
+        row += max(1, width // LANES)
+    return total.reshape(SMALL_ROWS, LANES).astype(jnp.bfloat16)
+
+
+def widen_kernel(devices, *refs):
+    small, sources = refs[0], refs[1 : (len(refs) - 5) // 2 + 1]
+    targets, vectors = refs[len(sources) + 1 : -4], refs[-4:]
+    pl.when(pl.program_id(0) == 0)(lambda: unpack_vectors(small, devices, vectors))
+    for source, target in zip(sources, targets):
+        target[...] = source[...].astype(target.dtype).reshape(target.shape)
+
+
+def widen(small, sums, kept, widths, devices):
+    steps = 8
+    arrays = [*sums, *kept]
+    whole = lambda i: (0, 0)
+    in_specs = [
+        pl.BlockSpec((array.shape[0] // steps, array.shape[1]), lambda i: (i, 0))
+        for array in arrays
+    ]
+    out_specs = [
+        pl.BlockSpec((1, array.shape[0] // steps, array.shape[1]), lambda i: (0, i, 0))
+        for array in sums
+    ] + in_specs[len(sums) :]
+    out_specs += [pl.BlockSpec((1, width), whole) for width in widths]
+    shapes = [jax.ShapeDtypeStruct((1, *array.shape), jnp.float32) for array in sums]
+    shapes += [jax.ShapeDtypeStruct(array.shape, array.dtype) for array in kept]
+    shapes += [jax.ShapeDtypeStruct((1, width), jnp.float32) for width in widths]
+    return pl.pallas_call(
+        partial(widen_kernel, devices),
+        out_shape=shapes,
+        grid=(steps,),
+        in_specs=[pl.BlockSpec(small.shape, whole)] + in_specs,
+        out_specs=out_specs,
+        compiler_params=pltpu.CompilerParams(vmem_limit_bytes=60 * 2**20),
+        name="widen",
+    )(small, *arrays)
 
 
 def local(
@@ -1115,18 +1143,21 @@
         pack_vectors((norm_gain, norm_offset, outer_bias, inner_bias)),
     ]
     results = run_blocks(lengths, hidden_in, cotangent, owns, 1)
-    hidden_out, input_grad = results[:2]
     shapes = [(own.shape[0] * devices, own.shape[1]) for own in owns[:4]]
-    joint_sum, output_sum, expand_sum, contract_sum, small_sum = reduce_all(
-        results[2:8], results[8], shapes, 2
-    )
-    gain_sum, offset_sum, outer_sum, inner_sum = unpack_sums(
-        small_sum, norm_gain.shape[1], inner_bias.shape[1], devices
-    )
-    joint_sum, output_sum, expand_sum, contract_sum = [
-        member.astype(jnp.float32)[None]
-        for member in (joint_sum, output_sum, expand_sum, contract_sum)
-    ]
+    *sums, small_sum = reduce_all(results[2:8], results[8], shapes, 2)
+    width, wide = norm_gain.shape[1] * devices, inner_bias.shape[1] * devices
+    (
+        joint_sum,
+        output_sum,
+        expand_sum,
+        contract_sum,
+        hidden_out,
+        input_grad,
+        gain_sum,
+        offset_sum,
+        outer_sum,
+        inner_sum,
+    ) = widen(small_sum, sums, results[:2], (width, width, width, wide), devices)
     return (
         hidden_out,
         input_grad,

time: 561 us -> 545 us (0.971)
  other arithmetic: 34.1 us -> 3.34 us
  Pallas kernels: 514 us -> 541 us
  local copies, waits for them, and re-layouts: 7.2 us -> 0 us
    broadcast_in_dim x4 -> x0, other arithmetic: 32.7 us -> none  [local(): member.astype(jnp.float32)[None]]
    pallas_call x0 -> x1, Pallas kernels: none -> 26.4 us  [widen(): pl.pallas_call(partial(widen_kernel, devices), out_shape=shapes, grid=(st...]
where the time goes in v7:
time: 545 us
  Pallas kernels  541 us (99%)
    pallas_call x1, Pallas kernels, reduce_all(): pl.pallas_call(partial(reduce_kernel, pieces), out_shape=[jax.ShapeDtypeS...  266 us
    pallas_call x1, Pallas kernels, run_blocks(): pl.pallas_call(partial(blocks_kernel, pieces), out_shape=outputs, in_spec...  249 us
    pallas_call x1, Pallas kernels, widen(): pl.pallas_call(partial(widen_kernel, devices), out_shape=shapes, grid=(st...  26.4 us

profile of v7, /device:TPU:1, one launch (start us, length us, event | category | flops | bytes accessed | tf_op | source)
XLA Modules:
  0.0 545.2 jit_solution(16324485324230412916)
XLA Ops:
  0.7 0.7 convert_element_type.32
  1.4 0.7 convert_element_type.33
  2.0 0.7 convert_element_type.34
  2.7 1.4 convert_reduce_fusion
  4.0 248.8 %two_blocks.1 = (bf16[512,512]{1,0:T(8,128)(2,1)}, bf16[512,512]{1,0:T(8,128)(2,1)}, bf16[512,1024]{1,0:T(8,128)(2,1)}, bf16[512,1024]{1,0:T(8,128)(2,1)}, bf16[...) custom-call(s32[2]{0:T(128)} %refs_0_.1, ...), custom_call_target="tpu_custom_call" | custom-call | tf_op jit(solution)/shard_map/two_blocks/pallas_call | solution.py:1059
  252.9 265.7 %reduce_gradients.1 = (bf16[1024,3072]{1,0:T(8,128)(2,1)}, bf16[1024,1024]{1,0:T(8,128)(2,1)}, bf16[1024,4096]{1,0:T(8,128)(2,1)}, bf16[4096,1024]{1,0:T(8,128)(2,1)}, bf16[256,128]{1,0:T(8,128)(2,1)}) custom-call(bf16[512,1024]{1,0:T(8,128)(2,1)} %get-tuple-element.34.refs_0_, bf16[512,1024]{1,0:T(8,128)(2,1)} %get-tuple-element.35.refs_1_, ...), custom_call_target="tpu_custom_call" | custom-call | tf_op jit(solution)/shard_map/reduce_gradients/pallas_call | solution.py:568
  518.6 26.4 %widen.1 = (f32[1,1024,3072]{2,1,0:T(8,128)}, f32[1,1024,1024]{2,1,0:T(8,128)}, f32[1,1024,4096]{2,1,0:T(8,128)}, f32[1,4096,1024]{2,1,0:T(8,128)}, bf16[512,512...) custom-call(bf16[256,128]{1,0:T(8,128)(2,1)} %get-tuple-element.41.r, ...), custom_call_target="tpu_custom_call" | custom-call | tf_op jit(solution)/shard_map/widen/pallas_call | solution.py:1113

commit v8 on v7

--- a/solution.py
+++ b/solution.py
@@ -491,7 +491,7 @@
 
 def reduce_kernel(pieces, *refs):
     count = len(pieces)
-    sources, outs, rest = refs[:7], refs[7:12], refs[12:]
+    sources, change, outs, input_grad, rest = refs[:7], refs[7], refs[8:13], refs[13], refs[14:]
     factors, small, made = rest[:6], rest[6], rest[7]
     rest = rest[8:]
     buffers = [rest[i * count : (i + 1) * count] for i in range(5)]
@@ -504,7 +504,24 @@
     order = (1, 5, 2, 0, 3, 4, 6)
     for i in order:
         loads[i].start()
-    greet(here, False)
+    greet(here, True)
+    section = lax.axis_index("section")
+    half = input_grad.shape[1]
+    over = pltpu.make_async_remote_copy(
+        change.at[:, pl.ds(half, half)],
+        input_grad,
+        rest[-1].at[0],
+        rest[-1].at[1],
+        device_id={"section": 1 - section},
+        device_id_type=MESH,
+    )
+    keep = pltpu.make_async_copy(change.at[:, pl.ds(0, half)], input_grad, rest[-1].at[2])
+
+    @pl.when(section == 0)
+    def _():
+        over.start()
+        keep.start()
+
     reduce = Reduce(here, pieces, factors, small, made, buffers, rest[:8])
     needs = {1: (1, 5), 3: (2,), 0: (0, 3), 2: (4,), 4: (6,)}
 
@@ -516,7 +533,7 @@
 
     reduce.run(waits)
     owns = [buffers[0][p].at[here.z, here.y] for p in range(count)]
-    spread = Spread(here, pieces, owns, outs, rest[8:])
+    spread = Spread(here, pieces, owns, outs, rest[8:-1])
     turned = [p for p in range(count) if not pieces[p].direct]
     for p in turned:
         reduce.settle(p)
@@ -534,8 +551,15 @@
     spread.received(range(count))
     spread.sent()
 
-
-def reduce_all(factors, small, shapes, number):
+    @pl.when(section == 0)
+    def _():
+        over.wait_send()
+        keep.wait()
+
+    pl.when(section == 1)(over.wait_recv)
+
+
+def reduce_all(factors, small, change, shapes, number):
     levels = lax.axis_size("batch") // 4
     shapes = [*shapes, small.shape]
     pieces = pieces_of([(rows // (4 * levels), columns) for rows, columns in shapes])
@@ -564,18 +588,20 @@
         dma((count, levels, 2)),
         dma((count, levels + 1, 2)),
         pltpu.SemaphoreType.REGULAR,
-    ] + spread_semaphores(count, levels)
+    ]
+    scratch += spread_semaphores(count, levels) + [dma((3,))]
+    results = [*shapes, (change.shape[0], change.shape[1] // 2)]
     return pl.pallas_call(
         partial(reduce_kernel, pieces),
-        out_shape=[jax.ShapeDtypeStruct(shape, low) for shape in shapes],
-        in_specs=[ANY] * 7,
-        out_specs=[ANY] * 5,
+        out_shape=[jax.ShapeDtypeStruct(shape, low) for shape in results],
+        in_specs=[ANY] * 8,
+        out_specs=[ANY] * 6,
         scratch_shapes=scratch,
         compiler_params=pltpu.CompilerParams(
             collective_id=number, has_side_effects=True, vmem_limit_bytes=60 * 2**20
         ),
         name="reduce_gradients",
-    )(*factors, small)
+    )(*factors, small, change)
 
 
 def rotary_rows():
@@ -653,8 +679,8 @@
 
             lax.fori_loop(0, width // (2 * HEAD_DIM), rotary, 0)
 
-    query = lax.broadcasted_iota(jnp.int32, (SLOT, SLOT), 0)
-    key = lax.broadcasted_iota(jnp.int32, (SLOT, SLOT), 1)
+    key = lax.broadcasted_iota(jnp.int32, (SLOT, SLOT), 0)
+    query = lax.broadcasted_iota(jnp.int32, (SLOT, SLOT), 1)
     allowed = (key <= query) & (key < length)
     pairs = width // (2 * HEAD_DIM)
     low = low_lanes(2 * HEAD_DIM)
@@ -665,12 +691,12 @@
         mixed = []
         for half in range(2):
             own = jnp.where(low == (half == 0), queries, jnp.zeros_like(queries))
-            scores = jnp.where(allowed, product(own, keys, 1, 1), masked_score)
-            raised = jnp.exp(scores - jnp.max(scores, axis=-1, keepdims=True))
-            share = raised * (1.0 / jnp.sum(raised, axis=-1, keepdims=True))
+            scores = jnp.where(allowed, product(keys, own, 1, 1), masked_score)
+            raised = jnp.exp(scores - jnp.max(scores, axis=0, keepdims=True))
+            share = raised * (1.0 / jnp.sum(raised, axis=0, keepdims=True))
             share = share.astype(jnp.bfloat16)
             attention[m, 2 * i + half] = share
-            mixed.append(product(share, values))
+            mixed.append(product(share, values, 0, 0))
         mixture[m, :, pair_lanes(i)] = jnp.where(low, mixed[0], mixed[1]).astype(jnp.bfloat16)
         return carry
 
@@ -733,14 +759,14 @@
         for half in range(2):
             share = attention[m, 2 * i + half]
             own = jnp.where(low == (half == 0), mixed_grad, jnp.zeros_like(mixed_grad))
-            value_grads.append(product(share, mixed_grad, 0, 0))
-            share_grad = product(own, values, 1, 1)
+            value_grads.append(product(share, mixed_grad))
+            share_grad = product(values, own, 1, 1)
             weight = share.astype(jnp.float32)
             weighted = weight * share_grad
-            score_grad = weighted - weight * jnp.sum(weighted, axis=-1, keepdims=True)
+            score_grad = weighted - weight * jnp.sum(weighted, axis=0, keepdims=True)
             score_grad = score_grad.astype(jnp.bfloat16)
-            query_grads.append(product(score_grad, keys))
-            key_grads.append(product(score_grad, queries, 0, 0))
+            query_grads.append(product(score_grad, keys, 0, 0))
+            key_grads.append(product(score_grad, queries))
         query_grad = jnp.where(low, query_grads[0], query_grads[1]) * HEAD_DIM**-0.5
         key_grad = jnp.where(low, key_grads[0], key_grads[1])
         value_grad = jnp.where(low, value_grads[0], value_grads[1])
@@ -749,7 +775,7 @@
         qkv[m, :, pair_lanes(i + 2 * pairs)] = value_grad.astype(jnp.bfloat16)
         return carry
 
-    lax.fori_loop(0, pairs, heads, 0, unroll=2)
+    lax.fori_loop(0, pairs, heads, 0, unroll=8)
 
     def project(i, carry):
         at = rows_at(i, JOINT_STEP)
@@ -895,6 +921,11 @@
     def kept(target, start, m):
         return pltpu.make_async_copy(
             result.at[m, :, pl.ds(start, half)], target.at[rows_at(m, SLOT), :], half_keep.at[m]
+        )
+
+    def stored(m):
+        return pltpu.make_async_copy(
+            result.at[m], input_grad.at[rows_at(m, SLOT), :], half_keep.at[m]
         )
 
     def giving(i, source, m):
@@ -954,6 +985,7 @@
 
         @pl.when(section == 0)
         def _():
+            pl.when(m > 0)(lambda: handing(x, m - 1).wait_send())
             handing(x, m).start()
 
         @pl.when(section == 1)
@@ -970,7 +1002,7 @@
     def backward(m, carry):
         @pl.when(section == 0)
         def _():
-            handing(x, m).wait_send()
+            pl.when(m == 0)(lambda: handing(x, MICRO - 1).wait_send())
             handing(upstream, m).wait_recv()
 
         @pl.when(section == 1)
@@ -990,11 +1022,7 @@
         def _():
             handing(upstream, m).start()
 
-        @pl.when(section == 0)
-        def _():
-            away(input_grad, half, m).start()
-            kept(input_grad, 0, m).start()
-
+        pl.when(section == 0)(lambda: stored(m).start())
         for i, source in enumerate((qkv, slope, upstream)):
             giving(3 + i, source, m).start()
         return carry
@@ -1006,15 +1034,13 @@
         @pl.when(section == 0)
         def _():
             halving(cotangent, upstream, 0, m).wait_send()
-            away(input_grad, half, m).wait_send()
-            kept(input_grad, 0, m).wait()
+            stored(m).wait()
             away(hidden_out, 0, m).wait_recv()
 
         @pl.when(section == 1)
         def _():
             halving(hidden_in, x, half, m).wait_send()
             handing(upstream, m).wait_send()
-            away(input_grad, half, m).wait_recv()
 
         for i, source in enumerate((normed, mixture, active, qkv, slope, upstream)):
             giving(i, source, m).wait()
@@ -1035,7 +1061,7 @@
     vmem = pltpu.VMEM
     dma = pltpu.SemaphoreType.DMA
     pieces = pieces_of([own.shape for own in owns])
-    outputs = [shape((tokens, half), low)] * 2
+    outputs = [shape((tokens, half), low), shape((tokens, width), low)]
     outputs += [shape((tokens, n), low) for n in (width, width, wide, 3 * width, wide, width)]
     outputs += [shape((devices * SMALL_ROWS, LANES), low)]
     scratch = [vmem((devices * own.shape[0], own.shape[1]), low) for own in owns]
@@ -1144,7 +1170,7 @@
     ]
     results = run_blocks(lengths, hidden_in, cotangent, owns, 1)
     shapes = [(own.shape[0] * devices, own.shape[1]) for own in owns[:4]]
-    *sums, small_sum = reduce_all(results[2:8], results[8], shapes, 2)
+    *sums, small_sum, own_grad = reduce_all(results[2:8], results[8], results[1], shapes, 2)
     width, wide = norm_gain.shape[1] * devices, inner_bias.shape[1] * devices
     (
         joint_sum,
@@ -1157,7 +1183,7 @@
         offset_sum,
         outer_sum,
         inner_sum,
-    ) = widen(small_sum, sums, results[:2], (width, width, width, wide), devices)
+    ) = widen(small_sum, sums, [results[0], own_grad], (width, width, width, wide), devices)
     return (
         hidden_out,
         input_grad,

time: 545 us -> 529 us (0.971)
  Pallas kernels: 541 us -> 524 us
    pallas_call x1, Pallas kernels: 249 us -> 233 us  [run_blocks(): pl.pallas_call(partial(blocks_kernel, pieces), out_shape=outputs, in_spec...]
where the time goes in v8:
time: 529 us; the launch traced here: 528 us
  Pallas kernels  524 us (99%)
    pallas_call x1, Pallas kernels, reduce_all(): pl.pallas_call(partial(reduce_kernel, pieces), out_shape=[jax.ShapeDtypeS...  265 us
    pallas_call x1, Pallas kernels, run_blocks(): pl.pallas_call(partial(blocks_kernel, pieces), out_shape=outputs, in_spec...  233 us
    pallas_call x1, Pallas kernels, widen(): pl.pallas_call(partial(widen_kernel, devices), out_shape=shapes, grid=(st...  26.4 us

profile of v8, /device:TPU:1, one launch (start us, length us, event | category | flops | bytes accessed | tf_op | source)
XLA Modules:
  0.0 528.5 jit_solution(11786234834812973414)
XLA Ops:
  0.7 0.7 convert_element_type.32
  1.4 0.7 convert_element_type.33
  2.0 0.7 convert_element_type.34
  2.7 1.4 convert_reduce_fusion
  4.0 232.9 %two_blocks.1 = (bf16[512,512]{1,0:T(8,128)(2,1)}, bf16[512,1024]{1,0:T(8,128)(2,1)}, bf16[512,1024]{1,0:T(8,128)(2,1)}, bf16[512,1024]{1,0:T(8,128)(2,1)}, bf16...) custom-call(s32[2]{0:T(128)} %refs_0_.1, ...), custom_call_target="tpu_custom_call" | custom-call | tf_op jit(solution)/shard_map/two_blocks/pallas_call | solution.py:1085
  236.9 264.9 %reduce_gradients.1 = (bf16[1024,3072]{1,0:T(8,128)(2,1)}, bf16[1024,1024]{1,0:T(8,128)(2,1)}, bf16[1024,4096]{1,0:T(8,128)(2,1)}, bf16[4096,1024]{1,0:T(8,128)(...) custom-call(bf16[512,1024]{1,0:T(8,128)(2,1)} %get-tuple-element.35.refs_0_, ...), custom_call_target="tpu_custom_call" | custom-call | tf_op jit(solution)/shard_map/reduce_gradients/pallas_call | solution.py:594
  501.8 26.4 %widen.1 = (f32[1,1024,3072]{2,1,0:T(8,128)}, f32[1,1024,1024]{2,1,0:T(8,128)}, f32[1,1024,4096]{2,1,0:T(8,128)}, f32[1,4096,1024]{2,1,0:T(8,128)}, bf16[512,512...) custom-call(bf16[256,128]{1,0:T(8,128)(2,1)} %get-tuple-element.43.r, ...), custom_call_target="tpu_custom_call" | custom-call | tf_op jit(solution)/shard_map/widen/pallas_call | solution.py:1139

commit v9 on v8

--- a/solution.py
+++ b/solution.py
@@ -282,7 +282,7 @@
 
 
 FACTORS = ((0, 3), (1, 5), (0, 4), (2, 5))
-MAKE_ORDER = (1, 3, 0, 2, 4)
+MAKE_ORDER = (3, 1, 2, 0, 4)
 COLUMN_STEP = 1024
 
 
@@ -501,7 +501,7 @@
         pltpu.make_async_copy(source, target, rest[0].at[i])
         for i, (source, target) in enumerate(zip(sources, [*factors, small]))
     ]
-    order = (1, 5, 2, 0, 3, 4, 6)
+    order = (2, 5, 1, 0, 4, 3, 6)
     for i in order:
         loads[i].start()
     greet(here, True)
@@ -523,7 +523,7 @@
         keep.start()
 
     reduce = Reduce(here, pieces, factors, small, made, buffers, rest[:8])
-    needs = {1: (1, 5), 3: (2,), 0: (0, 3), 2: (4,), 4: (6,)}
+    needs = {3: (2, 5), 1: (1,), 2: (0, 4), 0: (3,), 4: (6,)}
 
     def waits(i, array):
         @pl.when(i == 0)
@@ -677,7 +677,7 @@
                 qkv[m, :, at] = pair.astype(jnp.bfloat16) * jnp.bfloat16(scale)
                 return carry
 
-            lax.fori_loop(0, width // (2 * HEAD_DIM), rotary, 0)
+            lax.fori_loop(0, width // (2 * HEAD_DIM), rotary, 0, unroll=8)
 
     key = lax.broadcasted_iota(jnp.int32, (SLOT, SLOT), 0)
     query = lax.broadcasted_iota(jnp.int32, (SLOT, SLOT), 1)
@@ -1098,7 +1098,7 @@
 def pack_vectors(vectors):
     device = lax.axis_index("batch")
     size = SMALL_ROWS * LANES
-    total = jnp.zeros((1, size), jnp.float32)
+    total = jnp.zeros((1, size), jnp.bfloat16)
     row = 0
     for vector in vectors:
         width = vector.shape[1]
@@ -1106,10 +1106,10 @@
         slot = device * width % LANES // used
         for i in range(LANES // used):
             start = row * LANES + i * used
-            moved = jnp.pad(vector.astype(jnp.float32), ((0, 0), (start, size - start - width)))
-            total = total + jnp.where(slot == i, moved, 0.0)
+            moved = jnp.pad(vector, ((0, 0), (start, size - start - width)))
+            total = total + jnp.where(slot == i, moved, jnp.zeros_like(moved))
         row += max(1, width // LANES)
-    return total.reshape(SMALL_ROWS, LANES).astype(jnp.bfloat16)
+    return total.reshape(SMALL_ROWS, LANES)
 
 
 def widen_kernel(devices, *refs):

time: 529 us -> 519 us (0.981)
  Pallas kernels: 524 us -> 517 us
where the time goes in v9:
time: 519 us
  Pallas kernels  517 us (100%)
    pallas_call x1, Pallas kernels, reduce_all(): pl.pallas_call(partial(reduce_kernel, pieces), out_shape=[jax.ShapeDtypeS...  261 us
    pallas_call x1, Pallas kernels, run_blocks(): pl.pallas_call(partial(blocks_kernel, pieces), out_shape=outputs, in_spec...  229 us
    pallas_call x1, Pallas kernels, widen(): pl.pallas_call(partial(widen_kernel, devices), out_shape=shapes, grid=(st...  26.4 us

profile of v9, /device:TPU:1, one launch (start us, length us, event | category | flops | bytes accessed | tf_op | source)
XLA Modules:
  0.0 519.3 jit_solution(9422894370267462517)
XLA Ops:
  0.7 1.4 fusion.6
  2.1 229.2 %two_blocks.1 = (bf16[512,512]{1,0:T(8,128)(2,1)}, bf16[512,1024]{1,0:T(8,128)(2,1)}, bf16[512,1024]{1,0:T(8,128)(2,1)}, bf16[512,1024]{1,0:T(8,128)(2,1)}, bf16...) custom-call(s32[2]{0:T(128)} %refs_0_.1, ...), custom_call_target="tpu_custom_call" | custom-call | tf_op jit(solution)/shard_map/two_blocks/pallas_call | solution.py:1085
  231.4 261.3 %reduce_gradients.1 = (bf16[1024,3072]{1,0:T(8,128)(2,1)}, bf16[1024,1024]{1,0:T(8,128)(2,1)}, bf16[1024,4096]{1,0:T(8,128)(2,1)}, bf16[4096,1024]{1,0:T(8,128)(...) custom-call(bf16[512,1024]{1,0:T(8,128)(2,1)} %get-tuple-element.35.refs_0_, ...), custom_call_target="tpu_custom_call" | custom-call | tf_op jit(solution)/shard_map/reduce_gradients/pallas_call | solution.py:594
  492.7 26.4 %widen.1 = (f32[1,1024,3072]{2,1,0:T(8,128)}, f32[1,1024,1024]{2,1,0:T(8,128)}, f32[1,1024,4096]{2,1,0:T(8,128)}, f32[1,4096,1024]{2,1,0:T(8,128)}, bf16[512,512...) custom-call(bf16[256,128]{1,0:T(8,128)(2,1)} %get-tuple-element.43.r, ...), custom_call_target="tpu_custom_call" | custom-call | tf_op jit(solution)/shard_map/widen/pallas_call | solution.py:1139

commit v10 on v9

--- a/solution.py
+++ b/solution.py
@@ -126,12 +126,16 @@
 
     def along(self, p, z, y, source, way):
         here = self.here
+        if way == 0:
+            target = jnp.minimum(here.z + 1, here.last)
+        else:
+            target = jnp.maximum(here.z - 1, 0)
         return remote(
             source,
             self.block(p, z, y, here.c),
             self.zs.at[p, z, y, way],
             self.zr.at[p, z, y],
-            here.at(z=here.z + (1 if way == 0 else -1)),
+            here.at(z=target),
         )
 
     def across(self, p, z, source):
@@ -1121,7 +1125,7 @@
 
 
 def widen(small, sums, kept, widths, devices):
-    steps = 8
+    steps = 4
     arrays = [*sums, *kept]
     whole = lambda i: (0, 0)
     in_specs = [

time: 519 us -> 518 us (level)
  no operation moved by 1% of the time
where the time goes in v10:
time: 518 us
  Pallas kernels  515 us (99%)
    pallas_call x1, Pallas kernels, reduce_all(): pl.pallas_call(partial(reduce_kernel, pieces), out_shape=[jax.ShapeDtypeS...  261 us
    pallas_call x1, Pallas kernels, run_blocks(): pl.pallas_call(partial(blocks_kernel, pieces), out_shape=outputs, in_spec...  229 us
    pallas_call x1, Pallas kernels, widen(): pl.pallas_call(partial(widen_kernel, devices), out_shape=shapes, grid=(st...  24.8 us

profile of v10, /device:TPU:1, one launch (start us, length us, event | category | flops | bytes accessed | tf_op | source)
XLA Modules:
  0.0 517.6 jit_solution(2842938335920825808)
XLA Ops:
  0.7 1.4 fusion.6
  2.1 229.2 %two_blocks.1 = (bf16[512,512]{1,0:T(8,128)(2,1)}, bf16[512,1024]{1,0:T(8,128)(2,1)}, bf16[512,1024]{1,0:T(8,128)(2,1)}, bf16[512,1024]{1,0:T(8,128)(2,1)}, bf16...) custom-call(s32[2]{0:T(128)} %refs_0_.1, ...), custom_call_target="tpu_custom_call" | custom-call | tf_op jit(solution)/shard_map/two_blocks/pallas_call | solution.py:1089
  231.4 261.3 %reduce_gradients.1 = (bf16[1024,3072]{1,0:T(8,128)(2,1)}, bf16[1024,1024]{1,0:T(8,128)(2,1)}, bf16[1024,4096]{1,0:T(8,128)(2,1)}, bf16[4096,1024]{1,0:T(8,128)(...) custom-call(bf16[512,1024]{1,0:T(8,128)(2,1)} %get-tuple-element.35.refs_0_, ...), custom_call_target="tpu_custom_call" | custom-call | tf_op jit(solution)/shard_map/reduce_gradients/pallas_call | solution.py:598
  492.7 24.8 %widen.1 = (f32[1,1024,3072]{2,1,0:T(8,128)}, f32[1,1024,1024]{2,1,0:T(8,128)}, f32[1,1024,4096]{2,1,0:T(8,128)}, f32[1,4096,1024]{2,1,0:T(8,128)}, bf16[512,512...) custom-call(bf16[256,128]{1,0:T(8,128)(2,1)} %get-tuple-element.43.r, ...), custom_call_target="tpu_custom_call" | custom-call | tf_op jit(solution)/shard_map/widen/pallas_call | solution.py:1143

commit v11 on v10

--- a/solution.py
+++ b/solution.py
@@ -274,7 +274,7 @@
 
 def add_rows(target, other):
     rows = target.shape[0]
-    step = min(rows, 16)
+    step = min(rows, 64)
 
     def body(i, carry):
         at = pl.ds(pl.multiple_of(i * step, step), step)

time: 518 us -> 518 us (level)
  no operation moved by 1% of the time
where the time goes in v11:
time: 518 us
  Pallas kernels  515 us (99%)
    pallas_call x1, Pallas kernels, reduce_all(): pl.pallas_call(partial(reduce_kernel, pieces), out_shape=[jax.ShapeDtypeS...  261 us
    pallas_call x1, Pallas kernels, run_blocks(): pl.pallas_call(partial(blocks_kernel, pieces), out_shape=outputs, in_spec...  229 us
    pallas_call x1, Pallas kernels, widen(): pl.pallas_call(partial(widen_kernel, devices), out_shape=shapes, grid=(st...  24.8 us

profile of v11, /device:TPU:1, one launch (start us, length us, event | category | flops | bytes accessed | tf_op | source)
XLA Modules:
  0.0 517.5 jit_solution(14095597436865050666)
XLA Ops:
  0.7 1.4 fusion.6
  2.1 229.2 %two_blocks.1 = (bf16[512,512]{1,0:T(8,128)(2,1)}, bf16[512,1024]{1,0:T(8,128)(2,1)}, bf16[512,1024]{1,0:T(8,128)(2,1)}, bf16[512,1024]{1,0:T(8,128)(2,1)}, bf16...) custom-call(s32[2]{0:T(128)} %refs_0_.1, ...), custom_call_target="tpu_custom_call" | custom-call | tf_op jit(solution)/shard_map/two_blocks/pallas_call | solution.py:1089
  231.4 261.1 %reduce_gradients.1 = (bf16[1024,3072]{1,0:T(8,128)(2,1)}, bf16[1024,1024]{1,0:T(8,128)(2,1)}, bf16[1024,4096]{1,0:T(8,128)(2,1)}, bf16[4096,1024]{1,0:T(8,128)(...) custom-call(bf16[512,1024]{1,0:T(8,128)(2,1)} %get-tuple-element.35.refs_0_, ...), custom_call_target="tpu_custom_call" | custom-call | tf_op jit(solution)/shard_map/reduce_gradients/pallas_call | solution.py:598
  492.5 24.8 %widen.1 = (f32[1,1024,3072]{2,1,0:T(8,128)}, f32[1,1024,1024]{2,1,0:T(8,128)}, f32[1,1024,4096]{2,1,0:T(8,128)}, f32[1,4096,1024]{2,1,0:T(8,128)}, bf16[512,512...) custom-call(bf16[256,128]{1,0:T(8,128)(2,1)} %get-tuple-element.43.r, ...), custom_call_target="tpu_custom_call" | custom-call | tf_op jit(solution)/shard_map/widen/pallas_call | solution.py:1143
